TPU v7x, 32 devices: a whole 2x2x4 slice. The times are simulated.
32 devices in a mesh: ctx: 8 (over z, y), head: 4 (over x, core).
Axes of the slice: x: 2, y: 2, z: 4, core: 2. Of those that a mesh axis runs over, the one named last changes fastest.
Arguments:
- query_local: bfloat16 [1536, 5120], P(('ctx', 'head')), may hold values from -6 to 6
- key_local: bfloat16 [1536, 1024], P(('ctx', 'head')), may hold values from -6 to 6
- value_local: bfloat16 [1536, 1024], P(('ctx', 'head')), may hold values from -6 to 6
- stretch_labels: int32 [1536], replicated, may hold values from 0 to 3, never falling along the last dimension, each value on 1 to 768 neighbouring positions
- query_global: bfloat16 [1536, 5120], P(('ctx', 'head')), may hold values from -5 to 5
- key_global: bfloat16 [1536, 1024], P(('ctx', 'head')), may hold values from -5 to 5
- value_global: bfloat16 [1536, 1024], P(('ctx', 'head')), may hold values from -6 to 6
Outputs:
- local_heads: bfloat16 [1536, 5120], P(('ctx', 'head'))
- global_heads: bfloat16 [1536, 5120], P(('ctx', 'head'))
Inputs may be any that keep to these rules, and one draw needn't show every extreme that they name: `stretch_labels`: stretches are runs of consecutive tokens; numbers never fall; each stretch has 1 to 768 tokens and some stretch has exactly 768.
All inputs are finite; a program needn't handle non-finite values.
Results may differ from a plain program's by a relative error of at most 0.0059.
Values may be sent and summed in bfloat16 or wider, within the bound.
No kernel may reach another device: no remote copies, remote signals or barrier semaphores. Data moves between devices by JAX's collectives and lax.ppermute only.
A program may use at most 128 MiB of HBM per device.

v0:
```python
import jax
import jax.numpy as jnp
from jax import lax
from jax.sharding import PartitionSpec as P

HEAD = 128
STRETCH_SPAN = 4


rope_base = 500000.0
norm_epsilon = 1e-06
temper_floor = 8192
temper_slope = 0.1
masked_score = -1e30


def passed_along(shard, axis, by):
    size = lax.axis_size(axis)
    pairs = [(i, i + by) for i in range(size) if 0 <= i + by < size]
    return lax.ppermute(shard, axis, pairs)


def rotate(tensor, positions):
    head_width = tensor.shape[-1]
    half_width = head_width // 2
    frequency = rope_base ** (-(jnp.arange(half_width, dtype=jnp.float32) * 2.0 / head_width))
    angles = positions.astype(jnp.float32)[:, None] * frequency[None, :]
    extra_dims = tensor.ndim - 2
    angles = angles.reshape((angles.shape[0],) + (1,) * extra_dims + (half_width,))
    cosine = jnp.cos(angles)
    sine_part = jnp.sin(angles)
    first_part = tensor[..., :half_width]
    second_part = tensor[..., half_width:]
    return jnp.concatenate(
        [
            first_part * cosine - second_part * sine_part,
            first_part * sine_part + second_part * cosine,
        ],
        axis=-1,
    )


def normalize(tensor):
    return tensor * lax.rsqrt(jnp.mean(tensor * tensor, axis=-1, keepdims=True) + norm_epsilon)


def tempering(positions):
    return 1.0 + temper_slope * jnp.log(((positions + 1) // temper_floor + 1).astype(jnp.float32))


def local_update(
    running, queries, query_ids, query_pos, key_block, value_block, key_ids, key_pos, scaling
):
    allowed = (key_ids[None, :] == query_ids[:, None]) & (key_pos[None, :] <= query_pos[:, None])

    def update(carried):
        weighted, totals = carried
        scores = (
            jnp.einsum("qhgd,khd->hgqk", queries, key_block, preferred_element_type=jnp.float32)
            * scaling
        )
        weights = jnp.where(allowed[None, None], jnp.exp(scores), 0.0)
        totals = totals + jnp.sum(weights, axis=-1)
        weighted = weighted + jnp.einsum(
            "hgqk,khd->qhgd",
            weights.astype(jnp.bfloat16),
            value_block,
            preferred_element_type=jnp.float32,
        )
        return (weighted, totals)

    return lax.cond(jnp.any(allowed), update, lambda carried: carried, running)


def global_update(running, queries, query_pos, query_scale, key_block, value_block, key_pos):
    allowed = key_pos[None, :] <= query_pos[:, None]

    def update(carried):
        row_peak, totals, weighted = carried
        scores = (
            jnp.einsum("qhgd,khd->hgqk", queries, key_block, preferred_element_type=jnp.float32)
            * query_scale[None, None, :, None]
        )
        scores = jnp.where(allowed[None, None], scores, masked_score)
        new_peak = jnp.maximum(row_peak, jnp.max(scores, axis=-1))
        weights = jnp.where(allowed[None, None], jnp.exp(scores - new_peak[..., None]), 0.0)
        factor = jnp.exp(row_peak - new_peak)
        totals = totals * factor + jnp.sum(weights, axis=-1)
        weighted = weighted * jnp.transpose(factor, (2, 0, 1))[..., None] + jnp.einsum(
            "hgqk,khd->qhgd",
            weights.astype(jnp.bfloat16),
            value_block,
            preferred_element_type=jnp.float32,
        )
        return (new_peak, totals, weighted)

    return lax.cond(jnp.any(allowed), update, lambda carried: carried, running)


def shards(
    query_local, key_local, value_local, stretch_labels, query_global, key_global, value_global
):
    ctx_index = lax.axis_index("ctx")
    query_local, key_local, value_local, query_global, key_global, value_global = (
        lax.all_to_all(query_local, "head", split_axis=1, concat_axis=0, tiled=True),
        lax.all_to_all(key_local, "head", split_axis=1, concat_axis=0, tiled=True),
        lax.all_to_all(value_local, "head", split_axis=1, concat_axis=0, tiled=True),
        lax.all_to_all(query_global, "head", split_axis=1, concat_axis=0, tiled=True),
        lax.all_to_all(key_global, "head", split_axis=1, concat_axis=0, tiled=True),
        lax.all_to_all(value_global, "head", split_axis=1, concat_axis=0, tiled=True),
    )
    tokens = query_local.shape[0]
    half_rows = tokens // 2
    key_heads = key_local.shape[1] // HEAD
    group_size = query_local.shape[1] // (key_heads * HEAD)
    scaling = HEAD ** (-0.5)
    query_shape = (tokens, key_heads, group_size, HEAD)
    key_shape = (tokens, key_heads, HEAD)
    offsets = jnp.arange(tokens, dtype=jnp.int32)
    positions = ctx_index * tokens + offsets
    queries = normalize(
        rotate(query_local.astype(jnp.float32).reshape(query_shape), positions)
    ).astype(jnp.bfloat16)
    keys_normed = normalize(
        rotate(key_local.astype(jnp.float32).reshape(key_shape), positions)
    ).astype(jnp.bfloat16)
    values_local = value_local.reshape(key_shape)
    query_ids = lax.dynamic_slice_in_dim(stretch_labels, ctx_index * tokens, tokens, 0)
    local_state = (
        jnp.zeros(query_shape, jnp.float32),
        jnp.zeros((key_heads, group_size, tokens), jnp.float32),
    )
    local_state = local_update(
        local_state,
        queries,
        query_ids,
        positions,
        keys_normed,
        values_local,
        query_ids,
        positions,
        scaling,
    )
    source = (keys_normed, values_local)
    for distance in range(1, STRETCH_SPAN + 1):
        source = passed_along((keys_normed, values_local), "ctx", distance)
        first_row = (ctx_index - distance) * tokens
        key_ids = lax.dynamic_slice_in_dim(stretch_labels, jnp.maximum(first_row, 0), tokens, 0)
        key_ids = jnp.where(first_row >= 0, key_ids, -1)
        local_state = local_update(
            local_state,
            queries,
            query_ids,
            positions,
            source[0],
            source[1],
            key_ids,
            first_row + offsets,
            scaling,
        )
    weighted, totals = local_state
    local_heads = (
        (weighted / jnp.transpose(totals, (2, 0, 1))[..., None])
        .astype(jnp.bfloat16)
        .reshape(tokens, -1)
    )
    query_halves = (query_global[:half_rows], query_global[half_rows:])
    query_pos = jnp.concatenate(
        [positions[:half_rows], ctx_index * tokens + offsets[half_rows:]], axis=0
    )
    query_parts = []
    for branch in range(2):
        part_pos = query_pos[branch * half_rows : (branch + 1) * half_rows]
        query_parts.append(
            (
                query_halves[branch].reshape(half_rows, key_heads, group_size, HEAD),
                part_pos,
                tempering(part_pos) * scaling,
            )
        )
    initial = (
        jnp.full((key_heads, group_size, half_rows), masked_score, jnp.float32),
        jnp.zeros((key_heads, group_size, half_rows), jnp.float32),
        jnp.zeros((half_rows, key_heads, group_size, HEAD), jnp.float32),
    )

    def absorb(carried, key_block, value_block, block_pos):
        return tuple(
            (
                global_update(
                    carried[member],
                    query_parts[member][0],
                    query_parts[member][1],
                    query_parts[member][2],
                    key_block,
                    value_block,
                    block_pos,
                )
                for member in range(2)
            )
        )

    key_piece = lax.all_gather(key_global, "ctx", axis=0, tiled=True)
    value_piece = lax.all_gather(value_global, "ctx", axis=0, tiled=True)
    piece_rows = key_piece.shape[0]
    key_piece = key_piece.reshape(piece_rows, key_heads, HEAD)
    value_piece = value_piece.reshape(piece_rows, key_heads, HEAD)
    key_pos = jnp.arange(piece_rows, dtype=jnp.int32)

    def advance(number, running):
        anchor = number * half_rows
        return absorb(
            running,
            lax.dynamic_slice_in_dim(key_piece, anchor, half_rows, 0),
            lax.dynamic_slice_in_dim(value_piece, anchor, half_rows, 0),
            lax.dynamic_slice_in_dim(key_pos, anchor, half_rows, 0),
        )

    states = lax.fori_loop(0, piece_rows // half_rows, advance, (initial, initial))
    output_halves = []
    for branch in range(2):
        row_peak, totals, weighted = states[branch]
        output_halves.append(
            (weighted / jnp.transpose(totals, (2, 0, 1))[..., None])
            .astype(jnp.bfloat16)
            .reshape(half_rows, -1)
        )
    global_heads = jnp.concatenate(output_halves, axis=0)
    return (
        lax.all_to_all(local_heads, "head", split_axis=0, concat_axis=1, tiled=True),
        lax.all_to_all(global_heads, "head", split_axis=0, concat_axis=1, tiled=True),
    )


def solution(mesh):
    return jax.shard_map(
        shards,
        mesh=mesh,
        in_specs=(
            P(("ctx", "head"), None),
            P(("ctx", "head"), None),
            P(("ctx", "head"), None),
            P(),
            P(("ctx", "head"), None),
            P(("ctx", "head"), None),
            P(("ctx", "head"), None),
        ),
        out_specs=(P(("ctx", "head"), None), P(("ctx", "head"), None)),
        check_vma=False,
    )
```

profile of v0, /device:TPU:28, one launch (start us, length us, event | category | flops | bytes accessed | tf_op | source)
XLA Modules:
  0.0 248.1 jit_solution(1621009465908867308)
XLA Ops:
  0.7 1.6 copy.329
  2.3 3.3 %all-to-all-start = ((bf16[48,4,256]{2,0,1:T(8,128)(2,1)}), bf16[48,4,256]{2,0,1:T(8,128)(2,1)S(1)}, u32[]{:S(2)}, u32[]{:S(2)}) async-start(bf16[48,4,256]{2,0,1:T(8,128)(2,1)} %bitcast.158), calls=%async_computation | async-start | bytes 196608 | tf_op jit(solution)/shard_map/all_to_all | solution.py:106
  6.2 1.0 dynamic-slice_select_fusion
  7.2 1.7 compare_and_fusion
  12.1 1.8 copy.325
  16.7 3.3 %all-to-all-start.2 = ((bf16[48,4,256]{2,0,1:T(8,128)(2,1)}), bf16[48,4,256]{2,0,1:T(8,128)(2,1)S(1)}, u32[]{:S(2)}, u32[]{:S(2)}) async-start(bf16[48,4,256]{2,0,1:T(8,128)(2,1)} %bitcast.157), calls=%async_computation.2 | async-start | bytes 196608 | tf_op jit(solution)/shard_map/all_to_all | solution.py:107
  21.1 3.2 %all-to-all-done.2 = bf16[48,4,256]{2,0,1:T(8,128)(2,1)S(1)} async-done(((bf16[48,4,256]{2,0,1:T(8,128)(2,1)}), bf16[48,4,256]{2,0,1:T(8,128)(2,1)S(1)}, u32[]{:S(2)}, u32[]{:S(2)}) %all-to-all-start.2) | async-done | bytes 98336 | tf_op jit(solution)/shard_map/all_to_all | solution.py:107
  24.3 3.3 %all-to-all-start.4 = ((bf16[48,4,256]{2,0,1:T(8,128)(2,1)}), bf16[48,4,256]{2,0,1:T(8,128)(2,1)S(1)}, u32[]{:S(2)}, u32[]{:S(2)}) async-start(bf16[48,4,256]{2,0,1:T(8,128)(2,1)} %bitcast.156), calls=%async_computation.4 | async-start | bytes 196608 | tf_op jit(solution)/shard_map/all_to_all | solution.py:109
  27.6 4.2 %all-to-all-done.4 = bf16[48,4,256]{2,0,1:T(8,128)(2,1)S(1)} async-done(((bf16[48,4,256]{2,0,1:T(8,128)(2,1)}), bf16[48,4,256]{2,0,1:T(8,128)(2,1)S(1)}, u32[]{:S(2)}, u32[]{:S(2)}) %all-to-all-start.4) | async-done | bytes 98336 | tf_op jit(solution)/shard_map/all_to_all | solution.py:109
  31.8 3.3 %all-to-all-start.5 = ((bf16[48,4,256]{2,0,1:T(8,128)(2,1)}), bf16[48,4,256]{2,0,1:T(8,128)(2,1)S(1)}, u32[]{:S(2)}, u32[]{:S(2)}) async-start(bf16[48,4,256]{2,0,1:T(8,128)(2,1)} %bitcast.155), calls=%async_computation.5 | async-start | bytes 196608 | tf_op jit(solution)/shard_map/all_to_all | solution.py:110
  35.1 1.1 multiply_convert_fusion.1
  36.3 1.3 collective-permute-start
  37.5 1.3 collective-permute-start.2
  39.5 1.3 collective-permute-start.1
  40.8 1.3 collective-permute-start.3
  42.1 1.3 collective-permute-start.4
  43.4 3.5 %all-to-all-start.1 = ((bf16[48,4,1280]{2,0,1:T(8,128)(2,1)}), bf16[48,4,1280]{2,0,1:T(8,128)(2,1)S(1)}, u32[]{:S(2)}, u32[]{:S(2)}) async-start(bf16[48,4,1280]{2,0,1:T(8,128)(2,1)} %bitcast.154), calls=%async_computation.1 | async-start | bytes 983040 | tf_op jit(solution)/shard_map/all_to_all | solution.py:105
  46.9 38.8 %all_gather.6 = bf16[1536,256]{1,0:T(8,128)(2,1)S(1)} all-gather(bf16[192,256]{1,0:T(8,128)(2,1)S(1)} %bitcast.172), channel_id=1, replica_groups=mesh['ctx'=8,'head'=4] {'ctx'}, dimensions={0}, use_global_device_ids=true | all-gather | bytes 884736 | tf_op jit(solution)/shard_map/all_gather | solution.py:203
  86.0 1.2 copy.210
  87.2 32.1 %all_gather.7 = bf16[1536,256]{1,0:T(8,128)(2,1)S(1)} all-gather(bf16[192,256]{1,0:T(8,128)(2,1)S(1)} %bitcast.174), channel_id=1, replica_groups=mesh['ctx'=8,'head'=4] {'ctx'}, dimensions={0}, use_global_device_ids=true | all-gather | bytes 884736 | tf_op jit(solution)/shard_map/all_gather | solution.py:204
  119.5 1.2 copy.211
  120.7 4.2 %all-to-all-start.6 = ((bf16[48,4,1280]{2,0,1:T(8,128)(2,1)}), bf16[48,4,1280]{2,0,1:T(8,128)(2,1)}, u32[]{:S(2)}, u32[]{:S(2)}) async-start(bf16[48,4,1280]{2,0,1:T(8,128)(2,1)} %bitcast.153), calls=%async_computation.6 | async-start | bytes 983040 | tf_op jit(solution)/shard_map/all_to_all | solution.py:108
  125.7 1.2 copy-done
  126.9 1.1 multiply_reduce_fusion
  128.3 1.3 collective-permute-start.5
  129.7 1.3 collective-permute-start.6
  131.0 1.3 collective-permute-start.7
  132.3 2.3 multiply_convert_fusion
  134.6 3.1 %conditional.7 = (f32[192,2,5,128]{3,0,2,1:T(8,128)S(1)}, f32[2,5,192]{2,1,0:T(8,128)S(1)}) conditional(s32[]{:T(128)} %convert_element_type.103, () %tuple.68, (pred[192,192]{0,1:T(8,128)(4,1)S(1)}, bf16[192,2,128]{2,1,0:T(2,128)(2,1)}, bf16[192,2,5,128]{3,2,1,0:T(8,128)(2,1)S(1)}, bf16[192,2,128]{2,1,0:T(2,128)(2,1)}) %tuple.193), branch_computations={%region_7.8_spmd, %region_8.10_spmd} | conditional | flops 190953600 | bytes 4701712 | solution.py:72
  134.6 1.6 fusion
  136.2 1.5 convolution_bitcast_fusion
  137.7 3.4 %conditional.8 = ((f32[192,2,5,128]{3,0,2,1:T(8,128)S(1)}, f32[2,5,192]{2,1,0:T(8,128)S(1)})) conditional(s32[]{:T(128)} %convert_element_type.102, (f32[192,2,5,128]{3,0,2,1:T(8,128)S(1)}, f32[2,5,192]{2,1,0:T(8,128)S(1)}) %conditional.7, (pred[192,192]{0,1:T(8,128)(4,1)S(1)}, bf16[192,2,128]{2,1,0:T(2,128)(2,1)}, ...), branch_computations={%region_10.11_spmd, %region_11.13_spmd} | conditional | flops 191201280 | bytes 5707800 | solution.py:72
  137.7 1.6 fusion.12
  139.3 1.8 fusion.14
  141.3 3.5 %collective-permute-done.6 = bf16[192,2,128]{2,1,0:T(2,128)(2,1)S(1)} collective-permute-done((bf16[192,2,128]{2,1,0:T(2,128)(2,1)}, bf16[192,2,128]{2,1,0:T(2,128)(2,1)S(1)}, u32[]{:S(2)}, u32[]{:S(2)}) %collective-permute-start.6) | collective-permute-done | bytes 98336 | tf_op jit(solution)/shard_map/ppermute | solution.py:20
  144.8 2.1 collective-permute-done.7
  147.6 1.3 all_to_all.107
  148.9 3.5 %all-to-all-start.3 = ((bf16[4,48,1280]{2,1,0:T(8,128)(2,1)}), bf16[4,48,1280]{2,1,0:T(8,128)(2,1)S(1)}, u32[]{:S(2)}, u32[]{:S(2)}) async-start(bf16[4,48,1280]{2,1,0:T(8,128)(2,1)} %all_to_all.107), calls=%async_computation.3 | async-start | bytes 983040 | tf_op jit(solution)/shard_map/all_to_all | solution.py:230
  152.4 1.1 fusion.100
  154.4 78.8 %while.23 = (s32[]{:T(128)}, f32[2,5,96]{2,1,0:T(8,128)S(1)}, f32[2,5,96]{2,1,0:T(8,128)S(1)}, f32[96,2,5,128]{3,0,2,1:T(8,128)S(1)}, f32[2,5,96]{2,1,0:T(8,128)...) while((s32[]{:T(128)}, f32[2,5,96]{2,1,0:T(8,128)S(1)}, ...), condition=%wide.region_33.34_spmd, body=%wide.region_22.33_spmd.sunk | while | flops 96564864 | bytes 5262447 | solution.py:219
  156.8 0.9 conditional.14
  158.4 0.9 conditional.15
  161.8 0.9 conditional.14
  163.4 0.9 conditional.15
  166.8 0.9 conditional.14
  168.4 0.9 conditional.15
  173.4 0.9 conditional.15
  176.8 0.9 conditional.14
  178.4 0.9 conditional.15
  183.4 0.9 conditional.15
  186.8 0.9 conditional.14
  188.4 0.9 conditional.15
  193.3 0.9 conditional.15
  198.3 0.9 conditional.15
  203.3 0.9 conditional.15
  208.3 0.9 conditional.15
  213.3 0.9 conditional.15
  218.3 0.9 conditional.15
  223.3 0.9 conditional.15
  228.2 0.9 conditional.15
  232.3 0.9 conditional.15
  234.4 1.0 copy.216
  235.4 3.5 %all-to-all-start.7 = ((bf16[4,48,1280]{2,1,0:T(8,128)(2,1)}), bf16[4,48,1280]{2,1,0:T(8,128)(2,1)S(1)}, u32[]{:S(2)}, u32[]{:S(2)}) async-start(bf16[4,48,1280]{2,1,0:T(8,128)(2,1)} %bitcast.50), calls=%async_computation.7 | async-start | bytes 983040 | tf_op jit(solution)/shard_map/all_to_all | solution.py:231
  239.7 7.6 %all-to-all-done.7 = bf16[4,48,1280]{2,1,0:T(8,128)(2,1)S(1)} async-done(((bf16[4,48,1280]{2,1,0:T(8,128)(2,1)}), bf16[4,48,1280]{2,1,0:T(8,128)(2,1)S(1)}, u32[]{:S(2)}, u32[]{:S(2)}) %all-to-all-start.7) | async-done | bytes 491552 | tf_op jit(solution)/shard_map/all_to_all | solution.py:231
  (321 shorter events, 75.6 us)
Async XLA Ops:
  0.6 13.3 %copy-start.3 = (bf16[48,1024]{1,0:T(8,128)(2,1)S(1)}, bf16[48,1024]{1,0:T(8,128)(2,1)}, u32[]{:S(2)}) copy-start(bf16[48,1024]{1,0:T(8,128)(2,1)} %param.25) | copy-start | bytes 294916
  0.6 13.9 %copy-start.4 = (bf16[48,1024]{1,0:T(8,128)(2,1)S(1)}, bf16[48,1024]{1,0:T(8,128)(2,1)}, u32[]{:S(2)}) copy-start(bf16[48,1024]{1,0:T(8,128)(2,1)} %param.28) | copy-start | bytes 294916
  0.7 14.6 %copy-start.5 = (bf16[48,1024]{1,0:T(8,128)(2,1)S(1)}, bf16[48,1024]{1,0:T(8,128)(2,1)}, u32[]{:S(2)}) copy-start(bf16[48,1024]{1,0:T(8,128)(2,1)} %param.29) | copy-start | bytes 294916
  0.7 15.2 %copy-start.1 = (bf16[48,5120]{1,0:T(8,128)(2,1)S(1)}, bf16[48,5120]{1,0:T(8,128)(2,1)}, u32[]{:S(2)}) copy-start(bf16[48,5120]{1,0:T(8,128)(2,1)} %param.27) | copy-start | bytes 1474564
  2.3 14.4 %all-to-all-start = ((bf16[48,4,256]{2,0,1:T(8,128)(2,1)}), bf16[48,4,256]{2,0,1:T(8,128)(2,1)S(1)}, u32[]{:S(2)}, u32[]{:S(2)}) async-start(bf16[48,4,256]{2,0,1:T(8,128)(2,1)} %bitcast.158), calls=%async_computation | async-start | bytes 196608 | tf_op jit(solution)/shard_map/all_to_all | solution.py:106
  5.6 14.5 %copy-start.6 = (s32[192]{0:T(256)}, s32[192]{0:T(256)S(1)}, u32[]{:S(2)}) copy-start(s32[192]{0:T(256)S(1)} %iota_add_fusion.3) | copy-start | bytes 2308
  16.7 7.6 %all-to-all-start.2 = ((bf16[48,4,256]{2,0,1:T(8,128)(2,1)}), bf16[48,4,256]{2,0,1:T(8,128)(2,1)S(1)}, u32[]{:S(2)}, u32[]{:S(2)}) async-start(bf16[48,4,256]{2,0,1:T(8,128)(2,1)} %bitcast.157), calls=%async_computation.2 | async-start | bytes 196608 | tf_op jit(solution)/shard_map/all_to_all | solution.py:107
  24.3 7.6 %all-to-all-start.4 = ((bf16[48,4,256]{2,0,1:T(8,128)(2,1)}), bf16[48,4,256]{2,0,1:T(8,128)(2,1)S(1)}, u32[]{:S(2)}, u32[]{:S(2)}) async-start(bf16[48,4,256]{2,0,1:T(8,128)(2,1)} %bitcast.156), calls=%async_computation.4 | async-start | bytes 196608 | tf_op jit(solution)/shard_map/all_to_all | solution.py:109
  31.8 11.6 %all-to-all-start.5 = ((bf16[48,4,256]{2,0,1:T(8,128)(2,1)}), bf16[48,4,256]{2,0,1:T(8,128)(2,1)S(1)}, u32[]{:S(2)}, u32[]{:S(2)}) async-start(bf16[48,4,256]{2,0,1:T(8,128)(2,1)} %bitcast.155), calls=%async_computation.5 | async-start | bytes 196608 | tf_op jit(solution)/shard_map/all_to_all | solution.py:110
  36.3 92.1 %collective-permute-start = (bf16[192,2,128]{2,1,0:T(2,128)(2,1)}, bf16[192,2,128]{2,1,0:T(2,128)(2,1)}, u32[]{:S(2)}, u32[]{:S(2)}) collective-permute-start(bf16[192,2,128]{2,1,0:T(2,128)(2,1)} %multiply_convert_fusion.1), channel_id=1, source_target_pairs={{0,4},{4,8},{8,12},{12,16},{16,20},{20,24},{24,28},{1,5},{5,9},{9,... | collective-permute-start | bytes 294920 | tf_op jit(solution)/shard_map/ppermute | solution.py:20
  37.5 93.4 %collective-permute-start.2 = (bf16[192,2,128]{2,1,0:T(2,128)(2,1)}, bf16[192,2,128]{2,1,0:T(2,128)(2,1)}, u32[]{:S(2)}, u32[]{:S(2)}) collective-permute-start(bf16[192,2,128]{2,1,0:T(2,128)(2,1)} %multiply_convert_fusion.1), channel_id=1, source_target_pairs={{0,8},{4,12},{8,16},{12,20},{16,24},{20,28},{1,9},{5,13},{9,17},{1... | collective-permute-start | bytes 294920 | tf_op jit(solution)/shard_map/ppermute | solution.py:20
  39.5 90.1 %collective-permute-start.1 = (bf16[192,2,128]{2,1,0:T(2,128)(2,1)}, bf16[192,2,128]{2,1,0:T(2,128)(2,1)}, u32[]{:S(2)}, u32[]{:S(2)}) collective-permute-start(bf16[192,2,128]{2,1,0:T(2,128)(2,1)} %reshape.238), channel_id=1, source_target_pairs={{0,4},{4,8},{8,12},{12,16},{16,20},{20,24},{24,28},{1,5},{5,9},{9,... | collective-permute-start | bytes 294920 | tf_op jit(solution)/shard_map/ppermute | solution.py:20
  40.8 100.3 %collective-permute-start.3 = (bf16[192,2,128]{2,1,0:T(2,128)(2,1)}, bf16[192,2,128]{2,1,0:T(2,128)(2,1)}, u32[]{:S(2)}, u32[]{:S(2)}) collective-permute-start(bf16[192,2,128]{2,1,0:T(2,128)(2,1)} %reshape.238), channel_id=1, source_target_pairs={{0,8},{4,12},{8,16},{12,20},{16,24},{20,28},{1,9},{5,13},{9,17},{1... | collective-permute-start | bytes 294920 | tf_op jit(solution)/shard_map/ppermute | solution.py:20
  42.1 99.2 %collective-permute-start.4 = (bf16[192,2,128]{2,1,0:T(2,128)(2,1)}, bf16[192,2,128]{2,1,0:T(2,128)(2,1)}, u32[]{:S(2)}, u32[]{:S(2)}) collective-permute-start(bf16[192,2,128]{2,1,0:T(2,128)(2,1)} %multiply_convert_fusion.1), channel_id=1, source_target_pairs={{0,12},{4,16},{8,20},{12,24},{16,28},{1,13},{5,17},{9,21},{13,25},... | collective-permute-start | bytes 294920 | tf_op jit(solution)/shard_map/ppermute | solution.py:20
  43.4 77.3 %all-to-all-start.1 = ((bf16[48,4,1280]{2,0,1:T(8,128)(2,1)}), bf16[48,4,1280]{2,0,1:T(8,128)(2,1)S(1)}, u32[]{:S(2)}, u32[]{:S(2)}) async-start(bf16[48,4,1280]{2,0,1:T(8,128)(2,1)} %bitcast.154), calls=%async_computation.1 | async-start | bytes 983040 | tf_op jit(solution)/shard_map/all_to_all | solution.py:105
  120.7 28.2 %all-to-all-start.6 = ((bf16[48,4,1280]{2,0,1:T(8,128)(2,1)}), bf16[48,4,1280]{2,0,1:T(8,128)(2,1)}, u32[]{:S(2)}, u32[]{:S(2)}) async-start(bf16[48,4,1280]{2,0,1:T(8,128)(2,1)} %bitcast.153), calls=%async_computation.6 | async-start | bytes 983040 | tf_op jit(solution)/shard_map/all_to_all | solution.py:108
  125.7 1.2 copy-start
  128.3 6.2 %copy-start.2 = (pred[192,192]{0,1:T(8,128)(4,1)S(1)}, pred[192,192]{0,1:T(8,128)(4,1)}, u32[]{:S(2)}) copy-start(pred[192,192]{0,1:T(8,128)(4,1)} %get-tuple-element.763) | copy-start | bytes 110596
  128.3 13.0 %collective-permute-start.5 = (bf16[192,2,128]{2,1,0:T(2,128)(2,1)}, bf16[192,2,128]{2,1,0:T(2,128)(2,1)S(1)}, u32[]{:S(2)}, u32[]{:S(2)}) collective-permute-start(bf16[192,2,128]{2,1,0:T(2,128)(2,1)} %reshape.238), channel_id=1, source_target_pairs={{0,12},{4,16},{8,20},{12,24},{16,28},{1,13},{5,17},{9,21},{13,25},... | collective-permute-start | bytes 294920 | tf_op jit(solution)/shard_map/ppermute | solution.py:20
  129.7 15.2 %collective-permute-start.6 = (bf16[192,2,128]{2,1,0:T(2,128)(2,1)}, bf16[192,2,128]{2,1,0:T(2,128)(2,1)S(1)}, u32[]{:S(2)}, u32[]{:S(2)}) collective-permute-start(bf16[192,2,128]{2,1,0:T(2,128)(2,1)} %multiply_convert_fusion.1), channel_id=1, source_target_pairs={{0,16},{4,20},{8,24},{12,28},{1,17},{5,21},{9,25},{13,29},{2,18},{... | collective-permute-start | bytes 294920 | tf_op jit(solution)/shard_map/ppermute | solution.py:20
  131.0 15.9 %collective-permute-start.7 = (bf16[192,2,128]{2,1,0:T(2,128)(2,1)}, bf16[192,2,128]{2,1,0:T(2,128)(2,1)S(1)}, u32[]{:S(2)}, u32[]{:S(2)}) collective-permute-start(bf16[192,2,128]{2,1,0:T(2,128)(2,1)} %reshape.238), channel_id=1, source_target_pairs={{0,16},{4,20},{8,24},{12,28},{1,17},{5,21},{9,25},{13,29},{2,18},{... | collective-permute-start | bytes 294920 | tf_op jit(solution)/shard_map/ppermute | solution.py:20
  148.9 86.5 %all-to-all-start.3 = ((bf16[4,48,1280]{2,1,0:T(8,128)(2,1)}), bf16[4,48,1280]{2,1,0:T(8,128)(2,1)S(1)}, u32[]{:S(2)}, u32[]{:S(2)}) async-start(bf16[4,48,1280]{2,1,0:T(8,128)(2,1)} %all_to_all.107), calls=%async_computation.3 | async-start | bytes 983040 | tf_op jit(solution)/shard_map/all_to_all | solution.py:230
  153.5 0.9 slice-start
  235.4 11.9 %all-to-all-start.7 = ((bf16[4,48,1280]{2,1,0:T(8,128)(2,1)}), bf16[4,48,1280]{2,1,0:T(8,128)(2,1)S(1)}, u32[]{:S(2)}, u32[]{:S(2)}) async-start(bf16[4,48,1280]{2,1,0:T(8,128)(2,1)} %bitcast.50), calls=%async_computation.7 | async-start | bytes 983040 | tf_op jit(solution)/shard_map/all_to_all | solution.py:231
where the time goes:
time: 251 us; the launch traced here: 248 us
  blocking collectives  70.9 us (28%)
  starting transfers between devices  38.1 us (15%)
  local copies, waits for them, and re-layouts  33.1 us (13%)
  matrix products  29.6 us (12%)
  other arithmetic  27.3 us (11%)
  loops' own time  24 us (10%)
  waiting for transfers between devices  20.6 us (8%)
  between operations  4.43 us (2%)
    all_gather x1, blocking collectives, shards(): key_piece = lax.all_gather(key_global, 'ctx', axis=0, tiled=True)  38.8 us
    all_gather x1, blocking collectives, shards(): value_piece = lax.all_gather(value_global, 'ctx', axis=0, tiled=True)  32.1 us
    another operation x1, loops' own time, shards(): lax.fori_loop(0, piece_rows // half_rows, advance, (initial, initial))  22.2 us
    dot_general x33, matrix products, update(): jnp.einsum('hgqk,khd->qhgd', weights.astype(jnp.bfloat16), value_block, p...  17 us
    dynamic_slice x16, local copies, waits for them, and re-layouts, advance(): lax.dynamic_slice_in_dim(value_piece, anchor, half_rows, 0)  13.5 us
    reduce_or x16, other arithmetic, global_update(): return lax.cond(jnp.any(allowed), update, lambda carried: carried, running)  12.8 us
    dot_general x33, matrix products, update(): jnp.einsum('qhgd,khd->hgqk', queries, key_block, preferred_element_type=j...  12.6 us
    ppermute x8, starting transfers between devices, passed_along(): return lax.ppermute(shard, axis, pairs)  10.3 us
  transfers between devices with their start and end apart: 16, of which 5 were waited for; matrix products, arithmetic and copies ran while one was open for 34% of the time, Pallas kernels for 0%

commit v1 on v0

v1 whole, which is shorter than its diff:
```python
import functools
import math

import jax
import jax.numpy as jnp
from jax import lax
from jax.experimental import pallas as pl
from jax.experimental.pallas import tpu as pltpu
from jax.sharding import Mesh
from jax.sharding import PartitionSpec as P

HEAD = 128
STRETCH = 768

rope_base = 500000.0
norm_epsilon = 1e-06
temper_floor = 8192
temper_slope = 0.1
masked_score = -1e30
log2e = 1.4426950408889634

IN_PLANE = ("row", "head")


def rope_tables(positions):
    half = HEAD // 2
    lane = lax.broadcasted_iota(jnp.int32, (1, HEAD), 1)
    index = jnp.where(lane < half, lane, lane - half).astype(jnp.float32)
    frequency = rope_base ** (-(index * 2.0 / HEAD))
    angles = positions.astype(jnp.float32)[:, None] * frequency
    sine = jnp.sin(angles)
    return jnp.cos(angles), jnp.where(lane < half, -sine, sine)


def rotated_unit(x, cosine, sine):
    y = x * cosine + pltpu.roll(x, HEAD // 2, 1) * sine
    return y * lax.rsqrt(jnp.mean(y * y, axis=-1, keepdims=True) + norm_epsilon)


def vmem_call(body, out_shapes, n_in, flops=0, nbytes=0, exps=0, scratch=(), smem=0):
    return pl.pallas_call(
        body,
        out_shape=out_shapes,
        in_specs=[pl.BlockSpec(memory_space=pltpu.SMEM)] * smem
        + [pl.BlockSpec(memory_space=pltpu.VMEM)] * n_in,
        out_specs=jax.tree.map(lambda _: pl.BlockSpec(memory_space=pltpu.VMEM), out_shapes),
        scratch_shapes=list(scratch),
        cost_estimate=pl.CostEstimate(flops=flops, bytes_accessed=nbytes, transcendentals=exps),
    )


def pack_pair_body(k_ref, v_ref, o_ref):
    for d in range(o_ref.shape[0]):
        o_ref[d, 0] = k_ref[:, d * HEAD : (d + 1) * HEAD]
        o_ref[d, 1] = v_ref[:, d * HEAD : (d + 1) * HEAD]


def pack_pair(key, value):
    tokens, width = key.shape
    shape = jax.ShapeDtypeStruct((width // HEAD, 2, tokens, HEAD), key.dtype)
    return vmem_call(pack_pair_body, shape, 2, nbytes=4 * key.size * 2)(key, value)


def pack_query_body(q_ref, cos_ref, sin_ref, o_ref):
    members = o_ref.shape[2] // HEAD
    cosine, sine = cos_ref[...], sin_ref[...]
    for d in range(o_ref.shape[0]):
        for g in range(members):
            at = (d * members + g) * HEAD
            x = q_ref[:, at : at + HEAD].astype(jnp.float32)
            o_ref[d, :, g * HEAD : (g + 1) * HEAD] = rotated_unit(x, cosine, sine).astype(o_ref.dtype)


def pack_plain_body(q_ref, o_ref):
    width = o_ref.shape[2]
    for d in range(o_ref.shape[0]):
        o_ref[d] = q_ref[:, d * width : (d + 1) * width]


def unpack_body(x_ref, o_ref):
    width = x_ref.shape[2]
    for d in range(x_ref.shape[0]):
        o_ref[:, d * width : (d + 1) * width] = x_ref[d]


def unpack(x):
    parts, tokens, width = x.shape
    shape = jax.ShapeDtypeStruct((tokens, parts * width), x.dtype)
    return vmem_call(unpack_body, shape, 1, nbytes=4 * x.size)(x)


def causal(rows):
    r = lax.broadcasted_iota(jnp.int32, (rows, rows), 0)
    c = lax.broadcasted_iota(jnp.int32, (rows, rows), 1)
    return c <= r


def extended(value):
    return jnp.concatenate([value, jnp.ones_like(value)], axis=1)


NT = (((1,), (1,)), ((), ()))


def local_body(n_back, plane_ref, *refs):
    q_ref, qid_ref, kid_ref, cos_ref, sin_ref = refs[:5]
    pairs = refs[5 : 5 + n_back + 1]
    o_ref, acc_ref, k_ref, v_ref = refs[5 + n_back + 1 :]
    parts, tokens, width = q_ref.shape
    rows = parts * tokens
    members = width // HEAD
    plane = plane_ref[0]
    scale = log2e * HEAD**-0.5
    q_all = q_ref.at[...]

    for d in range(n_back + 1):

        @pl.when(plane >= d)
        def _(d=d):
            keys = pairs[d][:, 0].reshape(rows, HEAD).astype(jnp.float32)
            k_ref[...] = rotated_unit(keys, cos_ref[d], sin_ref[d]).astype(k_ref.dtype)
            v_ref[...] = extended(pairs[d][:, 1].reshape(rows, HEAD))
            allowed = qid_ref[:, :1] == kid_ref[d, :1, :]
            if d == 0:
                allowed = allowed & causal(rows)

            def member(g, carry):
                at = pl.multiple_of(g * HEAD, HEAD)
                q = q_all[:, :, pl.ds(at, HEAD)].reshape(rows, HEAD)
                scores = lax.dot_general(q, k_ref[...], NT, preferred_element_type=jnp.float32)
                weights = jnp.where(allowed, jnp.exp2(scores * scale), 0.0).astype(jnp.bfloat16)
                part = jnp.dot(weights, v_ref[...], preferred_element_type=jnp.float32)
                if d == 0:
                    acc_ref[g] = part
                else:
                    acc_ref[g] += part
                return carry

            lax.fori_loop(0, members, member, 0)

    def finish(g, carry):
        at = pl.multiple_of(g * HEAD, HEAD)
        acc = acc_ref[g]
        out = (acc[:, :HEAD] / acc[:, HEAD:]).astype(o_ref.dtype)
        o_ref[:, :, pl.ds(at, HEAD)] = out.reshape(parts, tokens, HEAD)
        return carry

    lax.fori_loop(0, members, finish, 0)


def global_body(n_back, plane_ref, *refs):
    q_ref, scale_ref = refs[:2]
    pairs = refs[2 : 2 + n_back + 1]
    o_ref, acc_ref, peak_ref, v_ref = refs[2 + n_back + 1 :]
    parts, tokens, width = q_ref.shape
    rows = parts * tokens
    members = width // HEAD
    plane = plane_ref[0]

    for d in range(n_back + 1):

        @pl.when(plane >= d)
        def _(d=d):
            v_ref[...] = extended(pairs[d][:, 1].reshape(rows, HEAD))
            allowed = causal(rows) if d == 0 else None

            def member(g, carry):
                at = pl.multiple_of(g * HEAD, HEAD)
                q = q_ref[:, :, pl.ds(at, HEAD)].reshape(rows, HEAD)
                keys = pairs[d][:, 0].reshape(rows, HEAD)
                scores = lax.dot_general(q, keys, NT, preferred_element_type=jnp.float32)
                scores = scores * scale_ref[:, :1]
                if d == 0:
                    scores = jnp.where(allowed, scores, masked_score)
                    peak = jnp.max(scores, axis=1, keepdims=True)
                else:
                    before = peak_ref[g][:, :1]
                    peak = jnp.maximum(before, jnp.max(scores, axis=1, keepdims=True))
                weights = jnp.exp2(scores - peak).astype(jnp.bfloat16)
                part = jnp.dot(weights, v_ref[...], preferred_element_type=jnp.float32)
                peak_ref[g] = jnp.broadcast_to(peak, (rows, HEAD))
                if d == 0:
                    acc_ref[g] = part
                else:
                    acc_ref[g] = acc_ref[g] * jnp.exp2(before - peak) + part
                return carry

            lax.fori_loop(0, members, member, 0)

    def finish(g, carry):
        at = pl.multiple_of(g * HEAD, HEAD)
        acc = acc_ref[g]
        out = (acc[:, :HEAD] / acc[:, HEAD:]).astype(o_ref.dtype)
        o_ref[:, :, pl.ds(at, HEAD)] = out.reshape(parts, tokens, HEAD)
        return carry

    lax.fori_loop(0, members, finish, 0)


def exchange(x):
    return lax.all_to_all(x, IN_PLANE, split_axis=0, concat_axis=0, tiled=True)


def upward(x, by):
    size = lax.axis_size("plane")
    return lax.ppermute(x, "plane", [(i, i + by) for i in range(size - by)])


def gathered(own, n_back):
    blocks = [own]
    for d in range(1, n_back + 1):
        step = 1 if d < 3 else 3
        blocks.append(upward(blocks[d - step], step))
    return blocks


def shards(query_local, key_local, value_local, labels, query_global, key_global, value_global):
    planes = lax.axis_size("plane")
    plane = lax.axis_index("plane")
    parts = lax.axis_size("row") * lax.axis_size("head")
    spot = lax.axis_index("row") * lax.axis_size("head") + lax.axis_index("head")
    tokens = query_local.shape[0]
    width = query_local.shape[1] // parts
    members = width // HEAD
    rows = parts * tokens
    local_back = min(planes - 1, -(-(STRETCH - 1) // rows))

    local_pair = exchange(pack_pair(key_local, value_local))
    global_pair = exchange(pack_pair(key_global, value_global))
    local_blocks = gathered(local_pair, local_back)
    global_blocks = gathered(global_pair, planes - 1)

    own_pos = (plane * parts + spot) * tokens + jnp.arange(tokens, dtype=jnp.int32)
    cosine, sine = rope_tables(own_pos)
    packed = jax.ShapeDtypeStruct((parts, tokens, width), query_local.dtype)
    q_local = exchange(vmem_call(pack_query_body, packed, 3, nbytes=4 * query_local.size)(query_local, cosine, sine))
    q_global = exchange(vmem_call(pack_plain_body, packed, 1, nbytes=4 * query_local.size)(query_global))

    plane_arg = plane.reshape(1).astype(jnp.int32)
    row_pos = plane * rows + jnp.arange(rows, dtype=jnp.int32)
    back = jnp.arange(local_back + 1, dtype=jnp.int32)
    key_pos = ((plane - back)[:, None] * rows + jnp.arange(rows, dtype=jnp.int32)[None, :]).reshape(-1)
    k_cos, k_sin = rope_tables(key_pos)
    k_cos = k_cos.reshape(local_back + 1, rows, HEAD)
    k_sin = k_sin.reshape(local_back + 1, rows, HEAD)
    row_ids = lax.dynamic_slice_in_dim(labels, plane * rows, rows, 0)
    q_ids = jnp.broadcast_to(row_ids[:, None], (rows, HEAD))
    key_ids = jnp.stack(
        [lax.dynamic_slice_in_dim(labels, jnp.maximum(plane - d, 0) * rows, rows, 0) for d in range(local_back + 1)]
    )
    key_ids = jnp.broadcast_to(key_ids[:, None, :], (local_back + 1, 8, rows))
    temper = 1.0 + temper_slope * jnp.log(((row_pos + 1) // temper_floor + 1).astype(jnp.float32))
    scale = jnp.broadcast_to((temper * (log2e * HEAD**-0.5))[:, None], (rows, HEAD))

    out_shape = jax.ShapeDtypeStruct((parts, tokens, width), query_local.dtype)
    pair_flops = 2 * 3 * rows * rows * HEAD * members
    local_out = vmem_call(
        functools.partial(local_body, local_back),
        out_shape,
        5 + local_back + 1,
        flops=pair_flops * (local_back + 1),
        nbytes=4 * rows * width * 2,
        exps=rows * rows * members * (local_back + 1),
        scratch=[
            pltpu.VMEM((members, rows, 2 * HEAD), jnp.float32),
            pltpu.VMEM((rows, HEAD), jnp.bfloat16),
            pltpu.VMEM((rows, 2 * HEAD), jnp.bfloat16),
        ],
        smem=1,
    )(plane_arg, q_local, q_ids, key_ids, k_cos, k_sin, *local_blocks)
    local_heads = unpack(exchange(local_out))

    global_out = vmem_call(
        functools.partial(global_body, planes - 1),
        out_shape,
        2 + planes,
        flops=pair_flops * planes,
        nbytes=4 * rows * width * 2,
        exps=rows * rows * members * planes,
        scratch=[
            pltpu.VMEM((members, rows, 2 * HEAD), jnp.float32),
            pltpu.VMEM((members, rows, HEAD), jnp.float32),
            pltpu.VMEM((rows, 2 * HEAD), jnp.bfloat16),
        ],
        smem=1,
    )(plane_arg, q_global, scale, *global_blocks)
    global_heads = unpack(exchange(global_out))
    return local_heads, global_heads


def solution(mesh):
    ctx, head = mesh.shape["ctx"], mesh.shape["head"]

    def run(*args):
        key_heads = args[1].shape[1] // HEAD
        row = max(1, key_heads // head)
        grid = Mesh(mesh.devices.reshape(ctx // row, row, head), ("plane", "row", "head"))
        spread = P(("plane", "row", "head"), None)
        return jax.shard_map(
            shards,
            mesh=grid,
            in_specs=(spread, spread, spread, P(), spread, spread, spread),
            out_specs=(spread, spread),
            check_vma=False,
        )(*args)

    return run
```

time: 251 us -> 120 us (0.48)
  blocking collectives: 70.9 us -> 0 us
  Pallas kernels: 0 us -> 43 us
  matrix products: 29.6 us -> 0 us
  local copies, waits for them, and re-layouts: 33.1 us -> 4.68 us
  loops' own time: 24 us -> 0 us
  other arithmetic: 27.3 us -> 4.19 us
  waiting for transfers between devices: 20.6 us -> 32.4 us
  starting transfers between devices: 38.1 us -> 32.9 us
  between operations: 4.43 us -> 0.75 us
    all_gather x2 -> x0, blocking collectives: 70.9 us -> none  [the longest x1 38.8 us: shards(): key_piece = lax.all_gather(key_global, 'ctx', axis=0, tiled=True)]
    pallas_call x0 -> x8, Pallas kernels: none -> 43 us  [the longest x1 18.5 us: shards(): vmem_call(functools.partial(global_body, planes - 1), out_shape, 2 + plan...]
    dot_general x66 -> x0, matrix products: 29.6 us -> none  [the longest x33 17 us: update(): jnp.einsum('hgqk,khd->qhgd', weights.astype(jnp.bfloat16), value_block, p...]
    another operation x38 -> x0, loops' own time: 24 us -> none  [the longest x1 22.2 us: shards(): lax.fori_loop(0, piece_rows // half_rows, advance, (initial, initial))]
    dynamic_slice x32 -> x1, local copies, waits for them, and re-layouts: 14.8 us -> 0.1 us  [shards(): lax.dynamic_slice_in_dim(labels, jnp.maximum(plane - d, 0) * rows, rows, 0)]
    ppermute x8 -> x5, waiting for transfers between devices: 5.56 us -> 18.6 us  [upward(): return lax.ppermute(x, 'plane', [(i, i + by) for i in range(size - by)])]
    reduce_or x16 -> x0, other arithmetic: 12.8 us -> none  [global_update(): return lax.cond(jnp.any(allowed), update, lambda carried: carried, running)]
    all_to_all x9 -> x0, local copies, waits for them, and re-layouts: 9.16 us -> none  [the longest x2 2.14 us: shards(): lax.all_to_all(local_heads, 'head', split_axis=0, concat_axis=1, tiled=True)]
  transfers between devices with their start and end apart: 16 -> 11, of which waited for: 5 -> 6; matrix products, arithmetic and copies ran while one was open for 34% -> 5% of each run, Pallas kernels for 0% -> 34%
where the time goes in v1:
time: 120 us; the launch traced here: 118 us
  Pallas kernels  43 us (36%)
  starting transfers between devices  32.9 us (27%)
  waiting for transfers between devices  32.4 us (27%)
  local copies, waits for them, and re-layouts  4.68 us (4%)
  other arithmetic  4.19 us (3%)
    all_to_all x6, starting transfers between devices, exchange(): return lax.all_to_all(x, IN_PLANE, split_axis=0, concat_axis=0, tiled=True)  26.5 us
    ppermute x5, waiting for transfers between devices, upward(): return lax.ppermute(x, 'plane', [(i, i + by) for i in range(size - by)])  18.6 us
    pallas_call x1, Pallas kernels, shards(): vmem_call(functools.partial(global_body, planes - 1), out_shape, 2 + plan...  18.5 us
    all_to_all x6, waiting for transfers between devices, exchange(): return lax.all_to_all(x, IN_PLANE, split_axis=0, concat_axis=0, tiled=True)  13.8 us
    pallas_call x1, Pallas kernels, shards(): vmem_call(functools.partial(local_body, local_back), out_shape, 5 + local...  10.7 us
    ppermute x5, starting transfers between devices, upward(): return lax.ppermute(x, 'plane', [(i, i + by) for i in range(size - by)])  6.44 us
    pallas_call x1, Pallas kernels, shards(): vmem_call(pack_query_body, packed, 3, nbytes=4 * query_local.size)  5 us
    select_n x2, other arithmetic, rope_tables(): return (jnp.cos(angles), jnp.where(lane < half, -sine, sine))  4.06 us
  transfers between devices with their start and end apart: 11, of which 6 were waited for; matrix products, arithmetic and copies ran while one was open for 5% of the time, Pallas kernels for 34%

profile of v1, /device:TPU:28, one launch (start us, length us, event | category | flops | bytes accessed | tf_op | source)
XLA Modules:
  0.0 118.0 jit_solution(16817219844423328864)
XLA Ops:
  0.6 1.7 %shard_map.87 = bf16[8,2,48,128]{3,2,1,0:T(8,128)(2,1)} custom-call(bf16[48,1024]{1,0:T(8,128)(2,1)} %k_ref.2, bf16[48,1024]{1,0:T(8,128)(2,1)} %v_ref.2), custom_call_target="tpu_custom_call" | custom-call | bytes 393216 | tf_op jit(solution)/shard_map/pallas_call | solution.py:61
  2.3 4.2 %all-to-all-start.1 = ((bf16[8,2,48,128]{3,2,1,0:T(8,128)(2,1)}), bf16[8,2,48,128]{3,2,1,0:T(8,128)(2,1)S(1)}, u32[]{:S(2)}, u32[]{:S(2)}) async-start(bf16[8,2,48,128]{3,2,1,0:T(8,128)(2,1)} %shard_map.87), calls=%async_computation.1 | async-start | bytes 393216 | tf_op jit(solution)/shard_map/all_to_all | solution.py:201
  6.5 1.7 %shard_map.91 = bf16[8,2,48,128]{3,2,1,0:T(8,128)(2,1)} custom-call(bf16[48,1024]{1,0:T(8,128)(2,1)} %k_ref.3, bf16[48,1024]{1,0:T(8,128)(2,1)} %v_ref.3), custom_call_target="tpu_custom_call" | custom-call | bytes 393216 | tf_op jit(solution)/shard_map/pallas_call | solution.py:61
  8.2 3.1 %all-to-all-done.1.refs_5_ = bf16[8,2,48,128]{3,2,1,0:T(8,128)(2,1)S(1)} async-done(((bf16[8,2,48,128]{3,2,1,0:T(8,128)(2,1)}), bf16[8,2,48,128]{3,2,1,0:T(8,128)(2,1)S(1)}, u32[]{:S(2)}, u32[]{:S(2)}) %all-to-all-start.1) | async-done | bytes 196640 | tf_op jit(solution)/shard_map/all_to_all | solution.py:201
  11.2 0.0 copy-start.4
  11.3 4.8 %all-to-all-start.4 = ((bf16[8,2,48,128]{3,2,1,0:T(8,128)(2,1)}), bf16[8,2,48,128]{3,2,1,0:T(8,128)(2,1)S(1)}, u32[]{:S(2)}, u32[]{:S(2)}) async-start(bf16[8,2,48,128]{3,2,1,0:T(8,128)(2,1)} %shard_map.91), calls=%async_computation.4 | async-start | bytes 393216 | tf_op jit(solution)/shard_map/all_to_all | solution.py:201
  16.0 0.8 negate_select_fusion.1
  16.8 5.0 %shard_map.86 = bf16[8,48,640]{2,1,0:T(8,128)(2,1)} custom-call(bf16[48,5120]{1,0:T(8,128)(2,1)} %q_ref.2, f32[48,128]{1,0:T(8,128)} %get-tuple-element.9.cos_ref, f32[48,128]{1,0:T(8,128)} %get-tuple-element.8.sin_ref), custom_call_target="tpu_custom_call" | custom-call | bytes 983040 | tf_op jit(solution)/shard_map/pallas_call | solution.py:236
  21.8 0.0 all-to-all-done.4.refs_2_
  21.8 0.0 copy-start.5
  21.8 4.2 %all-to-all-start = ((bf16[8,48,640]{2,1,0:T(8,128)(2,1)}), bf16[8,48,640]{2,1,0:T(8,128)(2,1)S(1)}, u32[]{:S(2)}, u32[]{:S(2)}) async-start(bf16[8,48,640]{2,1,0:T(8,128)(2,1)} %shard_map.86), calls=%async_computation | async-start | bytes 983040 | tf_op jit(solution)/shard_map/all_to_all | solution.py:201
  26.0 1.8 %shard_map.90 = bf16[8,48,640]{2,1,0:T(8,128)(2,1)} custom-call(bf16[48,5120]{1,0:T(8,128)(2,1)} %q_ref.3), custom_call_target="tpu_custom_call" | custom-call | bytes 983040 | tf_op jit(solution)/shard_map/pallas_call | solution.py:237
  27.9 0.1 add_convert_fusion
  28.0 0.0 copy-done.4
  28.0 1.3 %collective-permute-start = (bf16[8,2,48,128]{3,2,1,0:T(8,128)(2,1)S(1)}, bf16[8,2,48,128]{3,2,1,0:T(8,128)(2,1)S(1)}, u32[]{:S(2)}, u32[]{:S(2)}) collective-permute-start(bf16[8,2,48,128]{3,2,1,0:T(8,128)(2,1)S(1)} %all-to-all-done.1.refs_5_), channel_id=1, source_target_pairs={{0,8},{8,16},{16,24},{1,9},{9,17},{17,25},{2,10},{10,18},{18,26},{... | collective-permute-start | bytes 589832 | tf_op jit(solution)/shard_map/ppermute | solution.py:206
  29.3 4.7 %all-to-all-done.refs_0_ = bf16[8,48,640]{2,1,0:T(8,128)(2,1)S(1)} async-done(((bf16[8,48,640]{2,1,0:T(8,128)(2,1)}), bf16[8,48,640]{2,1,0:T(8,128)(2,1)S(1)}, u32[]{:S(2)}, u32[]{:S(2)}) %all-to-all-start) | async-done | bytes 491552 | tf_op jit(solution)/shard_map/all_to_all | solution.py:201
  33.9 0.0 copy-start.3
  33.9 4.9 %all-to-all-start.3 = ((bf16[8,48,640]{2,1,0:T(8,128)(2,1)}), bf16[8,48,640]{2,1,0:T(8,128)(2,1)S(1)}, u32[]{:S(2)}, u32[]{:S(2)}) async-start(bf16[8,48,640]{2,1,0:T(8,128)(2,1)} %shard_map.90), calls=%async_computation.3 | async-start | bytes 983040 | tf_op jit(solution)/shard_map/all_to_all | solution.py:201
  38.8 3.3 %negate_select_fusion = (f32[3,384,128]{2,1,0:T(8,128)}, f32[3,384,128]{2,1,0:T(8,128)}) fusion(f32[128]{0:T(128)S(1)} %fusion.12, f32[3,384]{1,0:T(4,128)S(1)} %add_convert_fusion, pred[128]{0:T(512)(128)(4,1)S(1)} %iota_compare_fusion), kind=kLoop, calls=%fused_computation | loop fusion | flops 442368 | bytes 1184896 | tf_op jit(solution)/shard_map/jit(_where)/select_n | solution.py:32
  42.1 0.0 copy-done.3
  42.1 0.0 copy-start.6
  42.1 0.0 collective-permute-done.refs_6_
  42.1 0.0 copy-start.7
  42.1 1.3 %collective-permute-start.1 = (bf16[8,2,48,128]{3,2,1,0:T(8,128)(2,1)S(1)}, bf16[8,2,48,128]{3,2,1,0:T(8,128)(2,1)S(1)}, u32[]{:S(2)}, u32[]{:S(2)}) collective-permute-start(bf16[8,2,48,128]{3,2,1,0:T(8,128)(2,1)S(1)} %collective-permute-done.refs_6_), channel_id=1, source_target_pairs={{0,8},{8,16},{16,24},{1,9},{9,17},{17,25},{2,10},{10,18},{18,26},{... | collective-permute-start | bytes 589832 | tf_op jit(solution)/shard_map/ppermute | solution.py:206
  43.4 0.0 copy-done.6
  43.4 0.1 fusion.13
  43.5 1.3 %collective-permute-start.2 = (bf16[8,2,48,128]{3,2,1,0:T(8,128)(2,1)S(1)}, bf16[8,2,48,128]{3,2,1,0:T(8,128)(2,1)S(1)}, u32[]{:S(2)}, u32[]{:S(2)}) collective-permute-start(bf16[8,2,48,128]{3,2,1,0:T(8,128)(2,1)S(1)} %all-to-all-done.4.refs_2_), channel_id=1, source_target_pairs={{0,8},{8,16},{16,24},{1,9},{9,17},{17,25},{2,10},{10,18},{18,26},{... | collective-permute-start | bytes 589832 | tf_op jit(solution)/shard_map/ppermute | solution.py:206
  44.8 6.9 %collective-permute-done.1.refs_7_ = bf16[8,2,48,128]{3,2,1,0:T(8,128)(2,1)S(1)} collective-permute-done((bf16[8,2,48,128]{3,2,1,0:T(8,128)(2,1)S(1)}, bf16[8,2,48,128]{3,2,1,0:T(8,128)(2,1)S(1)}, u32[]{:S(2)}, u32[]{:S(2)}) %collective-permute-start.1) | collective-permute-done | bytes 196640 | tf_op jit(solution)/shard_map/ppermute | solution.py:206
  51.8 0.0 copy-start.9
  51.8 0.8 broadcast_in_dim.23.refs_1_
  52.6 0.6 broadcast_in_dim.24.refs_2_
  53.2 0.0 copy-done.7
  53.2 0.0 copy-done.9
  53.2 10.7 %shard_map.88 = bf16[8,48,640]{2,1,0:T(8,128)(2,1)} custom-call(s32[1]{0:T(128)} %bitcast.plane_ref, bf16[8,48,640]{2,1,0:T(8,128)(2,1)} %copy-done.3, s32[384,128]{1,0:T(8,128)} %broadcast_in_dim.23.refs_1_, s32[3,8,384]{2,1,0:T(8,128)} %broadcast_in_dim.24.refs_2_, f32[3,384,128]{2,1,0:T(8,128)} %get-tuple-element.7.refs_3_, ...), custom_call_target="tpu_custom_call" | custom-call | flops 1698693120 | bytes 1966080 | tf_op jit(solution)/shard_map/pallas_call | solution.py:257
  63.9 0.0 all-to-all-done.3.refs_0_
  63.9 0.0 copy-start.2
  63.9 0.8 copy-done.2
  64.7 4.2 %all-to-all-start.2 = ((bf16[8,48,640]{2,1,0:T(8,128)(2,1)}), bf16[8,48,640]{2,1,0:T(8,128)(2,1)S(1)}, u32[]{:S(2)}, u32[]{:S(2)}) async-start(bf16[8,48,640]{2,1,0:T(8,128)(2,1)} %shard_map.88), calls=%async_computation.2 | async-start | bytes 983040 | tf_op jit(solution)/shard_map/all_to_all | solution.py:201
  68.9 0.0 copy-done.5
  68.9 1.3 %collective-permute-start.4 = (bf16[8,2,48,128]{3,2,1,0:T(8,128)(2,1)S(1)}, bf16[8,2,48,128]{3,2,1,0:T(8,128)(2,1)S(1)}, u32[]{:S(2)}, u32[]{:S(2)}) collective-permute-start(bf16[8,2,48,128]{3,2,1,0:T(8,128)(2,1)S(1)} %all-to-all-done.4.refs_2_), channel_id=1, source_target_pairs={{0,24},{1,25},{2,26},{3,27},{4,28},{5,29},{6,30},{7,31}} | collective-permute-start | bytes 589832 | tf_op jit(solution)/shard_map/ppermute | solution.py:206
  70.2 0.0 collective-permute-done.2.refs_3_
  70.2 0.0 copy-start.8
  70.2 1.3 %collective-permute-start.3 = (bf16[8,2,48,128]{3,2,1,0:T(8,128)(2,1)S(1)}, bf16[8,2,48,128]{3,2,1,0:T(8,128)(2,1)S(1)}, u32[]{:S(2)}, u32[]{:S(2)}) collective-permute-start(bf16[8,2,48,128]{3,2,1,0:T(8,128)(2,1)S(1)} %collective-permute-done.2.refs_3_), channel_id=1, source_target_pairs={{0,8},{8,16},{16,24},{1,9},{9,17},{17,25},{2,10},{10,18},{18,26},{... | collective-permute-start | bytes 589832 | tf_op jit(solution)/shard_map/ppermute | solution.py:206
  71.5 8.9 %collective-permute-done.4.refs_5_ = bf16[8,2,48,128]{3,2,1,0:T(8,128)(2,1)S(1)} collective-permute-done((bf16[8,2,48,128]{3,2,1,0:T(8,128)(2,1)S(1)}, bf16[8,2,48,128]{3,2,1,0:T(8,128)(2,1)S(1)}, u32[]{:S(2)}, u32[]{:S(2)}) %collective-permute-start.4) | collective-permute-done | bytes 196640 | tf_op jit(solution)/shard_map/ppermute | solution.py:206
  80.4 0.0 copy-start.10
  80.4 2.8 %collective-permute-done.3.refs_4_ = bf16[8,2,48,128]{3,2,1,0:T(8,128)(2,1)S(1)} collective-permute-done((bf16[8,2,48,128]{3,2,1,0:T(8,128)(2,1)S(1)}, bf16[8,2,48,128]{3,2,1,0:T(8,128)(2,1)S(1)}, u32[]{:S(2)}, u32[]{:S(2)}) %collective-permute-start.3) | collective-permute-done | bytes 196640 | tf_op jit(solution)/shard_map/ppermute | solution.py:206
  83.2 0.0 copy-start.11
  83.2 0.8 broadcast_in_dim.26.refs_1_
  84.0 0.0 copy-done.8
  84.0 0.0 copy-done.10
  84.0 0.0 copy-done.11
  84.0 18.5 %shard_map.92 = bf16[8,48,640]{2,1,0:T(8,128)(2,1)} custom-call(s32[1]{0:T(128)} %bitcast.plane_ref, bf16[8,48,640]{2,1,0:T(8,128)(2,1)} %copy-done.2, f32[384,128]{1,0:T(8,128)} %broadcast_in_dim.26.refs_1_, bf16[8,2,48,128]{3,2,1,0:T(8,128)(2,1)} %copy-done.5, bf16[8,2,48,128]{3,2,1,0:T(8,128)(2,1)} %copy-done.8, bf16[8,2,48,128]{3,2,1,0:T(8,128)(2,1)} %copy-done.11, ...), custom_call_target="tpu_custom_call" | custom-call | flops 2264924160 | bytes 1966080 | tf_op jit(solution)/shard_map/pallas_call | solution.py:273
  102.5 0.0 all-to-all-done.2.x_ref
  102.5 0.0 copy-start
  102.5 0.8 copy-done
  103.3 4.2 %all-to-all-start.5 = ((bf16[8,48,640]{2,1,0:T(8,128)(2,1)}), bf16[8,48,640]{2,1,0:T(8,128)(2,1)S(1)}, u32[]{:S(2)}, u32[]{:S(2)}) async-start(bf16[8,48,640]{2,1,0:T(8,128)(2,1)} %shard_map.92), calls=%async_computation.5 | async-start | bytes 983040 | tf_op jit(solution)/shard_map/all_to_all | solution.py:201
  107.5 1.8 %shard_map.89 = bf16[48,5120]{1,0:T(8,128)(2,1)} custom-call(bf16[8,48,640]{2,1,0:T(8,128)(2,1)} %copy-done), custom_call_target="tpu_custom_call" | custom-call | bytes 983040 | tf_op jit(solution)/shard_map/pallas_call | solution.py:89
  109.3 6.1 %all-to-all-done.5.x_ref = bf16[8,48,640]{2,1,0:T(8,128)(2,1)S(1)} async-done(((bf16[8,48,640]{2,1,0:T(8,128)(2,1)}), bf16[8,48,640]{2,1,0:T(8,128)(2,1)S(1)}, u32[]{:S(2)}, u32[]{:S(2)}) %all-to-all-start.5) | async-done | bytes 491552 | tf_op jit(solution)/shard_map/all_to_all | solution.py:201
  115.4 0.0 copy-start.1
  115.4 0.8 copy-done.1
  116.2 1.8 %shard_map.93 = bf16[48,5120]{1,0:T(8,128)(2,1)} custom-call(bf16[8,48,640]{2,1,0:T(8,128)(2,1)} %copy-done.1), custom_call_target="tpu_custom_call" | custom-call | bytes 983040 | tf_op jit(solution)/shard_map/pallas_call | solution.py:89
  (9 shorter events, 0.1 us)
Async XLA Ops:
  2.3 9.0 %all-to-all-start.1 = ((bf16[8,2,48,128]{3,2,1,0:T(8,128)(2,1)}), bf16[8,2,48,128]{3,2,1,0:T(8,128)(2,1)S(1)}, u32[]{:S(2)}, u32[]{:S(2)}) async-start(bf16[8,2,48,128]{3,2,1,0:T(8,128)(2,1)} %shard_map.87), calls=%async_computation.1 | async-start | bytes 393216 | tf_op jit(solution)/shard_map/all_to_all | solution.py:201
  11.2 16.7 %copy-start.4 = (bf16[8,2,48,128]{3,2,1,0:T(8,128)(2,1)}, bf16[8,2,48,128]{3,2,1,0:T(8,128)(2,1)S(1)}, u32[]{:S(2)}) copy-start(bf16[8,2,48,128]{3,2,1,0:T(8,128)(2,1)S(1)} %all-to-all-done.1.refs_5_) | copy-start | bytes 589828
  11.3 10.6 %all-to-all-start.4 = ((bf16[8,2,48,128]{3,2,1,0:T(8,128)(2,1)}), bf16[8,2,48,128]{3,2,1,0:T(8,128)(2,1)S(1)}, u32[]{:S(2)}, u32[]{:S(2)}) async-start(bf16[8,2,48,128]{3,2,1,0:T(8,128)(2,1)} %shard_map.91), calls=%async_computation.4 | async-start | bytes 393216 | tf_op jit(solution)/shard_map/all_to_all | solution.py:201
  21.8 47.1 %copy-start.5 = (bf16[8,2,48,128]{3,2,1,0:T(8,128)(2,1)}, bf16[8,2,48,128]{3,2,1,0:T(8,128)(2,1)S(1)}, u32[]{:S(2)}) copy-start(bf16[8,2,48,128]{3,2,1,0:T(8,128)(2,1)S(1)} %all-to-all-done.4.refs_2_) | copy-start | bytes 589828
  21.8 12.1 %all-to-all-start = ((bf16[8,48,640]{2,1,0:T(8,128)(2,1)}), bf16[8,48,640]{2,1,0:T(8,128)(2,1)S(1)}, u32[]{:S(2)}, u32[]{:S(2)}) async-start(bf16[8,48,640]{2,1,0:T(8,128)(2,1)} %shard_map.86), calls=%async_computation | async-start | bytes 983040 | tf_op jit(solution)/shard_map/all_to_all | solution.py:201
  28.0 14.1 %collective-permute-start = (bf16[8,2,48,128]{3,2,1,0:T(8,128)(2,1)S(1)}, bf16[8,2,48,128]{3,2,1,0:T(8,128)(2,1)S(1)}, u32[]{:S(2)}, u32[]{:S(2)}) collective-permute-start(bf16[8,2,48,128]{3,2,1,0:T(8,128)(2,1)S(1)} %all-to-all-done.1.refs_5_), channel_id=1, source_target_pairs={{0,8},{8,16},{16,24},{1,9},{9,17},{17,25},{2,10},{10,18},{18,26},{... | collective-permute-start | bytes 589832 | tf_op jit(solution)/shard_map/ppermute | solution.py:206
  33.9 8.1 %copy-start.3 = (bf16[8,48,640]{2,1,0:T(8,128)(2,1)}, bf16[8,48,640]{2,1,0:T(8,128)(2,1)S(1)}, u32[]{:S(2)}) copy-start(bf16[8,48,640]{2,1,0:T(8,128)(2,1)S(1)} %all-to-all-done.refs_0_) | copy-start | bytes 1474564
  33.9 29.9 %all-to-all-start.3 = ((bf16[8,48,640]{2,1,0:T(8,128)(2,1)}), bf16[8,48,640]{2,1,0:T(8,128)(2,1)S(1)}, u32[]{:S(2)}, u32[]{:S(2)}) async-start(bf16[8,48,640]{2,1,0:T(8,128)(2,1)} %shard_map.90), calls=%async_computation.3 | async-start | bytes 983040 | tf_op jit(solution)/shard_map/all_to_all | solution.py:201
  42.1 1.3 %copy-start.6 = (s32[1536]{0:T(1024)S(1)}, s32[1536]{0:T(1024)}, u32[]{:S(2)}) copy-start(s32[1536]{0:T(1024)} %param.10) | copy-start | bytes 18436
  42.1 11.1 %copy-start.7 = (bf16[8,2,48,128]{3,2,1,0:T(8,128)(2,1)}, bf16[8,2,48,128]{3,2,1,0:T(8,128)(2,1)S(1)}, u32[]{:S(2)}) copy-start(bf16[8,2,48,128]{3,2,1,0:T(8,128)(2,1)S(1)} %collective-permute-done.refs_6_) | copy-start | bytes 589828
  42.1 9.7 %collective-permute-start.1 = (bf16[8,2,48,128]{3,2,1,0:T(8,128)(2,1)S(1)}, bf16[8,2,48,128]{3,2,1,0:T(8,128)(2,1)S(1)}, u32[]{:S(2)}, u32[]{:S(2)}) collective-permute-start(bf16[8,2,48,128]{3,2,1,0:T(8,128)(2,1)S(1)} %collective-permute-done.refs_6_), channel_id=1, source_target_pairs={{0,8},{8,16},{16,24},{1,9},{9,17},{17,25},{2,10},{10,18},{18,26},{... | collective-permute-start | bytes 589832 | tf_op jit(solution)/shard_map/ppermute | solution.py:206
  43.5 26.6 %collective-permute-start.2 = (bf16[8,2,48,128]{3,2,1,0:T(8,128)(2,1)S(1)}, bf16[8,2,48,128]{3,2,1,0:T(8,128)(2,1)S(1)}, u32[]{:S(2)}, u32[]{:S(2)}) collective-permute-start(bf16[8,2,48,128]{3,2,1,0:T(8,128)(2,1)S(1)} %all-to-all-done.4.refs_2_), channel_id=1, source_target_pairs={{0,8},{8,16},{16,24},{1,9},{9,17},{17,25},{2,10},{10,18},{18,26},{... | collective-permute-start | bytes 589832 | tf_op jit(solution)/shard_map/ppermute | solution.py:206
  51.8 1.4 %copy-start.9 = (bf16[8,2,48,128]{3,2,1,0:T(8,128)(2,1)}, bf16[8,2,48,128]{3,2,1,0:T(8,128)(2,1)S(1)}, u32[]{:S(2)}) copy-start(bf16[8,2,48,128]{3,2,1,0:T(8,128)(2,1)S(1)} %collective-permute-done.1.refs_7_) | copy-start | bytes 589828
  63.9 0.8 copy-start.2
  64.7 37.8 %all-to-all-start.2 = ((bf16[8,48,640]{2,1,0:T(8,128)(2,1)}), bf16[8,48,640]{2,1,0:T(8,128)(2,1)S(1)}, u32[]{:S(2)}, u32[]{:S(2)}) async-start(bf16[8,48,640]{2,1,0:T(8,128)(2,1)} %shard_map.88), calls=%async_computation.2 | async-start | bytes 983040 | tf_op jit(solution)/shard_map/all_to_all | solution.py:201
  68.9 11.5 %collective-permute-start.4 = (bf16[8,2,48,128]{3,2,1,0:T(8,128)(2,1)S(1)}, bf16[8,2,48,128]{3,2,1,0:T(8,128)(2,1)S(1)}, u32[]{:S(2)}, u32[]{:S(2)}) collective-permute-start(bf16[8,2,48,128]{3,2,1,0:T(8,128)(2,1)S(1)} %all-to-all-done.4.refs_2_), channel_id=1, source_target_pairs={{0,24},{1,25},{2,26},{3,27},{4,28},{5,29},{6,30},{7,31}} | collective-permute-start | bytes 589832 | tf_op jit(solution)/shard_map/ppermute | solution.py:206
  70.2 13.8 %copy-start.8 = (bf16[8,2,48,128]{3,2,1,0:T(8,128)(2,1)}, bf16[8,2,48,128]{3,2,1,0:T(8,128)(2,1)S(1)}, u32[]{:S(2)}) copy-start(bf16[8,2,48,128]{3,2,1,0:T(8,128)(2,1)S(1)} %collective-permute-done.2.refs_3_) | copy-start | bytes 589828
  70.2 13.0 %collective-permute-start.3 = (bf16[8,2,48,128]{3,2,1,0:T(8,128)(2,1)S(1)}, bf16[8,2,48,128]{3,2,1,0:T(8,128)(2,1)S(1)}, u32[]{:S(2)}, u32[]{:S(2)}) collective-permute-start(bf16[8,2,48,128]{3,2,1,0:T(8,128)(2,1)S(1)} %collective-permute-done.2.refs_3_), channel_id=1, source_target_pairs={{0,8},{8,16},{16,24},{1,9},{9,17},{17,25},{2,10},{10,18},{18,26},{... | collective-permute-start | bytes 589832 | tf_op jit(solution)/shard_map/ppermute | solution.py:206
  80.4 3.6 %copy-start.10 = (bf16[8,2,48,128]{3,2,1,0:T(8,128)(2,1)}, bf16[8,2,48,128]{3,2,1,0:T(8,128)(2,1)S(1)}, u32[]{:S(2)}) copy-start(bf16[8,2,48,128]{3,2,1,0:T(8,128)(2,1)S(1)} %collective-permute-done.4.refs_5_) | copy-start | bytes 589828
  83.2 0.8 copy-start.11
  102.5 0.8 copy-start
  103.3 12.1 %all-to-all-start.5 = ((bf16[8,48,640]{2,1,0:T(8,128)(2,1)}), bf16[8,48,640]{2,1,0:T(8,128)(2,1)S(1)}, u32[]{:S(2)}, u32[]{:S(2)}) async-start(bf16[8,48,640]{2,1,0:T(8,128)(2,1)} %shard_map.92), calls=%async_computation.5 | async-start | bytes 983040 | tf_op jit(solution)/shard_map/all_to_all | solution.py:201
  115.4 0.8 copy-start.1

commit v2 on v1

v2 whole, which is shorter than its diff:
```python
import functools

import jax
import jax.numpy as jnp
from jax import lax
from jax.experimental import pallas as pl
from jax.experimental.pallas import tpu as pltpu
from jax.sharding import Mesh
from jax.sharding import PartitionSpec as P


HEAD = 128
STRETCH = 768

rope_base = 500000.0
norm_epsilon = 1e-06
temper_floor = 8192
temper_slope = 0.1
masked_score = -1e30
log2e = 1.4426950408889634

IN_PLANE = ("row", "head")


def rope_tables(positions):
    half = HEAD // 2
    lane = lax.broadcasted_iota(jnp.int32, (1, HEAD), 1)
    index = jnp.where(lane < half, lane, lane - half).astype(jnp.float32)
    frequency = rope_base ** (-(index * 2.0 / HEAD))
    angles = positions.astype(jnp.float32)[:, None] * frequency
    sine = jnp.sin(angles)
    return jnp.cos(angles), jnp.where(lane < half, -sine, sine)


def rotated_unit(x, cosine, sine):
    y = x * cosine + pltpu.roll(x, HEAD // 2, 1) * sine
    return y * lax.rsqrt(jnp.mean(y * y, axis=-1, keepdims=True) + norm_epsilon)


def vmem_call(body, out_shapes, n_in, flops=0, nbytes=0, exps=0, scratch=(), smem=0):
    return pl.pallas_call(
        body,
        out_shape=out_shapes,
        in_specs=[pl.BlockSpec(memory_space=pltpu.SMEM)] * smem
        + [pl.BlockSpec(memory_space=pltpu.VMEM)] * n_in,
        out_specs=jax.tree.map(lambda _: pl.BlockSpec(memory_space=pltpu.VMEM), out_shapes),
        scratch_shapes=list(scratch),
        cost_estimate=pl.CostEstimate(flops=flops, bytes_accessed=nbytes, transcendentals=exps),
    )


def pack_body(kl_ref, vl_ref, kg_ref, vg_ref, o_ref):
    for d in range(o_ref.shape[0]):
        for a, ref in enumerate((kl_ref, vl_ref, kg_ref, vg_ref)):
            o_ref[d, a] = ref[:, d * HEAD : (d + 1) * HEAD]


def pack_query_body(ql_ref, qg_ref, cos_ref, sin_ref, turn_ref, temper_ref, o_ref):
    members = o_ref.shape[3] // HEAD
    cosine, sine = cos_ref[...], sin_ref[...]
    for d in range(o_ref.shape[0]):
        for g in range(members):
            at = (d * members + g) * HEAD
            x = ql_ref[:, at : at + HEAD]
            turned = jnp.dot(x, turn_ref[...], preferred_element_type=jnp.float32)
            y = x.astype(jnp.float32) * cosine + turned * sine
            y = y * lax.rsqrt(jnp.mean(y * y, axis=-1, keepdims=True) + norm_epsilon)
            to = slice(g * HEAD, (g + 1) * HEAD)
            o_ref[d, 0, :, to] = y.astype(o_ref.dtype)
            z = qg_ref[:, at : at + HEAD].astype(jnp.float32) * temper_ref[...]
            o_ref[d, 1, :, to] = z.astype(o_ref.dtype)


def causal(rows):
    r = lax.broadcasted_iota(jnp.int32, (rows, rows), 0)
    c = lax.broadcasted_iota(jnp.int32, (rows, rows), 1)
    return c <= r


NT = (((1,), (1,)), ((), ()))


def local_body(n_back, plane_ref, *refs):
    q_ref, qid_ref, kid_ref, cos_ref, sin_ref = refs[:5]
    blocks = refs[5 : 5 + n_back + 1]
    o_ref, k_ref, v_ref = refs[5 + n_back + 1 :]
    parts, _, tokens, width = q_ref.shape
    rows = parts * tokens
    members = width // HEAD
    scale = log2e * HEAD**-0.5
    for d in range(n_back + 1):
        keys = blocks[d][:, 0].reshape(rows, HEAD).astype(jnp.float32)
        k_ref[d] = rotated_unit(keys, cos_ref[d], sin_ref[d]).astype(k_ref.dtype)
        v_ref[d, :, :HEAD] = blocks[d][:, 1].reshape(rows, HEAD)
        v_ref[d, :, HEAD:] = jnp.ones((rows, HEAD), v_ref.dtype)
    qid = jnp.concatenate([qid_ref[...]] * (rows // HEAD), axis=1)

    def member(g, carry):
        at = pl.multiple_of(g * HEAD, HEAD)
        q = q_ref[:, 0, :, pl.ds(at, HEAD)].reshape(rows, HEAD)
        acc = None
        for d in range(n_back + 1):
            allowed = qid == kid_ref[d, :1, :]
            if d == 0:
                allowed = allowed & causal(rows)
            scores = lax.dot_general(q, k_ref[d], NT, preferred_element_type=jnp.float32)
            weights = jnp.where(allowed, jnp.exp2(scores * scale), 0.0).astype(jnp.bfloat16)
            part = jnp.dot(weights, v_ref[d], preferred_element_type=jnp.float32)
            acc = part if acc is None else acc + part
        out = (acc[:, :HEAD] / acc[:, HEAD:]).astype(o_ref.dtype)
        o_ref[:, :, pl.ds(at, HEAD)] = out.reshape(parts, tokens, HEAD)
        return carry

    lax.fori_loop(0, members, member, 0)


def global_body(distances, plane_ref, *refs):
    n = len(distances)
    q_ref = refs[0]
    blocks = refs[1 : 1 + n]
    o_ref, v_ref = refs[1 + n :]
    parts, _, tokens, width = q_ref.shape
    rows = parts * tokens
    members = width // HEAD
    plane = plane_ref[0]
    scale = log2e * HEAD**-0.5
    for i in range(n):
        v_ref[i, :, :HEAD] = blocks[i][:, blocks[i].shape[1] - 1].reshape(rows, HEAD)
        v_ref[i, :, HEAD:] = jnp.ones((rows, HEAD), v_ref.dtype)

    def member(g, carry):
        at = pl.multiple_of(g * HEAD, HEAD)
        q = q_ref[:, 1, :, pl.ds(at, HEAD)].reshape(rows, HEAD)
        peak, acc = None, None
        for first in range(0, n, 4):
            group = range(first, min(n, first + 4))
            every, new_peak = [], peak
            for i in group:
                keys = blocks[i][:, blocks[i].shape[1] - 2].reshape(rows, HEAD)
                scores = lax.dot_general(q, keys, NT, preferred_element_type=jnp.float32)
                if distances[i] == 0:
                    scores = jnp.where(causal(rows), scores, masked_score)
                every.append(scores)
                top = scores[:, :HEAD]
                for j in range(HEAD, rows, HEAD):
                    top = jnp.maximum(top, scores[:, j : j + HEAD])
                top = jnp.max(top, axis=1, keepdims=True) * scale
                if distances[i] > 0:
                    top = jnp.where(plane >= distances[i], top, masked_score)
                new_peak = top if new_peak is None else jnp.maximum(new_peak, top)
            if acc is not None:
                acc = acc * jnp.exp2(peak - new_peak)
            peak = new_peak
            for i, scores in zip(group, every):
                shift = peak
                if distances[i] > 0:
                    shift = jnp.where(plane >= distances[i], peak, -masked_score)
                weights = jnp.exp2(scores * scale - shift).astype(jnp.bfloat16)
                part = jnp.dot(weights, v_ref[i], preferred_element_type=jnp.float32)
                acc = part if acc is None else acc + part
        out = (acc[:, :HEAD] / acc[:, HEAD:]).astype(o_ref.dtype)
        o_ref[:, :, pl.ds(at, HEAD)] = out.reshape(parts, tokens, HEAD)
        return carry

    lax.fori_loop(0, members, member, 0)


def exchange(x):
    return lax.all_to_all(x, IN_PLANE, split_axis=0, concat_axis=0, tiled=True)


def upward(x, by):
    size = lax.axis_size("plane")
    return lax.ppermute(x, "plane", [(i, i + by) for i in range(size - by)])


def unpack(x):
    parts, tokens, width = x.shape
    return x.transpose(1, 0, 2).reshape(tokens, parts * width)


def shards(query_local, key_local, value_local, labels, query_global, key_global, value_global):
    planes = lax.axis_size("plane")
    plane = lax.axis_index("plane")
    parts = lax.axis_size("row") * lax.axis_size("head")
    spot = lax.axis_index("row") * lax.axis_size("head") + lax.axis_index("head")
    tokens = query_local.shape[0]
    width = query_local.shape[1] // parts
    members = width // HEAD
    rows = parts * tokens
    dtype = query_local.dtype
    local_back = min(planes - 1, -(-(STRETCH - 1) // rows))

    packed = jax.ShapeDtypeStruct((parts, 4, tokens, HEAD), dtype)
    pack = vmem_call(pack_body, packed, 4, nbytes=16 * key_local.size)
    pack = pack(key_local, value_local, key_global, value_global)
    own = exchange(pack)
    local_blocks, global_blocks = [own], [own]
    for d in range(1, planes):
        if d == 1:
            came = upward(own, 1)
            local_blocks.append(came)
            global_blocks.append(came)
        elif d == 2:
            if d <= local_back:
                local_blocks.append(upward(came[:, :2], 1))
            global_blocks.append(upward(came[:, 2:], 1))
        else:
            if d <= local_back:
                local_blocks.append(upward(local_blocks[d - 3][:, :2], 3))
            source = global_blocks[d - 3]
            global_blocks.append(upward(source[:, source.shape[1] - 2 :], 3))

    own_pos = (plane * parts + spot) * tokens + jnp.arange(tokens, dtype=jnp.int32)
    cosine, sine = rope_tables(own_pos)
    half = HEAD // 2
    i, j = lax.broadcasted_iota(jnp.int32, (HEAD, HEAD), 0), lax.broadcasted_iota(jnp.int32, (HEAD, HEAD), 1)
    turn = jnp.where((i + half) % HEAD == j, 1.0, 0.0).astype(dtype)
    temper = 1.0 + temper_slope * jnp.log(((own_pos + 1) // temper_floor + 1).astype(jnp.float32))
    temper = jnp.broadcast_to(temper[:, None], (tokens, HEAD))
    packed = jax.ShapeDtypeStruct((parts, 2, tokens, width), dtype)
    pack = vmem_call(pack_query_body, packed, 6, nbytes=8 * query_local.size, flops=2 * HEAD * query_local.size)
    pack = pack(query_local, query_global, cosine, sine, turn, temper)
    queries = exchange(pack)

    plane_arg = plane.reshape(1).astype(jnp.int32)
    back = jnp.arange(local_back + 1, dtype=jnp.int32)
    key_pos = ((plane - back)[:, None] * rows + jnp.arange(rows, dtype=jnp.int32)[None, :]).reshape(-1)
    k_cos, k_sin = rope_tables(key_pos)
    k_cos = k_cos.reshape(local_back + 1, rows, HEAD)
    k_sin = k_sin.reshape(local_back + 1, rows, HEAD)
    row_ids = lax.dynamic_slice_in_dim(labels, plane * rows, rows, 0)
    q_ids = jnp.broadcast_to(row_ids[:, None], (rows, HEAD))
    key_ids = []
    for d in range(local_back + 1):
        ids = lax.dynamic_slice_in_dim(labels, jnp.maximum(plane - d, 0) * rows, rows, 0)
        key_ids.append(jnp.where(plane >= d, ids, -1))
    key_ids = jnp.broadcast_to(jnp.stack(key_ids)[:, None, :], (local_back + 1, 8, rows))

    out_shape = jax.ShapeDtypeStruct((parts, tokens, width), dtype)
    pair_flops = 2 * 3 * rows * rows * HEAD * members
    local_out = vmem_call(
        functools.partial(local_body, local_back),
        out_shape,
        5 + local_back + 1,
        flops=pair_flops * (local_back + 1),
        nbytes=4 * rows * width * 2,
        exps=rows * rows * members * (local_back + 1),
        scratch=[
            pltpu.VMEM((local_back + 1, rows, HEAD), jnp.bfloat16),
            pltpu.VMEM((local_back + 1, rows, 2 * HEAD), jnp.bfloat16),
        ],
        smem=1,
    )(plane_arg, queries, q_ids, key_ids, k_cos, k_sin, *local_blocks)
    local_heads = exchange(local_out)
    global_out = vmem_call(
        functools.partial(global_body, tuple(range(planes))),
        out_shape,
        1 + planes,
        flops=pair_flops * planes,
        nbytes=4 * rows * width * 2,
        exps=rows * rows * members * planes,
        scratch=[pltpu.VMEM((planes, rows, 2 * HEAD), jnp.bfloat16)],
        smem=1,
    )(plane_arg, queries, *global_blocks)
    global_heads = exchange(global_out)
    return unpack(local_heads), unpack(global_heads)


def solution(mesh):
    ctx, head = mesh.shape["ctx"], mesh.shape["head"]

    def run(*args):
        key_heads = args[1].shape[1] // HEAD
        row = max(1, key_heads // head)
        grid = Mesh(mesh.devices.reshape(ctx // row, row, head), ("plane", "row", "head"))
        spread = P(("plane", "row", "head"), None)
        return jax.shard_map(
            shards,
            mesh=grid,
            in_specs=(spread, spread, spread, P(), spread, spread, spread),
            out_specs=(spread, spread),
            check_vma=False,
        )(*args)

    return run
```

time: 120 us -> 94.7 us (0.79)
  the two profiles are of different devices: /device:TPU:28 before, /device:TPU:0 now
where the time goes in v2:
time: 94.7 us; the launch traced here: 94.1 us
  starting transfers between devices  31.9 us (34%)
  waiting for transfers between devices  28.6 us (30%)
  Pallas kernels  22.5 us (24%)
  local copies, waits for them, and re-layouts  5.23 us (6%)
  other arithmetic  5.1 us (5%)
    ppermute x4, waiting for transfers between devices, upward(): return lax.ppermute(x, 'plane', [(i, i + by) for i in range(size - by)])  17 us
    all_to_all x4, starting transfers between devices, exchange(): return lax.all_to_all(x, IN_PLANE, split_axis=0, concat_axis=0, tiled=True)  16.3 us
    ppermute x4, starting transfers between devices, upward(): return lax.ppermute(x, 'plane', [(i, i + by) for i in range(size - by)])  15.6 us
    all_to_all x4, waiting for transfers between devices, exchange(): return lax.all_to_all(x, IN_PLANE, split_axis=0, concat_axis=0, tiled=True)  11.6 us
    pallas_call x1, Pallas kernels, shards(): vmem_call(functools.partial(global_body, tuple(range(planes))), out_shape...  10.1 us
    pallas_call x1, Pallas kernels, shards(): vmem_call(functools.partial(local_body, local_back), out_shape, 5 + local...  7.73 us
    select_n x2, other arithmetic, rope_tables(): return (jnp.cos(angles), jnp.where(lane < half, -sine, sine))  4.14 us
    pallas_call x1, Pallas kernels, shards(): pack = pack(query_local, query_global, cosine, sine, turn, temper)  2.83 us
  transfers between devices with their start and end apart: 8, of which 6 were waited for; matrix products, arithmetic and copies ran while one was open for 7% of the time, Pallas kernels for 14%

profile of v2, /device:TPU:0, one launch (start us, length us, event | category | flops | bytes accessed | tf_op | source)
XLA Modules:
  0.0 94.1 jit_solution(12371215733549315198)
XLA Ops:
  0.6 1.9 %shard_map.87 = bf16[8,4,48,128]{3,2,1,0:T(8,128)(2,1)} custom-call(bf16[48,1024]{1,0:T(8,128)(2,1)} %kl_ref.1, bf16[48,1024]{1,0:T(8,128)(2,1)} %vl_ref.1, bf16[48,1024]{1,0:T(8,128)(2,1)} %kg_ref.1, bf16[48,1024]{1,0:T(8,128)(2,1)} %vg_ref.1), custom_call_target="tpu_custom_call" | custom-call | bytes 786432 | tf_op jit(solution)/shard_map/pallas_call | solution.py:196
  2.5 5.2 %all-to-all-start.1 = ((bf16[8,4,48,128]{3,2,1,0:T(8,128)(2,1)}), bf16[8,4,48,128]{3,2,1,0:T(8,128)(2,1)S(1)}, u32[]{:S(2)}, u32[]{:S(2)}) async-start(bf16[8,4,48,128]{3,2,1,0:T(8,128)(2,1)} %shard_map.87), calls=%async_computation.1 | async-start | bytes 786432 | tf_op jit(solution)/shard_map/all_to_all | solution.py:169
  7.8 0.7 select_convert_fusion.turn_ref
  8.5 0.8 negate_select_fusion.1
  9.3 0.7 broadcast_in_dim.55.temper_ref
  10.0 0.0 copy-start.4
  10.0 2.8 %shard_map.86 = bf16[8,2,48,640]{3,2,1,0:T(8,128)(2,1)} custom-call(bf16[48,5120]{1,0:T(8,128)(2,1)} %ql_ref.1, bf16[48,5120]{1,0:T(8,128)(2,1)} %qg_ref.1, f32[48,128]{1,0:T(8,128)} %get-tuple-element.11.cos_ref, f32[48,128]{1,0:T(8,128)} %get-tuple-element.10.sin_ref, bf16[128,128]{1,0:T(8,128)(2,1)} %select_convert_fusion.turn_ref, ...), custom_call_target="tpu_custom_call" | custom-call | flops 62914560 | bytes 1966080 | tf_op jit(solution)/shard_map/pallas_call | solution.py:223
  12.8 0.0 copy-done.4
  12.8 0.1 dynamic-slice_select_fusion.2
  12.9 3.1 %all-to-all-done.1.refs_5_.refs_1_ = bf16[8,4,48,128]{3,2,1,0:T(8,128)(2,1)S(1)} async-done(((bf16[8,4,48,128]{3,2,1,0:T(8,128)(2,1)}), bf16[8,4,48,128]{3,2,1,0:T(8,128)(2,1)S(1)}, u32[]{:S(2)}, u32[]{:S(2)}) %all-to-all-start.1) | async-done | bytes 393248 | tf_op jit(solution)/shard_map/all_to_all | solution.py:169
  16.0 0.0 copy-start.1
  16.0 3.6 %all-to-all-start = ((bf16[8,2,48,640]{3,2,1,0:T(8,128)(2,1)}), bf16[8,2,48,640]{3,2,1,0:T(8,128)(2,1)S(1)}, u32[]{:S(2)}, u32[]{:S(2)}) async-start(bf16[8,2,48,640]{3,2,1,0:T(8,128)(2,1)} %shard_map.86), calls=%async_computation | async-start | bytes 1966080 | tf_op jit(solution)/shard_map/all_to_all | solution.py:169
  19.6 0.0 copy-done.1
  19.6 3.5 %collective-permute-start = (bf16[8,4,48,128]{3,2,1,0:T(8,128)(2,1)S(1)}, bf16[8,4,48,128]{3,2,1,0:T(8,128)(2,1)S(1)}, u32[]{:S(2)}, u32[]{:S(2)}) collective-permute-start(bf16[8,4,48,128]{3,2,1,0:T(8,128)(2,1)S(1)} %all-to-all-done.1.refs_5_.refs_1_), channel_id=1, source_target_pairs={{0,8},{8,16},{16,24},{1,9},{9,17},{17,25},{2,10},{10,18},{18,26},{... | collective-permute-start | bytes 1179656 | tf_op jit(solution)/shard_map/ppermute | solution.py:174
  23.1 0.1 add_convert_fusion
  23.2 8.7 %collective-permute-done.refs_6_.refs_2_ = bf16[8,4,48,128]{3,2,1,0:T(8,128)(2,1)S(1)} collective-permute-done((bf16[8,4,48,128]{3,2,1,0:T(8,128)(2,1)S(1)}, bf16[8,4,48,128]{3,2,1,0:T(8,128)(2,1)S(1)}, u32[]{:S(2)}, u32[]{:S(2)}) %collective-permute-start) | collective-permute-done | bytes 393248 | tf_op jit(solution)/shard_map/ppermute | solution.py:174
  32.0 0.0 copy-start.3
  32.0 0.7 copy-done.3
  32.7 4.4 %collective-permute-start.1 = (bf16[8,2,48,128]{3,2,1,0:T(8,128)(2,1)S(1)}, bf16[8,2,48,128]{3,2,1,0:T(8,128)(2,1)S(1)}, u32[]{:S(2)}, u32[]{:S(2)}) collective-permute-start(bf16[8,2,48,128]{3,2,1,0:T(8,128)(2,1)S(1)} %get-tuple-element.3), channel_id=1, source_target_pairs={{0,8},{8,16},{16,24},{1,9},{9,17},{17,25},{2,10},{10,18},{18,26},{... | collective-permute-start | bytes 589832 | tf_op jit(solution)/shard_map/ppermute | solution.py:174
  37.1 3.3 %negate_select_fusion = (f32[3,384,128]{2,1,0:T(8,128)}, f32[3,384,128]{2,1,0:T(8,128)}) fusion(f32[128]{0:T(128)S(1)} %fusion.3, f32[3,384]{1,0:T(4,128)S(1)} %add_convert_fusion, pred[128]{0:T(512)(128)(4,1)S(1)} %iota_compare_fusion.1), kind=kLoop, calls=%fused_computation | loop fusion | flops 442368 | bytes 1184896 | tf_op jit(solution)/shard_map/jit(_where)/select_n | solution.py:32
  40.4 0.0 all-to-all-done.refs_0_
  40.4 0.0 copy-start
  40.4 0.5 collective-permute-done.1.refs_7_
  40.9 0.0 copy-start.5
  40.9 0.8 broadcast_in_dim.56.refs_1_
  41.7 0.6 broadcast_in_dim.58.refs_2_
  42.4 0.0 copy-done
  42.4 0.0 copy-done.5
  42.4 7.7 %shard_map.88 = bf16[8,48,640]{2,1,0:T(8,128)(2,1)} custom-call(s32[1]{0:T(128)} %bitcast.plane_ref, bf16[8,2,48,640]{3,2,1,0:T(8,128)(2,1)} %copy-done, s32[384,128]{1,0:T(8,128)} %broadcast_in_dim.56.refs_1_, s32[3,8,384]{2,1,0:T(8,128)} %broadcast_in_dim.58.refs_2_, f32[3,384,128]{2,1,0:T(8,128)} %get-tuple-element.9.refs_3_, ...), custom_call_target="tpu_custom_call" | custom-call | flops 1698693120 | bytes 1966080 | tf_op jit(solution)/shard_map/pallas_call | solution.py:242
  50.1 0.0 copy-start.2
  50.1 3.8 %all-to-all-start.2 = ((bf16[8,48,640]{2,1,0:T(8,128)(2,1)}), bf16[8,48,640]{2,1,0:T(8,128)(2,1)S(1)}, u32[]{:S(2)}, u32[]{:S(2)}) async-start(bf16[8,48,640]{2,1,0:T(8,128)(2,1)} %shard_map.88), calls=%async_computation.2 | async-start | bytes 983040 | tf_op jit(solution)/shard_map/all_to_all | solution.py:169
  53.9 0.0 copy-done.2
  53.9 6.4 %collective-permute-start.3 = (bf16[8,2,48,128]{3,2,1,0:T(8,128)(2,1)S(1)}, bf16[8,2,48,128]{3,2,1,0:T(8,128)(2,1)S(1)}, u32[]{:S(2)}, u32[]{:S(2)}) collective-permute-start(bf16[8,2,48,128]{3,2,1,0:T(8,128)(2,1)S(1)} %slice.14), channel_id=1, source_target_pairs={{0,24},{1,25},{2,26},{3,27},{4,28},{5,29},{6,30},{7,31}} | collective-permute-start | bytes 589832 | tf_op jit(solution)/shard_map/ppermute | solution.py:174
  60.3 1.3 %collective-permute-start.2 = (bf16[8,2,48,128]{3,2,1,0:T(8,128)(2,1)S(1)}, bf16[8,2,48,128]{3,2,1,0:T(8,128)(2,1)S(1)}, u32[]{:S(2)}, u32[]{:S(2)}) collective-permute-start(bf16[8,2,48,128]{3,2,1,0:T(8,128)(2,1)S(1)} %get-tuple-element.2), channel_id=1, source_target_pairs={{0,8},{8,16},{16,24},{1,9},{9,17},{17,25},{2,10},{10,18},{18,26},{... | collective-permute-start | bytes 589832 | tf_op jit(solution)/shard_map/ppermute | solution.py:174
  61.6 4.0 %collective-permute-done.3.refs_4_ = bf16[8,2,48,128]{3,2,1,0:T(8,128)(2,1)S(1)} collective-permute-done((bf16[8,2,48,128]{3,2,1,0:T(8,128)(2,1)S(1)}, bf16[8,2,48,128]{3,2,1,0:T(8,128)(2,1)S(1)}, u32[]{:S(2)}, u32[]{:S(2)}) %collective-permute-start.3) | collective-permute-done | bytes 196640 | tf_op jit(solution)/shard_map/ppermute | solution.py:174
  65.6 0.0 copy-start.6
  65.6 3.7 %collective-permute-done.2.refs_3_ = bf16[8,2,48,128]{3,2,1,0:T(8,128)(2,1)S(1)} collective-permute-done((bf16[8,2,48,128]{3,2,1,0:T(8,128)(2,1)S(1)}, bf16[8,2,48,128]{3,2,1,0:T(8,128)(2,1)S(1)}, u32[]{:S(2)}, u32[]{:S(2)}) %collective-permute-start.2) | collective-permute-done | bytes 196640 | tf_op jit(solution)/shard_map/ppermute | solution.py:174
  69.3 0.0 copy-done.6
  69.3 0.0 copy-start.7
  69.3 0.7 copy-done.7
  70.0 10.1 %shard_map.89 = bf16[8,48,640]{2,1,0:T(8,128)(2,1)} custom-call(s32[1]{0:T(128)} %bitcast.plane_ref, bf16[8,2,48,640]{3,2,1,0:T(8,128)(2,1)} %copy-done, bf16[8,4,48,128]{3,2,1,0:T(8,128)(2,1)} %copy-done.1, bf16[8,4,48,128]{3,2,1,0:T(8,128)(2,1)} %copy-done.3, bf16[8,2,48,128]{3,2,1,0:T(8,128)(2,1)} %copy-done.7, bf16[8,2,48,128]{3,2,1,0:T(8,128)(2,1)} %copy-done.6), custom_call_target="tpu_custom_call" | custom-call | flops 2264924160 | bytes 1966080 | tf_op jit(solution)/shard_map/pallas_call | solution.py:256
  80.1 0.0 all-to-all-done.2
  80.1 3.8 %all-to-all-start.3 = ((bf16[8,48,640]{2,1,0:T(8,128)(2,1)}), bf16[8,48,640]{2,1,0:T(8,128)(2,1)S(1)}, u32[]{:S(2)}, u32[]{:S(2)}) async-start(bf16[8,48,640]{2,1,0:T(8,128)(2,1)} %shard_map.89), calls=%async_computation.3 | async-start | bytes 983040 | tf_op jit(solution)/shard_map/all_to_all | solution.py:169
  83.9 0.8 copy.11
  84.7 8.5 %all-to-all-done.3 = bf16[8,48,640]{2,1,0:T(8,128)(2,1)S(1)} async-done(((bf16[8,48,640]{2,1,0:T(8,128)(2,1)}), bf16[8,48,640]{2,1,0:T(8,128)(2,1)S(1)}, u32[]{:S(2)}, u32[]{:S(2)}) %all-to-all-start.3) | async-done | bytes 491552 | tf_op jit(solution)/shard_map/all_to_all | solution.py:169
  93.3 0.8 copy.12
  (13 shorter events, 0.1 us)
Async XLA Ops:
  2.5 13.5 %all-to-all-start.1 = ((bf16[8,4,48,128]{3,2,1,0:T(8,128)(2,1)}), bf16[8,4,48,128]{3,2,1,0:T(8,128)(2,1)S(1)}, u32[]{:S(2)}, u32[]{:S(2)}) async-start(bf16[8,4,48,128]{3,2,1,0:T(8,128)(2,1)} %shard_map.87), calls=%async_computation.1 | async-start | bytes 786432 | tf_op jit(solution)/shard_map/all_to_all | solution.py:169
  10.0 2.8 %copy-start.4 = (s32[1536]{0:T(1024)S(1)}, s32[1536]{0:T(1024)}, u32[]{:S(2)}) copy-start(s32[1536]{0:T(1024)} %param.10) | copy-start | bytes 18436
  16.0 3.6 %copy-start.1 = (bf16[8,4,48,128]{3,2,1,0:T(8,128)(2,1)}, bf16[8,4,48,128]{3,2,1,0:T(8,128)(2,1)S(1)}, u32[]{:S(2)}) copy-start(bf16[8,4,48,128]{3,2,1,0:T(8,128)(2,1)S(1)} %all-to-all-done.1.refs_5_.refs_1_) | copy-start | bytes 1179652
  16.0 24.4 %all-to-all-start = ((bf16[8,2,48,640]{3,2,1,0:T(8,128)(2,1)}), bf16[8,2,48,640]{3,2,1,0:T(8,128)(2,1)S(1)}, u32[]{:S(2)}, u32[]{:S(2)}) async-start(bf16[8,2,48,640]{3,2,1,0:T(8,128)(2,1)} %shard_map.86), calls=%async_computation | async-start | bytes 1966080 | tf_op jit(solution)/shard_map/all_to_all | solution.py:169
  19.6 12.4 %collective-permute-start = (bf16[8,4,48,128]{3,2,1,0:T(8,128)(2,1)S(1)}, bf16[8,4,48,128]{3,2,1,0:T(8,128)(2,1)S(1)}, u32[]{:S(2)}, u32[]{:S(2)}) collective-permute-start(bf16[8,4,48,128]{3,2,1,0:T(8,128)(2,1)S(1)} %all-to-all-done.1.refs_5_.refs_1_), channel_id=1, source_target_pairs={{0,8},{8,16},{16,24},{1,9},{9,17},{17,25},{2,10},{10,18},{18,26},{... | collective-permute-start | bytes 1179656 | tf_op jit(solution)/shard_map/ppermute | solution.py:174
  32.0 0.7 copy-start.3
  32.7 8.2 %collective-permute-start.1 = (bf16[8,2,48,128]{3,2,1,0:T(8,128)(2,1)S(1)}, bf16[8,2,48,128]{3,2,1,0:T(8,128)(2,1)S(1)}, u32[]{:S(2)}, u32[]{:S(2)}) collective-permute-start(bf16[8,2,48,128]{3,2,1,0:T(8,128)(2,1)S(1)} %get-tuple-element.3), channel_id=1, source_target_pairs={{0,8},{8,16},{16,24},{1,9},{9,17},{17,25},{2,10},{10,18},{18,26},{... | collective-permute-start | bytes 589832 | tf_op jit(solution)/shard_map/ppermute | solution.py:174
  40.4 1.9 %copy-start = (bf16[8,2,48,640]{3,2,1,0:T(8,128)(2,1)}, bf16[8,2,48,640]{3,2,1,0:T(8,128)(2,1)S(1)}, u32[]{:S(2)}) copy-start(bf16[8,2,48,640]{3,2,1,0:T(8,128)(2,1)S(1)} %all-to-all-done.refs_0_) | copy-start | bytes 2949124
  40.9 1.4 %copy-start.5 = (bf16[8,2,48,128]{3,2,1,0:T(8,128)(2,1)}, bf16[8,2,48,128]{3,2,1,0:T(8,128)(2,1)S(1)}, u32[]{:S(2)}) copy-start(bf16[8,2,48,128]{3,2,1,0:T(8,128)(2,1)S(1)} %collective-permute-done.1.refs_7_) | copy-start | bytes 589828
  50.1 3.8 %copy-start.2 = (bf16[8,4,48,128]{3,2,1,0:T(8,128)(2,1)S(1)}, bf16[8,4,48,128]{3,2,1,0:T(8,128)(2,1)}, u32[]{:S(2)}) copy-start(bf16[8,4,48,128]{3,2,1,0:T(8,128)(2,1)} %copy-done.1) | copy-start | bytes 1179652
  50.1 30.0 %all-to-all-start.2 = ((bf16[8,48,640]{2,1,0:T(8,128)(2,1)}), bf16[8,48,640]{2,1,0:T(8,128)(2,1)S(1)}, u32[]{:S(2)}, u32[]{:S(2)}) async-start(bf16[8,48,640]{2,1,0:T(8,128)(2,1)} %shard_map.88), calls=%async_computation.2 | async-start | bytes 983040 | tf_op jit(solution)/shard_map/all_to_all | solution.py:169
  53.9 11.7 %collective-permute-start.3 = (bf16[8,2,48,128]{3,2,1,0:T(8,128)(2,1)S(1)}, bf16[8,2,48,128]{3,2,1,0:T(8,128)(2,1)S(1)}, u32[]{:S(2)}, u32[]{:S(2)}) collective-permute-start(bf16[8,2,48,128]{3,2,1,0:T(8,128)(2,1)S(1)} %slice.14), channel_id=1, source_target_pairs={{0,24},{1,25},{2,26},{3,27},{4,28},{5,29},{6,30},{7,31}} | collective-permute-start | bytes 589832 | tf_op jit(solution)/shard_map/ppermute | solution.py:174
  60.3 9.1 %collective-permute-start.2 = (bf16[8,2,48,128]{3,2,1,0:T(8,128)(2,1)S(1)}, bf16[8,2,48,128]{3,2,1,0:T(8,128)(2,1)S(1)}, u32[]{:S(2)}, u32[]{:S(2)}) collective-permute-start(bf16[8,2,48,128]{3,2,1,0:T(8,128)(2,1)S(1)} %get-tuple-element.2), channel_id=1, source_target_pairs={{0,8},{8,16},{16,24},{1,9},{9,17},{17,25},{2,10},{10,18},{18,26},{... | collective-permute-start | bytes 589832 | tf_op jit(solution)/shard_map/ppermute | solution.py:174
  65.6 3.7 %copy-start.6 = (bf16[8,2,48,128]{3,2,1,0:T(8,128)(2,1)}, bf16[8,2,48,128]{3,2,1,0:T(8,128)(2,1)S(1)}, u32[]{:S(2)}) copy-start(bf16[8,2,48,128]{3,2,1,0:T(8,128)(2,1)S(1)} %collective-permute-done.3.refs_4_) | copy-start | bytes 589828
  69.3 0.7 copy-start.7
  80.1 13.2 %all-to-all-start.3 = ((bf16[8,48,640]{2,1,0:T(8,128)(2,1)}), bf16[8,48,640]{2,1,0:T(8,128)(2,1)S(1)}, u32[]{:S(2)}, u32[]{:S(2)}) async-start(bf16[8,48,640]{2,1,0:T(8,128)(2,1)} %shard_map.89), calls=%async_computation.3 | async-start | bytes 983040 | tf_op jit(solution)/shard_map/all_to_all | solution.py:169

commit v3 on v2

v3 whole, which is shorter than its diff:
```python
import functools

import jax
import jax.numpy as jnp
import numpy as np
from jax import lax
from jax.experimental import pallas as pl
from jax.experimental.pallas import tpu as pltpu
from jax.sharding import Mesh
from jax.sharding import PartitionSpec as P


HEAD = 128
STRETCH = 768

rope_base = 500000.0
norm_epsilon = 1e-06
temper_floor = 8192
temper_slope = 0.1
masked_score = -1e30
log2e = 1.4426950408889634
far = 30000.0

IN_PLANE = ("row", "head")


def rope_tables(count, step):
    half = HEAD // 2
    frequency = rope_base ** (-(np.arange(HEAD) % half) * 2.0 / HEAD)
    angles = (np.arange(count) * step)[:, None] * frequency[None, :]
    sign = np.where(np.arange(HEAD) < half, -1.0, 1.0)
    return jnp.asarray(np.cos(angles), jnp.float32), jnp.asarray(np.sin(angles) * sign, jnp.float32)


def turned(cos_base, sin_base, cos_row, sin_row):
    return cos_base * cos_row - sin_base * sin_row, sin_base * cos_row + cos_base * sin_row


def rotated_unit(x, turn, cosine, sine):
    swapped = jnp.dot(x, turn, preferred_element_type=jnp.float32)
    y = x.astype(jnp.float32) * cosine + swapped * sine
    return y * lax.rsqrt(jnp.mean(y * y, axis=-1, keepdims=True) + norm_epsilon)


def vmem_call(body, out_shapes, n_in, flops=0, nbytes=0, exps=0, scratch=(), smem=0):
    return pl.pallas_call(
        body,
        out_shape=out_shapes,
        in_specs=[pl.BlockSpec(memory_space=pltpu.SMEM)] * smem
        + [pl.BlockSpec(memory_space=pltpu.VMEM)] * n_in,
        out_specs=jax.tree.map(lambda _: pl.BlockSpec(memory_space=pltpu.VMEM), out_shapes),
        scratch_shapes=list(scratch),
        cost_estimate=pl.CostEstimate(flops=flops, bytes_accessed=nbytes, transcendentals=exps),
    )


def pack_body(kl_ref, vl_ref, kg_ref, vg_ref, o_ref):
    for d in range(o_ref.shape[0]):
        for a, ref in enumerate((kl_ref, vl_ref, kg_ref, vg_ref)):
            o_ref[d, a] = ref[:, d * HEAD : (d + 1) * HEAD]


def pack_query_body(where_ref, ql_ref, qg_ref, cosb_ref, sinb_ref, cosr_ref, sinr_ref, turn_ref, temper_ref, o_ref):
    members = o_ref.shape[3] // HEAD
    tokens = ql_ref.shape[0]
    plane, first = where_ref[0], pl.multiple_of(where_ref[1], 16)
    mine = pl.ds(first, tokens)
    cosine, sine = turned(cosb_ref[pl.ds(plane, 1)], sinb_ref[pl.ds(plane, 1)], cosr_ref[mine], sinr_ref[mine])
    turn = turn_ref[...]
    for d in range(o_ref.shape[0]):
        for g in range(members):
            at = (d * members + g) * HEAD
            to = slice(g * HEAD, (g + 1) * HEAD)
            y = rotated_unit(ql_ref[:, at : at + HEAD], turn, cosine, sine)
            o_ref[d, 0, :, to] = y.astype(o_ref.dtype)
            z = qg_ref[:, at : at + HEAD].astype(jnp.float32) * temper_ref[...]
            o_ref[d, 1, :, to] = z.astype(o_ref.dtype)


def causal(rows):
    r = lax.broadcasted_iota(jnp.int32, (rows, rows), 0)
    c = lax.broadcasted_iota(jnp.int32, (rows, rows), 1)
    return c <= r


NT = (((1,), (1,)), ((), ()))


def take_values(v_ref, i, values, valid):
    rows = values.shape[0]
    v_ref[i * rows : (i + 1) * rows, :HEAD] = values
    ones = jnp.broadcast_to(jnp.where(valid, 1.0, 0.0), (rows, HEAD))
    v_ref[i * rows : (i + 1) * rows, HEAD:] = ones.astype(v_ref.dtype)


def divided(acc, dtype):
    return (acc[:, :HEAD] / acc[:, HEAD:]).astype(dtype)


def local_body(n_back, where_ref, *refs):
    q_ref, labels_ref, cosb_ref, sinb_ref, cosr_ref, sinr_ref, turn_ref = refs[:7]
    blocks = refs[7 : 7 + n_back + 1]
    o_ref, k_ref, v_ref = refs[7 + n_back + 1 :]
    parts, _, tokens, width = q_ref.shape
    rows = parts * tokens
    members = width // HEAD
    plane = where_ref[0]
    scale = log2e * HEAD**-0.5
    turn = turn_ref[...]
    lane = lax.broadcasted_iota(jnp.int32, (HEAD, rows), 0)
    for d in range(n_back + 1):
        behind = jnp.maximum(plane - d, 0)
        base = pl.ds(behind, 1)
        cosine, sine = turned(cosb_ref[base], sinb_ref[base], cosr_ref[...], sinr_ref[...])
        at = slice(d * rows, (d + 1) * rows)
        keys = blocks[d][:, 0].reshape(rows, HEAD)
        k_ref[at, :HEAD] = rotated_unit(keys, turn, cosine, sine).astype(k_ref.dtype)
        ids = labels_ref[:, pl.ds(pl.multiple_of(behind * rows, HEAD), rows)]
        same = jnp.where(lane == ids, 1.0, 0.0).T
        k_ref[at, HEAD:] = same.astype(k_ref.dtype)
        if d == 0:
            other = ((same - 1.0) * far).astype(k_ref.dtype)
        take_values(v_ref, d, blocks[d][:, 1].reshape(rows, HEAD), plane >= d)

    def member(g, carry):
        at = pl.multiple_of(g * HEAD, HEAD)
        q = jnp.concatenate([q_ref[:, 0, :, pl.ds(at, HEAD)].reshape(rows, HEAD), other], axis=1)
        scores = lax.dot_general(q, k_ref[...], NT, preferred_element_type=jnp.float32)
        weights = jnp.exp2(scores * scale)
        first = jnp.where(causal(rows), weights[:, :rows], 0.0)
        weights = jnp.concatenate([first, weights[:, rows:]], axis=1).astype(jnp.bfloat16)
        acc = jnp.dot(weights, v_ref[...], preferred_element_type=jnp.float32)
        o_ref[:, :, pl.ds(at, HEAD)] = divided(acc, o_ref.dtype).reshape(parts, tokens, HEAD)
        return carry

    lax.fori_loop(0, members, member, 0, unroll=True)


def global_body(n, where_ref, *refs):
    q_ref = refs[0]
    blocks = refs[1 : 1 + n]
    o_ref, k_ref, v_ref = refs[1 + n :]
    parts, _, tokens, width = q_ref.shape
    rows = parts * tokens
    members = width // HEAD
    plane = where_ref[0]
    scale = log2e * HEAD**-0.5
    groups = [(i, min(n, i + 4)) for i in range(0, n, 4)]
    for i in range(n):
        last = blocks[i].shape[1] - 1
        k_ref[i * rows : (i + 1) * rows] = blocks[i][:, last - 1].reshape(rows, HEAD)
        take_values(v_ref, i, blocks[i][:, last].reshape(rows, HEAD), plane >= i)

    def query(g):
        at = pl.multiple_of(g * HEAD, HEAD)
        return q_ref[:, 1, :, pl.ds(at, HEAD)].reshape(rows, HEAD)

    def put(g, acc):
        at = pl.multiple_of(g * HEAD, HEAD)
        o_ref[:, :, pl.ds(at, HEAD)] = divided(acc, o_ref.dtype).reshape(parts, tokens, HEAD)

    def scored(q, group):
        keys = k_ref[group[0] * rows : group[1] * rows]
        return lax.dot_general(q, keys, NT, preferred_element_type=jnp.float32) * scale

    def summed(weights, group):
        if group[0] == 0:
            first = jnp.where(causal(rows), weights[:, :rows], 0.0)
            weights = jnp.concatenate([first, weights[:, rows:]], axis=1)
        values = v_ref[group[0] * rows : group[1] * rows]
        return jnp.dot(weights.astype(jnp.bfloat16), values, preferred_element_type=jnp.float32)

    def plain(g, carry):
        low, high = carry
        q = query(g)
        acc = summed(jnp.exp2(scored(q, groups[0])), groups[0])
        for group in groups[1:]:
            acc = acc + summed(jnp.exp2(scored(q, group)), group)
        put(g, acc)
        totals = acc[:, HEAD:]
        low = jnp.minimum(low, jnp.min(totals, axis=0, keepdims=True))
        high = jnp.maximum(high, jnp.max(totals, axis=0, keepdims=True))
        return low, high

    ones = jnp.ones((1, HEAD), jnp.float32)
    low, high = lax.fori_loop(0, members, plain, (ones, ones), unroll=len(groups) == 1)
    safe = (jnp.min(low) > 2.0**-80) & (jnp.max(high) < 2.0**100)

    @pl.when(jnp.logical_not(safe))
    def _():
        def shifted(g, carry):
            q = query(g)
            peak, acc = None, None
            for group in groups:
                scores = scored(q, group)
                parts_of = []
                for i in range(group[0], group[1]):
                    part = scores[:, (i - group[0]) * rows : (i - group[0] + 1) * rows]
                    if i == 0:
                        part = jnp.where(causal(rows), part, masked_score)
                    else:
                        part = jnp.where(plane >= i, part, masked_score)
                    parts_of.append(part)
                scores = jnp.concatenate(parts_of, axis=1)
                top = jnp.max(scores, axis=1, keepdims=True)
                new_peak = top if peak is None else jnp.maximum(peak, top)
                if acc is not None:
                    acc = acc * jnp.exp2(peak - new_peak)
                peak = new_peak
                part = summed(jnp.exp2(scores - peak), group)
                acc = part if acc is None else acc + part
            put(g, acc)
            return carry

        lax.fori_loop(0, members, shifted, 0)


def exchange(x):
    return lax.all_to_all(x, IN_PLANE, split_axis=0, concat_axis=0, tiled=True)


def upward(x, by):
    size = lax.axis_size("plane")
    return lax.ppermute(x, "plane", [(i, i + by) for i in range(size - by)])


def unpack(x):
    parts, tokens, width = x.shape
    return x.transpose(1, 0, 2).reshape(tokens, parts * width)


def shards(query_local, key_local, value_local, labels, query_global, key_global, value_global):
    planes = lax.axis_size("plane")
    plane = lax.axis_index("plane")
    parts = lax.axis_size("row") * lax.axis_size("head")
    spot = lax.axis_index("row") * lax.axis_size("head") + lax.axis_index("head")
    tokens = query_local.shape[0]
    width = query_local.shape[1] // parts
    members = width // HEAD
    rows = parts * tokens
    dtype = query_local.dtype
    local_back = min(planes - 1, -(-(STRETCH - 1) // rows))

    packed = jax.ShapeDtypeStruct((parts, 4, tokens, HEAD), dtype)
    pack = vmem_call(pack_body, packed, 4, nbytes=16 * key_local.size)
    pack = pack(key_local, value_local, key_global, value_global)
    own = exchange(pack)
    local_blocks, global_blocks = [own], [own]
    for d in range(1, planes):
        if d == 1:
            came = upward(own, 1)
            local_blocks.append(came)
            global_blocks.append(came)
        elif d == 2:
            if d <= local_back:
                local_blocks.append(upward(came[:, :2], 1))
            global_blocks.append(upward(came[:, 2:], 1))
        else:
            if d <= local_back:
                local_blocks.append(upward(local_blocks[d - 3][:, :2], 3))
            source = global_blocks[d - 3]
            global_blocks.append(upward(source[:, source.shape[1] - 2 :], 3))

    first = spot * tokens
    where = jnp.stack([plane, first]).astype(jnp.int32)
    bases = rope_tables(planes, rows)
    steps = rope_tables(rows, 1)
    turn = jnp.asarray(np.roll(np.eye(HEAD), HEAD // 2, axis=1), dtype)
    own_pos = plane * rows + first + jnp.arange(tokens, dtype=jnp.int32)
    temper = 1.0 + temper_slope * jnp.log(((own_pos + 1) // temper_floor + 1).astype(jnp.float32))
    temper = jnp.broadcast_to(temper[:, None], (tokens, HEAD))
    packed = jax.ShapeDtypeStruct((parts, 2, tokens, width), dtype)
    pack = vmem_call(pack_query_body, packed, 8, nbytes=8 * query_local.size, flops=2 * HEAD * query_local.size, smem=1)
    pack = pack(where, query_local, query_global, *bases, *steps, turn, temper)
    queries = exchange(pack)

    out_shape = jax.ShapeDtypeStruct((parts, tokens, width), dtype)
    pair_flops = 2 * 3 * rows * rows * HEAD * members
    local_out = vmem_call(
        functools.partial(local_body, local_back),
        out_shape,
        7 + local_back + 1,
        flops=pair_flops * (local_back + 1),
        nbytes=4 * rows * width * 2,
        exps=rows * rows * members * (local_back + 1),
        scratch=[
            pltpu.VMEM(((local_back + 1) * rows, 2 * HEAD), dtype),
            pltpu.VMEM(((local_back + 1) * rows, 2 * HEAD), dtype),
        ],
        smem=1,
    )(where, queries, labels[None, :], *bases, *steps, turn, *local_blocks)
    local_heads = exchange(local_out)
    global_out = vmem_call(
        functools.partial(global_body, planes),
        out_shape,
        1 + planes,
        flops=pair_flops * planes,
        nbytes=4 * rows * width * 2,
        exps=rows * rows * members * planes,
        scratch=[pltpu.VMEM((planes * rows, HEAD), dtype), pltpu.VMEM((planes * rows, 2 * HEAD), dtype)],
        smem=1,
    )(where, queries, *global_blocks)
    global_heads = exchange(global_out)
    return unpack(local_heads), unpack(global_heads)


def solution(mesh):
    ctx, head = mesh.shape["ctx"], mesh.shape["head"]

    def run(*args):
        key_heads = args[1].shape[1] // HEAD
        row = max(1, key_heads // head)
        grid = Mesh(mesh.devices.reshape(ctx // row, row, head), ("plane", "row", "head"))
        spread = P(("plane", "row", "head"), None)
        return jax.shard_map(
            shards,
            mesh=grid,
            in_specs=(spread, spread, spread, P(), spread, spread, spread),
            out_specs=(spread, spread),
            check_vma=False,
        )(*args)

    return run
```

time: 94.7 us -> 92.6 us (0.978)
  the two profiles are of different devices: /device:TPU:0 before, /device:TPU:28 now
where the time goes in v3:
time: 92.6 us; the launch traced here: 91 us
  waiting for transfers between devices  37.5 us (40%)
  Pallas kernels  24.3 us (26%)
  starting transfers between devices  22.8 us (25%)
  local copies, waits for them, and re-layouts  5.07 us (5%)
    ppermute x4, waiting for transfers between devices, upward(): return lax.ppermute(x, 'plane', [(i, i + by) for i in range(size - by)])  27.8 us
    all_to_all x4, starting transfers between devices, exchange(): return lax.all_to_all(x, IN_PLANE, split_axis=0, concat_axis=0, tiled=True)  17.7 us
    pallas_call x1, Pallas kernels, shards(): vmem_call(functools.partial(global_body, planes), out_shape, 1 + planes,...  13.8 us
    all_to_all x4, waiting for transfers between devices, exchange(): return lax.all_to_all(x, IN_PLANE, split_axis=0, concat_axis=0, tiled=True)  9.7 us
    pallas_call x1, Pallas kernels, shards(): vmem_call(functools.partial(local_body, local_back), out_shape, 7 + local...  5.7 us
    ppermute x4, starting transfers between devices, upward(): return lax.ppermute(x, 'plane', [(i, i + by) for i in range(size - by)])  5.13 us
    pallas_call x1, Pallas kernels, shards(): pack = pack(where, query_local, query_global, *bases, *steps, turn, temper)  2.96 us
    unnamed x14, local copies, waits for them, and re-layouts  2.11 us
  transfers between devices with their start and end apart: 8, of which 5 were waited for; matrix products, arithmetic and copies ran while one was open for 3% of the time, Pallas kernels for 10%

profile of v3, /device:TPU:28, one launch (start us, length us, event | category | flops | bytes accessed | tf_op | source)
XLA Modules:
  0.0 91.0 jit_solution(7864902931989655647)
XLA Ops:
  0.6 1.9 %shard_map.132 = bf16[8,4,48,128]{3,2,1,0:T(8,128)(2,1)} custom-call(bf16[48,1024]{1,0:T(8,128)(2,1)} %kl_ref.1, bf16[48,1024]{1,0:T(8,128)(2,1)} %vl_ref.1, bf16[48,1024]{1,0:T(8,128)(2,1)} %kg_ref.1, bf16[48,1024]{1,0:T(8,128)(2,1)} %vg_ref.1), custom_call_target="tpu_custom_call" | custom-call | bytes 786432 | tf_op jit(solution)/shard_map/pallas_call | solution.py:246
  2.5 4.2 %all-to-all-start.1 = ((bf16[8,4,48,128]{3,2,1,0:T(8,128)(2,1)}), bf16[8,4,48,128]{3,2,1,0:T(8,128)(2,1)S(1)}, u32[]{:S(2)}, u32[]{:S(2)}) async-start(bf16[8,4,48,128]{3,2,1,0:T(8,128)(2,1)} %shard_map.132), calls=%async_computation.1 | async-start | bytes 786432 | tf_op jit(solution)/shard_map/all_to_all | solution.py:219
  6.7 0.6 pad_add_fusion.where_ref
  7.3 0.7 broadcast_in_dim.4.temper_ref
  8.0 3.0 %shard_map.131 = bf16[8,2,48,640]{3,2,1,0:T(8,128)(2,1)} custom-call(s32[2]{0:T(128)} %pad_add_fusion.where_ref, bf16[48,5120]{1,0:T(8,128)(2,1)} %ql_ref.1, bf16[48,5120]{1,0:T(8,128)(2,1)} %qg_ref.1, f32[4,128]{1,0:T(4,128)} %constant.49.clone.cosb_ref.refs_2_, f32[4,128]{1,0:T(4,128)} %constant.50.clone.sinb_ref.refs_3_, ...), custom_call_target="tpu_custom_call" | custom-call | flops 62914560 | bytes 1966080 | tf_op jit(solution)/shard_map/pallas_call | solution.py:274
  10.9 2.6 %all-to-all-done.1.refs_7_.refs_1_ = bf16[8,4,48,128]{3,2,1,0:T(8,128)(2,1)S(1)} async-done(((bf16[8,4,48,128]{3,2,1,0:T(8,128)(2,1)}), bf16[8,4,48,128]{3,2,1,0:T(8,128)(2,1)S(1)}, u32[]{:S(2)}, u32[]{:S(2)}) %all-to-all-start.1) | async-done | bytes 393248 | tf_op jit(solution)/shard_map/all_to_all | solution.py:219
  13.6 0.0 copy-start.1
  13.6 4.9 %all-to-all-start = ((bf16[8,2,48,640]{3,2,1,0:T(8,128)(2,1)}), bf16[8,2,48,640]{3,2,1,0:T(8,128)(2,1)S(1)}, u32[]{:S(2)}, u32[]{:S(2)}) async-start(bf16[8,2,48,640]{3,2,1,0:T(8,128)(2,1)} %shard_map.131), calls=%async_computation | async-start | bytes 1966080 | tf_op jit(solution)/shard_map/all_to_all | solution.py:219
  18.5 1.3 %collective-permute-start = (bf16[8,4,48,128]{3,2,1,0:T(8,128)(2,1)S(1)}, bf16[8,4,48,128]{3,2,1,0:T(8,128)(2,1)S(1)}, u32[]{:S(2)}, u32[]{:S(2)}) collective-permute-start(bf16[8,4,48,128]{3,2,1,0:T(8,128)(2,1)S(1)} %all-to-all-done.1.refs_7_.refs_1_), channel_id=1, source_target_pairs={{0,8},{8,16},{16,24},{1,9},{9,17},{17,25},{2,10},{10,18},{18,26},{... | collective-permute-start | bytes 1179656 | tf_op jit(solution)/shard_map/ppermute | solution.py:224
  19.8 0.0 copy-done.1
  19.8 1.3 %collective-permute-start.3 = (bf16[8,2,48,128]{3,2,1,0:T(8,128)(2,1)S(1)}, bf16[8,2,48,128]{3,2,1,0:T(8,128)(2,1)S(1)}, u32[]{:S(2)}, u32[]{:S(2)}) collective-permute-start(bf16[8,2,48,128]{3,2,1,0:T(8,128)(2,1)S(1)} %slice.14), channel_id=1, source_target_pairs={{0,24},{1,25},{2,26},{3,27},{4,28},{5,29},{6,30},{7,31}} | collective-permute-start | bytes 589832 | tf_op jit(solution)/shard_map/ppermute | solution.py:224
  21.1 14.6 %collective-permute-done.refs_8_.refs_2_ = bf16[8,4,48,128]{3,2,1,0:T(8,128)(2,1)S(1)} collective-permute-done((bf16[8,4,48,128]{3,2,1,0:T(8,128)(2,1)S(1)}, bf16[8,4,48,128]{3,2,1,0:T(8,128)(2,1)S(1)}, u32[]{:S(2)}, u32[]{:S(2)}) %collective-permute-start) | collective-permute-done | bytes 393248 | tf_op jit(solution)/shard_map/ppermute | solution.py:224
  35.7 0.0 copy-start.2
  35.8 0.7 copy-done.2
  36.5 1.3 %collective-permute-start.2 = (bf16[8,2,48,128]{3,2,1,0:T(8,128)(2,1)S(1)}, bf16[8,2,48,128]{3,2,1,0:T(8,128)(2,1)S(1)}, u32[]{:S(2)}, u32[]{:S(2)}) collective-permute-start(bf16[8,2,48,128]{3,2,1,0:T(8,128)(2,1)S(1)} %get-tuple-element.2), channel_id=1, source_target_pairs={{0,8},{8,16},{16,24},{1,9},{9,17},{17,25},{2,10},{10,18},{18,26},{... | collective-permute-start | bytes 589832 | tf_op jit(solution)/shard_map/ppermute | solution.py:224
  37.8 0.0 collective-permute-done.3.refs_4_
  37.8 0.0 copy-start.4
  37.8 0.0 all-to-all-done.refs_0_
  37.8 0.0 copy-start
  37.8 6.2 %collective-permute-done.2.refs_3_ = bf16[8,2,48,128]{3,2,1,0:T(8,128)(2,1)S(1)} collective-permute-done((bf16[8,2,48,128]{3,2,1,0:T(8,128)(2,1)S(1)}, bf16[8,2,48,128]{3,2,1,0:T(8,128)(2,1)S(1)}, u32[]{:S(2)}, u32[]{:S(2)}) %collective-permute-start.2) | collective-permute-done | bytes 196640 | tf_op jit(solution)/shard_map/ppermute | solution.py:224
  44.0 0.0 copy-done.4
  44.1 0.0 copy-done
  44.1 0.0 copy-start.5
  44.1 0.7 copy-done.5
  44.7 13.8 %shard_map.134 = bf16[8,48,640]{2,1,0:T(8,128)(2,1)} custom-call(s32[2]{0:T(128)} %pad_add_fusion.where_ref, bf16[8,2,48,640]{3,2,1,0:T(8,128)(2,1)} %copy-done, bf16[8,4,48,128]{3,2,1,0:T(8,128)(2,1)} %copy-done.1, bf16[8,4,48,128]{3,2,1,0:T(8,128)(2,1)} %copy-done.2, bf16[8,2,48,128]{3,2,1,0:T(8,128)(2,1)} %copy-done.5, bf16[8,2,48,128]{3,2,1,0:T(8,128)(2,1)} %copy-done.4), custom_call_target="tpu_custom_call" | custom-call | flops 2264924160 | bytes 1966080 | tf_op jit(solution)/shard_map/pallas_call | solution.py:293
  58.5 0.0 copy-start.3
  58.5 4.3 %all-to-all-start.3 = ((bf16[8,48,640]{2,1,0:T(8,128)(2,1)}), bf16[8,48,640]{2,1,0:T(8,128)(2,1)S(1)}, u32[]{:S(2)}, u32[]{:S(2)}) async-start(bf16[8,48,640]{2,1,0:T(8,128)(2,1)} %shard_map.134), calls=%async_computation.3 | async-start | bytes 983040 | tf_op jit(solution)/shard_map/all_to_all | solution.py:219
  62.8 1.3 %collective-permute-start.1 = (bf16[8,2,48,128]{3,2,1,0:T(8,128)(2,1)S(1)}, bf16[8,2,48,128]{3,2,1,0:T(8,128)(2,1)S(1)}, u32[]{:S(2)}, u32[]{:S(2)}) collective-permute-start(bf16[8,2,48,128]{3,2,1,0:T(8,128)(2,1)S(1)} %get-tuple-element.3), channel_id=1, source_target_pairs={{0,8},{8,16},{16,24},{1,9},{9,17},{17,25},{2,10},{10,18},{18,26},{... | collective-permute-start | bytes 589832 | tf_op jit(solution)/shard_map/ppermute | solution.py:224
  64.1 0.0 copy-done.3
  64.1 0.6 broadcast_in_dim.10.refs_1_
  64.7 6.9 %collective-permute-done.1.refs_9_ = bf16[8,2,48,128]{3,2,1,0:T(8,128)(2,1)S(1)} collective-permute-done((bf16[8,2,48,128]{3,2,1,0:T(8,128)(2,1)S(1)}, bf16[8,2,48,128]{3,2,1,0:T(8,128)(2,1)S(1)}, u32[]{:S(2)}, u32[]{:S(2)}) %collective-permute-start.1) | collective-permute-done | bytes 196640 | tf_op jit(solution)/shard_map/ppermute | solution.py:224
  71.7 0.0 copy-start.6
  71.7 0.7 copy-done.6
  72.3 5.7 %shard_map.133 = bf16[8,48,640]{2,1,0:T(8,128)(2,1)} custom-call(s32[2]{0:T(128)} %pad_add_fusion.where_ref, bf16[8,2,48,640]{3,2,1,0:T(8,128)(2,1)} %copy-done, s32[1,1536]{1,0:T(1,128)} %broadcast_in_dim.10.refs_1_, f32[4,128]{1,0:T(4,128)} %constant.49.clone.cosb_ref.refs_2_, f32[4,128]{1,0:T(4,128)} %constant.50.clone.sinb_ref.refs_3_, ...), custom_call_target="tpu_custom_call" | custom-call | flops 1698693120 | bytes 1966080 | tf_op jit(solution)/shard_map/pallas_call | solution.py:279
  78.0 0.0 all-to-all-done.3
  78.0 4.2 %all-to-all-start.2 = ((bf16[8,48,640]{2,1,0:T(8,128)(2,1)}), bf16[8,48,640]{2,1,0:T(8,128)(2,1)S(1)}, u32[]{:S(2)}, u32[]{:S(2)}) async-start(bf16[8,48,640]{2,1,0:T(8,128)(2,1)} %shard_map.133), calls=%async_computation.2 | async-start | bytes 983040 | tf_op jit(solution)/shard_map/all_to_all | solution.py:219
  82.2 0.8 copy.17
  83.1 7.1 %all-to-all-done.2 = bf16[8,48,640]{2,1,0:T(8,128)(2,1)S(1)} async-done(((bf16[8,48,640]{2,1,0:T(8,128)(2,1)}), bf16[8,48,640]{2,1,0:T(8,128)(2,1)S(1)}, u32[]{:S(2)}, u32[]{:S(2)}) %all-to-all-start.2) | async-done | bytes 491552 | tf_op jit(solution)/shard_map/all_to_all | solution.py:219
  90.1 0.8 copy.16
  (3 shorter events, 0.1 us)
Async XLA Ops:
  2.5 11.1 %all-to-all-start.1 = ((bf16[8,4,48,128]{3,2,1,0:T(8,128)(2,1)}), bf16[8,4,48,128]{3,2,1,0:T(8,128)(2,1)S(1)}, u32[]{:S(2)}, u32[]{:S(2)}) async-start(bf16[8,4,48,128]{3,2,1,0:T(8,128)(2,1)} %shard_map.132), calls=%async_computation.1 | async-start | bytes 786432 | tf_op jit(solution)/shard_map/all_to_all | solution.py:219
  13.6 6.2 %copy-start.1 = (bf16[8,4,48,128]{3,2,1,0:T(8,128)(2,1)}, bf16[8,4,48,128]{3,2,1,0:T(8,128)(2,1)S(1)}, u32[]{:S(2)}) copy-start(bf16[8,4,48,128]{3,2,1,0:T(8,128)(2,1)S(1)} %all-to-all-done.1.refs_7_.refs_1_) | copy-start | bytes 1179652
  13.6 24.2 %all-to-all-start = ((bf16[8,2,48,640]{3,2,1,0:T(8,128)(2,1)}), bf16[8,2,48,640]{3,2,1,0:T(8,128)(2,1)S(1)}, u32[]{:S(2)}, u32[]{:S(2)}) async-start(bf16[8,2,48,640]{3,2,1,0:T(8,128)(2,1)} %shard_map.131), calls=%async_computation | async-start | bytes 1966080 | tf_op jit(solution)/shard_map/all_to_all | solution.py:219
  18.5 17.2 %collective-permute-start = (bf16[8,4,48,128]{3,2,1,0:T(8,128)(2,1)S(1)}, bf16[8,4,48,128]{3,2,1,0:T(8,128)(2,1)S(1)}, u32[]{:S(2)}, u32[]{:S(2)}) collective-permute-start(bf16[8,4,48,128]{3,2,1,0:T(8,128)(2,1)S(1)} %all-to-all-done.1.refs_7_.refs_1_), channel_id=1, source_target_pairs={{0,8},{8,16},{16,24},{1,9},{9,17},{17,25},{2,10},{10,18},{18,26},{... | collective-permute-start | bytes 1179656 | tf_op jit(solution)/shard_map/ppermute | solution.py:224
  19.8 18.0 %collective-permute-start.3 = (bf16[8,2,48,128]{3,2,1,0:T(8,128)(2,1)S(1)}, bf16[8,2,48,128]{3,2,1,0:T(8,128)(2,1)S(1)}, u32[]{:S(2)}, u32[]{:S(2)}) collective-permute-start(bf16[8,2,48,128]{3,2,1,0:T(8,128)(2,1)S(1)} %slice.14), channel_id=1, source_target_pairs={{0,24},{1,25},{2,26},{3,27},{4,28},{5,29},{6,30},{7,31}} | collective-permute-start | bytes 589832 | tf_op jit(solution)/shard_map/ppermute | solution.py:224
  35.7 0.8 copy-start.2
  36.5 7.6 %collective-permute-start.2 = (bf16[8,2,48,128]{3,2,1,0:T(8,128)(2,1)S(1)}, bf16[8,2,48,128]{3,2,1,0:T(8,128)(2,1)S(1)}, u32[]{:S(2)}, u32[]{:S(2)}) collective-permute-start(bf16[8,2,48,128]{3,2,1,0:T(8,128)(2,1)S(1)} %get-tuple-element.2), channel_id=1, source_target_pairs={{0,8},{8,16},{16,24},{1,9},{9,17},{17,25},{2,10},{10,18},{18,26},{... | collective-permute-start | bytes 589832 | tf_op jit(solution)/shard_map/ppermute | solution.py:224
  37.8 6.3 %copy-start.4 = (bf16[8,2,48,128]{3,2,1,0:T(8,128)(2,1)}, bf16[8,2,48,128]{3,2,1,0:T(8,128)(2,1)S(1)}, u32[]{:S(2)}) copy-start(bf16[8,2,48,128]{3,2,1,0:T(8,128)(2,1)S(1)} %collective-permute-done.3.refs_4_) | copy-start | bytes 589828
  37.8 6.2 %copy-start = (bf16[8,2,48,640]{3,2,1,0:T(8,128)(2,1)}, bf16[8,2,48,640]{3,2,1,0:T(8,128)(2,1)S(1)}, u32[]{:S(2)}) copy-start(bf16[8,2,48,640]{3,2,1,0:T(8,128)(2,1)S(1)} %all-to-all-done.refs_0_) | copy-start | bytes 2949124
  44.1 0.7 copy-start.5
  58.5 5.6 %copy-start.3 = (s32[1536]{0:T(1024)S(1)}, s32[1536]{0:T(1024)}, u32[]{:S(2)}) copy-start(s32[1536]{0:T(1024)} %param.15) | copy-start | bytes 18436
  58.5 19.5 %all-to-all-start.3 = ((bf16[8,48,640]{2,1,0:T(8,128)(2,1)}), bf16[8,48,640]{2,1,0:T(8,128)(2,1)S(1)}, u32[]{:S(2)}, u32[]{:S(2)}) async-start(bf16[8,48,640]{2,1,0:T(8,128)(2,1)} %shard_map.134), calls=%async_computation.3 | async-start | bytes 983040 | tf_op jit(solution)/shard_map/all_to_all | solution.py:219
  62.8 8.8 %collective-permute-start.1 = (bf16[8,2,48,128]{3,2,1,0:T(8,128)(2,1)S(1)}, bf16[8,2,48,128]{3,2,1,0:T(8,128)(2,1)S(1)}, u32[]{:S(2)}, u32[]{:S(2)}) collective-permute-start(bf16[8,2,48,128]{3,2,1,0:T(8,128)(2,1)S(1)} %get-tuple-element.3), channel_id=1, source_target_pairs={{0,8},{8,16},{16,24},{1,9},{9,17},{17,25},{2,10},{10,18},{18,26},{... | collective-permute-start | bytes 589832 | tf_op jit(solution)/shard_map/ppermute | solution.py:224
  71.7 0.7 copy-start.6
  78.0 12.1 %all-to-all-start.2 = ((bf16[8,48,640]{2,1,0:T(8,128)(2,1)}), bf16[8,48,640]{2,1,0:T(8,128)(2,1)S(1)}, u32[]{:S(2)}, u32[]{:S(2)}) async-start(bf16[8,48,640]{2,1,0:T(8,128)(2,1)} %shard_map.133), calls=%async_computation.2 | async-start | bytes 983040 | tf_op jit(solution)/shard_map/all_to_all | solution.py:219

commit v4 on v3

--- a/solution.py
+++ b/solution.py
@@ -20,6 +20,7 @@
 masked_score = -1e30
 log2e = 1.4426950408889634
 far = 30000.0
+near_bytes = 4 << 20
 
 IN_PLANE = ("row", "head")
 
@@ -215,6 +216,12 @@
         lax.fori_loop(0, members, shifted, 0)
 
 
+def near(*arrays):
+    if sum(x.size * x.dtype.itemsize for x in arrays) > near_bytes:
+        return arrays
+    return tuple(pltpu.with_memory_space_constraint(x, pltpu.VMEM) for x in arrays)
+
+
 def exchange(x):
     return lax.all_to_all(x, IN_PLANE, split_axis=0, concat_axis=0, tiled=True)
 
@@ -269,10 +276,15 @@
     own_pos = plane * rows + first + jnp.arange(tokens, dtype=jnp.int32)
     temper = 1.0 + temper_slope * jnp.log(((own_pos + 1) // temper_floor + 1).astype(jnp.float32))
     temper = jnp.broadcast_to(temper[:, None], (tokens, HEAD))
+    label_row = labels[None, :]
     packed = jax.ShapeDtypeStruct((parts, 2, tokens, width), dtype)
     pack = vmem_call(pack_query_body, packed, 8, nbytes=8 * query_local.size, flops=2 * HEAD * query_local.size, smem=1)
     pack = pack(where, query_local, query_global, *bases, *steps, turn, temper)
     queries = exchange(pack)
+
+    kept = near(queries, *local_blocks, *global_blocks[1:])
+    queries, local_blocks = kept[0], kept[1 : local_back + 2]
+    global_blocks = [local_blocks[0], *kept[local_back + 2 :]]
 
     out_shape = jax.ShapeDtypeStruct((parts, tokens, width), dtype)
     pair_flops = 2 * 3 * rows * rows * HEAD * members
@@ -288,7 +300,7 @@
             pltpu.VMEM(((local_back + 1) * rows, 2 * HEAD), dtype),
         ],
         smem=1,
-    )(where, queries, labels[None, :], *bases, *steps, turn, *local_blocks)
+    )(where, queries, label_row, *bases, *steps, turn, *local_blocks)
     local_heads = exchange(local_out)
     global_out = vmem_call(
         functools.partial(global_body, planes),

time: 92.6 us -> 88.7 us (0.958)
  local copies, waits for them, and re-layouts: 5.07 us -> 2.97 us
  Pallas kernels: 24.3 us -> 22.8 us
    unnamed x14 -> x2, local copies, waits for them, and re-layouts: 2.11 us -> 0.01 us
  transfers between devices with their start and end apart: 8 -> 8, of which waited for: 5 -> 5; matrix products, arithmetic and copies ran while one was open for 3% -> 3% of each run, Pallas kernels for 10% -> 9%
where the time goes in v4:
time: 88.7 us; the launch traced here: 87.1 us
  waiting for transfers between devices  37.1 us (42%)
  starting transfers between devices  22.9 us (26%)
  Pallas kernels  22.8 us (26%)
  local copies, waits for them, and re-layouts  2.97 us (3%)
    ppermute x4, waiting for transfers between devices, upward(): return lax.ppermute(x, 'plane', [(i, i + by) for i in range(size - by)])  27.5 us
    all_to_all x4, starting transfers between devices, exchange(): return lax.all_to_all(x, IN_PLANE, split_axis=0, concat_axis=0, tiled=True)  17.7 us
    pallas_call x1, Pallas kernels, shards(): vmem_call(functools.partial(global_body, planes), out_shape, 1 + planes,...  12.9 us
    all_to_all x4, waiting for transfers between devices, exchange(): return lax.all_to_all(x, IN_PLANE, split_axis=0, concat_axis=0, tiled=True)  9.66 us
    ppermute x4, starting transfers between devices, upward(): return lax.ppermute(x, 'plane', [(i, i + by) for i in range(size - by)])  5.14 us
    pallas_call x1, Pallas kernels, shards(): vmem_call(functools.partial(local_body, local_back), out_shape, 7 + local...  5.09 us
    pallas_call x1, Pallas kernels, shards(): pack = pack(where, query_local, query_global, *bases, *steps, turn, temper)  2.95 us
    pallas_call x1, Pallas kernels, shards(): pack = pack(key_local, value_local, key_global, value_global)  1.85 us
  transfers between devices with their start and end apart: 8, of which 5 were waited for; matrix products, arithmetic and copies ran while one was open for 3% of the time, Pallas kernels for 9%

profile of v4, /device:TPU:28, one launch (start us, length us, event | category | flops | bytes accessed | tf_op | source)
XLA Modules:
  0.0 87.1 jit_solution(17724349865748513181)
XLA Ops:
  0.6 1.9 %shard_map.132 = bf16[8,4,48,128]{3,2,1,0:T(8,128)(2,1)} custom-call(bf16[48,1024]{1,0:T(8,128)(2,1)} %kl_ref.1, bf16[48,1024]{1,0:T(8,128)(2,1)} %vl_ref.1, bf16[48,1024]{1,0:T(8,128)(2,1)} %kg_ref.1, bf16[48,1024]{1,0:T(8,128)(2,1)} %vg_ref.1), custom_call_target="tpu_custom_call" | custom-call | bytes 786432 | tf_op jit(solution)/shard_map/pallas_call | solution.py:253
  2.5 4.2 %all-to-all-start.1 = ((bf16[8,4,48,128]{3,2,1,0:T(8,128)(2,1)}), bf16[8,4,48,128]{3,2,1,0:T(8,128)(2,1)S(1)}, u32[]{:S(2)}, u32[]{:S(2)}) async-start(bf16[8,4,48,128]{3,2,1,0:T(8,128)(2,1)} %shard_map.132), calls=%async_computation.1 | async-start | bytes 786432 | tf_op jit(solution)/shard_map/all_to_all | solution.py:226
  6.7 0.6 pad_add_fusion.where_ref
  7.3 0.7 broadcast_in_dim.4.temper_ref
  8.0 2.9 %shard_map.131 = bf16[8,2,48,640]{3,2,1,0:T(8,128)(2,1)} custom-call(s32[2]{0:T(128)} %pad_add_fusion.where_ref, bf16[48,5120]{1,0:T(8,128)(2,1)} %ql_ref.1, bf16[48,5120]{1,0:T(8,128)(2,1)} %qg_ref.1, f32[4,128]{1,0:T(4,128)} %constant.49.clone.cosb_ref.refs_2_, f32[4,128]{1,0:T(4,128)} %constant.50.clone.sinb_ref.refs_3_, ...), custom_call_target="tpu_custom_call" | custom-call | flops 62914560 | bytes 1966080 | tf_op jit(solution)/shard_map/pallas_call | solution.py:282
  11.0 2.6 %all-to-all-done.1.refs_7_.refs_1_ = bf16[8,4,48,128]{3,2,1,0:T(8,128)(2,1)S(1)} async-done(((bf16[8,4,48,128]{3,2,1,0:T(8,128)(2,1)}), bf16[8,4,48,128]{3,2,1,0:T(8,128)(2,1)S(1)}, u32[]{:S(2)}, u32[]{:S(2)}) %all-to-all-start.1) | async-done | bytes 393248 | tf_op jit(solution)/shard_map/all_to_all | solution.py:226
  13.6 4.9 %all-to-all-start = ((bf16[8,2,48,640]{3,2,1,0:T(8,128)(2,1)}), bf16[8,2,48,640]{3,2,1,0:T(8,128)(2,1)S(1)}, u32[]{:S(2)}, u32[]{:S(2)}) async-start(bf16[8,2,48,640]{3,2,1,0:T(8,128)(2,1)} %shard_map.131), calls=%async_computation | async-start | bytes 1966080 | tf_op jit(solution)/shard_map/all_to_all | solution.py:226
  18.5 1.3 %collective-permute-start = (bf16[8,4,48,128]{3,2,1,0:T(8,128)(2,1)S(1)}, bf16[8,4,48,128]{3,2,1,0:T(8,128)(2,1)S(1)}, u32[]{:S(2)}, u32[]{:S(2)}) collective-permute-start(bf16[8,4,48,128]{3,2,1,0:T(8,128)(2,1)S(1)} %all-to-all-done.1.refs_7_.refs_1_), channel_id=1, source_target_pairs={{0,8},{8,16},{16,24},{1,9},{9,17},{17,25},{2,10},{10,18},{18,26},{... | collective-permute-start | bytes 1179656 | tf_op jit(solution)/shard_map/ppermute | solution.py:231
  19.8 1.3 %collective-permute-start.3 = (bf16[8,2,48,128]{3,2,1,0:T(8,128)(2,1)S(1)}, bf16[8,2,48,128]{3,2,1,0:T(8,128)(2,1)S(1)}, u32[]{:S(2)}, u32[]{:S(2)}) collective-permute-start(bf16[8,2,48,128]{3,2,1,0:T(8,128)(2,1)S(1)} %slice.14), channel_id=1, source_target_pairs={{0,24},{1,25},{2,26},{3,27},{4,28},{5,29},{6,30},{7,31}} | collective-permute-start | bytes 589832 | tf_op jit(solution)/shard_map/ppermute | solution.py:231
  21.1 14.3 %collective-permute-done.refs_8_.refs_2_ = bf16[8,4,48,128]{3,2,1,0:T(8,128)(2,1)S(1)} collective-permute-done((bf16[8,4,48,128]{3,2,1,0:T(8,128)(2,1)S(1)}, bf16[8,4,48,128]{3,2,1,0:T(8,128)(2,1)S(1)}, u32[]{:S(2)}, u32[]{:S(2)}) %collective-permute-start) | collective-permute-done | bytes 393248 | tf_op jit(solution)/shard_map/ppermute | solution.py:231
  35.5 1.3 %collective-permute-start.2 = (bf16[8,2,48,128]{3,2,1,0:T(8,128)(2,1)S(1)}, bf16[8,2,48,128]{3,2,1,0:T(8,128)(2,1)S(1)}, u32[]{:S(2)}, u32[]{:S(2)}) collective-permute-start(bf16[8,2,48,128]{3,2,1,0:T(8,128)(2,1)S(1)} %get-tuple-element.2), channel_id=1, source_target_pairs={{0,8},{8,16},{16,24},{1,9},{9,17},{17,25},{2,10},{10,18},{18,26},{... | collective-permute-start | bytes 589832 | tf_op jit(solution)/shard_map/ppermute | solution.py:231
  36.8 0.0 collective-permute-done.3.refs_4_
  36.8 0.0 all-to-all-done.refs_0_
  36.8 6.2 %collective-permute-done.2.refs_3_ = bf16[8,2,48,128]{3,2,1,0:T(8,128)(2,1)S(1)} collective-permute-done((bf16[8,2,48,128]{3,2,1,0:T(8,128)(2,1)S(1)}, bf16[8,2,48,128]{3,2,1,0:T(8,128)(2,1)S(1)}, u32[]{:S(2)}, u32[]{:S(2)}) %collective-permute-start.2) | collective-permute-done | bytes 196640 | tf_op jit(solution)/shard_map/ppermute | solution.py:231
  43.0 12.9 %shard_map.134 = bf16[8,48,640]{2,1,0:T(8,128)(2,1)} custom-call(s32[2]{0:T(128)} %pad_add_fusion.where_ref, bf16[8,2,48,640]{3,2,1,0:T(8,128)(2,1)S(1)} %all-to-all-done.refs_0_, bf16[8,4,48,128]{3,2,1,0:T(8,128)(2,1)S(1)} %all-to-all-done.1.refs_7_.refs_1_, bf16[8,4,48,128]{3,2,1,0:T(8,128)(2,1)S(1)} %collective-permute-done.refs_8_.refs_2_, ...), custom_call_target="tpu_custom_call" | custom-call | flops 2264924160 | bytes 1966080 | tf_op jit(solution)/shard_map/pallas_call | solution.py:305
  55.9 0.0 copy-start
  55.9 4.3 %all-to-all-start.3 = ((bf16[8,48,640]{2,1,0:T(8,128)(2,1)}), bf16[8,48,640]{2,1,0:T(8,128)(2,1)S(1)}, u32[]{:S(2)}, u32[]{:S(2)}) async-start(bf16[8,48,640]{2,1,0:T(8,128)(2,1)} %shard_map.134), calls=%async_computation.3 | async-start | bytes 983040 | tf_op jit(solution)/shard_map/all_to_all | solution.py:226
  60.2 1.3 %collective-permute-start.1 = (bf16[8,2,48,128]{3,2,1,0:T(8,128)(2,1)S(1)}, bf16[8,2,48,128]{3,2,1,0:T(8,128)(2,1)S(1)}, u32[]{:S(2)}, u32[]{:S(2)}) collective-permute-start(bf16[8,2,48,128]{3,2,1,0:T(8,128)(2,1)S(1)} %get-tuple-element.3), channel_id=1, source_target_pairs={{0,8},{8,16},{16,24},{1,9},{9,17},{17,25},{2,10},{10,18},{18,26},{... | collective-permute-start | bytes 589832 | tf_op jit(solution)/shard_map/ppermute | solution.py:231
  61.5 0.0 copy-done
  61.5 0.6 broadcast_in_dim.10.refs_1_
  62.1 6.9 %collective-permute-done.1.refs_9_ = bf16[8,2,48,128]{3,2,1,0:T(8,128)(2,1)S(1)} collective-permute-done((bf16[8,2,48,128]{3,2,1,0:T(8,128)(2,1)S(1)}, bf16[8,2,48,128]{3,2,1,0:T(8,128)(2,1)S(1)}, u32[]{:S(2)}, u32[]{:S(2)}) %collective-permute-start.1) | collective-permute-done | bytes 196640 | tf_op jit(solution)/shard_map/ppermute | solution.py:231
  69.0 5.1 %shard_map.133 = bf16[8,48,640]{2,1,0:T(8,128)(2,1)} custom-call(s32[2]{0:T(128)} %pad_add_fusion.where_ref, bf16[8,2,48,640]{3,2,1,0:T(8,128)(2,1)S(1)} %all-to-all-done.refs_0_, s32[1,1536]{1,0:T(1,128)} %broadcast_in_dim.10.refs_1_, f32[4,128]{1,0:T(4,128)} %constant.49.clone.cosb_ref.refs_2_, f32[4,128]{1,0:T(4,128)} %constant.50.clone.sinb_ref.refs_3_, ...), custom_call_target="tpu_custom_call" | custom-call | flops 1698693120 | bytes 1966080 | tf_op jit(solution)/shard_map/pallas_call | solution.py:291
  74.1 0.0 all-to-all-done.3
  74.1 4.2 %all-to-all-start.2 = ((bf16[8,48,640]{2,1,0:T(8,128)(2,1)}), bf16[8,48,640]{2,1,0:T(8,128)(2,1)S(1)}, u32[]{:S(2)}, u32[]{:S(2)}) async-start(bf16[8,48,640]{2,1,0:T(8,128)(2,1)} %shard_map.133), calls=%async_computation.2 | async-start | bytes 983040 | tf_op jit(solution)/shard_map/all_to_all | solution.py:226
  78.3 0.8 copy.17
  79.2 7.1 %all-to-all-done.2 = bf16[8,48,640]{2,1,0:T(8,128)(2,1)S(1)} async-done(((bf16[8,48,640]{2,1,0:T(8,128)(2,1)}), bf16[8,48,640]{2,1,0:T(8,128)(2,1)S(1)}, u32[]{:S(2)}, u32[]{:S(2)}) %all-to-all-start.2) | async-done | bytes 491552 | tf_op jit(solution)/shard_map/all_to_all | solution.py:226
  86.2 0.8 copy.16
  (3 shorter events, 0.1 us)
Async XLA Ops:
  2.5 11.1 %all-to-all-start.1 = ((bf16[8,4,48,128]{3,2,1,0:T(8,128)(2,1)}), bf16[8,4,48,128]{3,2,1,0:T(8,128)(2,1)S(1)}, u32[]{:S(2)}, u32[]{:S(2)}) async-start(bf16[8,4,48,128]{3,2,1,0:T(8,128)(2,1)} %shard_map.132), calls=%async_computation.1 | async-start | bytes 786432 | tf_op jit(solution)/shard_map/all_to_all | solution.py:226
  13.6 23.2 %all-to-all-start = ((bf16[8,2,48,640]{3,2,1,0:T(8,128)(2,1)}), bf16[8,2,48,640]{3,2,1,0:T(8,128)(2,1)S(1)}, u32[]{:S(2)}, u32[]{:S(2)}) async-start(bf16[8,2,48,640]{3,2,1,0:T(8,128)(2,1)} %shard_map.131), calls=%async_computation | async-start | bytes 1966080 | tf_op jit(solution)/shard_map/all_to_all | solution.py:226
  18.5 16.9 %collective-permute-start = (bf16[8,4,48,128]{3,2,1,0:T(8,128)(2,1)S(1)}, bf16[8,4,48,128]{3,2,1,0:T(8,128)(2,1)S(1)}, u32[]{:S(2)}, u32[]{:S(2)}) collective-permute-start(bf16[8,4,48,128]{3,2,1,0:T(8,128)(2,1)S(1)} %all-to-all-done.1.refs_7_.refs_1_), channel_id=1, source_target_pairs={{0,8},{8,16},{16,24},{1,9},{9,17},{17,25},{2,10},{10,18},{18,26},{... | collective-permute-start | bytes 1179656 | tf_op jit(solution)/shard_map/ppermute | solution.py:231
  19.8 17.0 %collective-permute-start.3 = (bf16[8,2,48,128]{3,2,1,0:T(8,128)(2,1)S(1)}, bf16[8,2,48,128]{3,2,1,0:T(8,128)(2,1)S(1)}, u32[]{:S(2)}, u32[]{:S(2)}) collective-permute-start(bf16[8,2,48,128]{3,2,1,0:T(8,128)(2,1)S(1)} %slice.14), channel_id=1, source_target_pairs={{0,24},{1,25},{2,26},{3,27},{4,28},{5,29},{6,30},{7,31}} | collective-permute-start | bytes 589832 | tf_op jit(solution)/shard_map/ppermute | solution.py:231
  35.5 7.6 %collective-permute-start.2 = (bf16[8,2,48,128]{3,2,1,0:T(8,128)(2,1)S(1)}, bf16[8,2,48,128]{3,2,1,0:T(8,128)(2,1)S(1)}, u32[]{:S(2)}, u32[]{:S(2)}) collective-permute-start(bf16[8,2,48,128]{3,2,1,0:T(8,128)(2,1)S(1)} %get-tuple-element.2), channel_id=1, source_target_pairs={{0,8},{8,16},{16,24},{1,9},{9,17},{17,25},{2,10},{10,18},{18,26},{... | collective-permute-start | bytes 589832 | tf_op jit(solution)/shard_map/ppermute | solution.py:231
  55.9 5.6 %copy-start = (s32[1536]{0:T(1024)S(1)}, s32[1536]{0:T(1024)}, u32[]{:S(2)}) copy-start(s32[1536]{0:T(1024)} %param.15) | copy-start | bytes 18436
  55.9 18.2 %all-to-all-start.3 = ((bf16[8,48,640]{2,1,0:T(8,128)(2,1)}), bf16[8,48,640]{2,1,0:T(8,128)(2,1)S(1)}, u32[]{:S(2)}, u32[]{:S(2)}) async-start(bf16[8,48,640]{2,1,0:T(8,128)(2,1)} %shard_map.134), calls=%async_computation.3 | async-start | bytes 983040 | tf_op jit(solution)/shard_map/all_to_all | solution.py:226
  60.2 8.8 %collective-permute-start.1 = (bf16[8,2,48,128]{3,2,1,0:T(8,128)(2,1)S(1)}, bf16[8,2,48,128]{3,2,1,0:T(8,128)(2,1)S(1)}, u32[]{:S(2)}, u32[]{:S(2)}) collective-permute-start(bf16[8,2,48,128]{3,2,1,0:T(8,128)(2,1)S(1)} %get-tuple-element.3), channel_id=1, source_target_pairs={{0,8},{8,16},{16,24},{1,9},{9,17},{17,25},{2,10},{10,18},{18,26},{... | collective-permute-start | bytes 589832 | tf_op jit(solution)/shard_map/ppermute | solution.py:231
  74.1 12.1 %all-to-all-start.2 = ((bf16[8,48,640]{2,1,0:T(8,128)(2,1)}), bf16[8,48,640]{2,1,0:T(8,128)(2,1)S(1)}, u32[]{:S(2)}, u32[]{:S(2)}) async-start(bf16[8,48,640]{2,1,0:T(8,128)(2,1)} %shard_map.133), calls=%async_computation.2 | async-start | bytes 983040 | tf_op jit(solution)/shard_map/all_to_all | solution.py:226

commit v5 on v4

v5 whole, which is shorter than its diff:
```python
import functools

import jax
import jax.numpy as jnp
import numpy as np
from jax import lax
from jax.experimental import pallas as pl
from jax.experimental.pallas import tpu as pltpu
from jax.sharding import Mesh
from jax.sharding import PartitionSpec as P


HEAD = 128
STRETCH = 768

rope_base = 500000.0
norm_epsilon = 1e-06
temper_floor = 8192
temper_slope = 0.1
masked_score = -1e30
log2e = 1.4426950408889634
far = 30000.0
near_bytes = 5 << 20
vmem_bytes = 40 << 20

IN_PLANE = ("row", "head")


def rope_tables(count, step):
    half = HEAD // 2
    frequency = rope_base ** (-(np.arange(HEAD) % half) * 2.0 / HEAD)
    angles = (np.arange(count) * step)[:, None] * frequency[None, :]
    sign = np.where(np.arange(HEAD) < half, -1.0, 1.0)
    return jnp.asarray(np.cos(angles), jnp.float32), jnp.asarray(np.sin(angles) * sign, jnp.float32)


def turned(cos_base, sin_base, cos_row, sin_row):
    return cos_base * cos_row - sin_base * sin_row, sin_base * cos_row + cos_base * sin_row


def rotated_unit(x, turn, cosine, sine):
    swapped = jnp.dot(x, turn, preferred_element_type=jnp.float32)
    y = x.astype(jnp.float32) * cosine + swapped * sine
    return y * lax.rsqrt(jnp.mean(y * y, axis=-1, keepdims=True) + norm_epsilon)


def vmem_call(body, out_shapes, n_in, flops=0, nbytes=0, exps=0, scratch=(), smem=0, limit=None):
    return pl.pallas_call(
        body,
        out_shape=out_shapes,
        in_specs=[pl.BlockSpec(memory_space=pltpu.SMEM)] * smem
        + [pl.BlockSpec(memory_space=pltpu.VMEM)] * n_in,
        out_specs=jax.tree.map(lambda _: pl.BlockSpec(memory_space=pltpu.VMEM), out_shapes),
        scratch_shapes=list(scratch),
        compiler_params=pltpu.CompilerParams(vmem_limit_bytes=limit),
        cost_estimate=pl.CostEstimate(flops=flops, bytes_accessed=nbytes, transcendentals=exps),
    )


def pack_body(kl_ref, vl_ref, kg_ref, vg_ref, o_ref):
    for d in range(o_ref.shape[0]):
        for a, ref in enumerate((kl_ref, vl_ref, kg_ref, vg_ref)):
            o_ref[d, a] = ref[:, d * HEAD : (d + 1) * HEAD]


def pack_query_body(where_ref, ql_ref, qg_ref, cosb_ref, sinb_ref, cosr_ref, sinr_ref, turn_ref, temper_ref, o_ref):
    members = o_ref.shape[3] // HEAD
    tokens = ql_ref.shape[0]
    plane, first = where_ref[0], pl.multiple_of(where_ref[1], 16)
    mine = pl.ds(first, tokens)
    cosine, sine = turned(cosb_ref[pl.ds(plane, 1)], sinb_ref[pl.ds(plane, 1)], cosr_ref[mine], sinr_ref[mine])
    turn = turn_ref[...]
    for d in range(o_ref.shape[0]):
        for g in range(members):
            at = (d * members + g) * HEAD
            to = slice(g * HEAD, (g + 1) * HEAD)
            y = rotated_unit(ql_ref[:, at : at + HEAD], turn, cosine, sine)
            o_ref[d, 0, :, to] = y.astype(o_ref.dtype)
            z = qg_ref[:, at : at + HEAD].astype(jnp.float32) * temper_ref[...]
            o_ref[d, 1, :, to] = z.astype(o_ref.dtype)


def causal(rows):
    r = lax.broadcasted_iota(jnp.int32, (rows, rows), 0)
    c = lax.broadcasted_iota(jnp.int32, (rows, rows), 1)
    return c <= r


def masked(weights, rows):
    first = jnp.where(causal(rows), weights[:, :rows], 0.0)
    if weights.shape[1] == rows:
        return first
    return jnp.concatenate([first, weights[:, rows:]], axis=1)


NT = (((1,), (1,)), ((), ()))


def take_values(v_ref, i, values, valid):
    rows = values.shape[0]
    v_ref[i * rows : (i + 1) * rows, :HEAD] = values
    ones = jnp.broadcast_to(jnp.where(valid, 1.0, 0.0), (rows, HEAD))
    v_ref[i * rows : (i + 1) * rows, HEAD:] = ones.astype(v_ref.dtype)


def same_stretch(labels_ref, behind, rows):
    ids = labels_ref[:, pl.ds(pl.multiple_of(behind * rows, HEAD), rows)]
    return jnp.where(lax.broadcasted_iota(jnp.int32, (HEAD, rows), 0) == ids, 1.0, 0.0).T


def take_local(shared, plane, distances, blocks, k_ref, v_ref):
    labels_ref, cosb_ref, sinb_ref, cosr_ref, sinr_ref, turn_ref = shared
    turn = turn_ref[...]
    for i, d in enumerate(distances):
        rows = k_ref.shape[0] // len(distances)
        behind = jnp.maximum(plane - d, 0)
        base = pl.ds(behind, 1)
        cosine, sine = turned(cosb_ref[base], sinb_ref[base], cosr_ref[...], sinr_ref[...])
        at = slice(i * rows, (i + 1) * rows)
        keys = blocks[i][:, 0].reshape(rows, HEAD)
        k_ref[at, :HEAD] = rotated_unit(keys, turn, cosine, sine).astype(k_ref.dtype)
        k_ref[at, HEAD:] = same_stretch(labels_ref, behind, rows).astype(k_ref.dtype)
        take_values(v_ref, i, blocks[i][:, 1].reshape(rows, HEAD), plane >= d)


def take_global(plane, distances, blocks, k_ref, v_ref):
    for i, d in enumerate(distances):
        rows = k_ref.shape[0] // len(distances)
        last = blocks[i].shape[1] - 1
        k_ref[i * rows : (i + 1) * rows] = blocks[i][:, last - 1].reshape(rows, HEAD)
        take_values(v_ref, i, blocks[i][:, last].reshape(rows, HEAD), plane >= d)


def query_of(q_ref, layer, g):
    parts, _, tokens, _ = q_ref.shape
    at = pl.multiple_of(g * HEAD, HEAD)
    return q_ref[:, layer, :, pl.ds(at, HEAD)].reshape(parts * tokens, HEAD)


def summed(q, k_ref, v_ref, rows, own):
    acc = None
    for at in range(0, k_ref.shape[0], 4 * rows):
        used = slice(at, min(k_ref.shape[0], at + 4 * rows))
        scores = lax.dot_general(q, k_ref[used], NT, preferred_element_type=jnp.float32)
        weights = jnp.exp2(scores * (log2e * HEAD**-0.5))
        if own and at == 0:
            weights = masked(weights, rows)
        part = jnp.dot(weights.astype(jnp.bfloat16), v_ref[used], preferred_element_type=jnp.float32)
        acc = part if acc is None else acc + part
    return acc


def early_body(n_near, where_ref, *refs):
    q_ref, *shared = refs[:7]
    blocks = refs[7 : 7 + n_near]
    lacc_ref, gacc_ref, lk_ref, lv_ref, gk_ref, gv_ref = refs[7 + n_near :]
    members, rows, _ = lacc_ref.shape
    plane = where_ref[0]
    take_local(shared, plane, range(n_near), blocks, lk_ref, lv_ref)
    take_global(plane, range(n_near), blocks, gk_ref, gv_ref)
    other = ((same_stretch(shared[0], plane, rows) - 1.0) * far).astype(lk_ref.dtype)

    def member(g, carry):
        q = jnp.concatenate([query_of(q_ref, 0, g), other], axis=1)
        lacc_ref[g] = summed(q, lk_ref, lv_ref, rows, True)
        gacc_ref[g] = summed(query_of(q_ref, 1, g), gk_ref, gv_ref, rows, True)
        return carry

    lax.fori_loop(0, members, member, 0, unroll=True)


def late_body(n_near, local_back, n, where_ref, *refs):
    q_ref, *shared = refs[:7]
    blocks = refs[7 : 7 + n]
    lacc_ref, gacc_ref, o_ref, lk_ref, lv_ref, gk_ref, gv_ref, allk_ref, allv_ref = refs[7 + n :]
    parts, _, tokens, _ = q_ref.shape
    members, rows, _ = lacc_ref.shape
    plane = where_ref[0]
    local_far = range(n_near, local_back + 1)
    take_local(shared, plane, local_far, [blocks[d] for d in local_far], lk_ref, lv_ref)
    take_global(plane, range(n_near, n), blocks[n_near:], gk_ref, gv_ref)
    other = ((same_stretch(shared[0], plane, rows) - 1.0) * far).astype(lk_ref.dtype)

    def put(g, layer, acc):
        at = pl.multiple_of(g * HEAD, HEAD)
        out = (acc[:, :HEAD] / acc[:, HEAD:]).astype(o_ref.dtype)
        o_ref[:, layer, :, pl.ds(at, HEAD)] = out.reshape(parts, tokens, HEAD)

    def member(g, carry):
        low, high = carry
        q = jnp.concatenate([query_of(q_ref, 0, g), other], axis=1)
        put(g, 0, lacc_ref[g] + summed(q, lk_ref, lv_ref, rows, False))
        acc = gacc_ref[g] + summed(query_of(q_ref, 1, g), gk_ref, gv_ref, rows, False)
        put(g, 1, acc)
        totals = acc[:, HEAD:]
        low = jnp.minimum(low, jnp.min(totals, axis=0, keepdims=True))
        high = jnp.maximum(high, jnp.max(totals, axis=0, keepdims=True))
        return low, high

    ones = jnp.ones((1, HEAD), jnp.float32)
    low, high = lax.fori_loop(0, members, member, (ones, ones), unroll=n <= 4)
    safe = (jnp.min(low) > 2.0**-80) & (jnp.max(high) < 2.0**100)

    @pl.when(jnp.logical_not(safe))
    def _():
        take_global(plane, range(n), blocks, allk_ref, allv_ref)

        def shifted(g, carry):
            q = query_of(q_ref, 1, g)
            peak, acc = None, None
            for first in range(0, n, 4):
                group = range(first, min(n, first + 4))
                used = slice(group[0] * rows, (group[-1] + 1) * rows)
                scores = lax.dot_general(q, allk_ref[used], NT, preferred_element_type=jnp.float32)
                scores = scores * (log2e * HEAD**-0.5)
                pieces = []
                for i in group:
                    piece = scores[:, (i - first) * rows : (i - first + 1) * rows]
                    allowed = causal(rows) if i == 0 else plane >= i
                    pieces.append(jnp.where(allowed, piece, masked_score))
                scores = jnp.concatenate(pieces, axis=1)
                top = jnp.max(scores, axis=1, keepdims=True)
                new_peak = top if peak is None else jnp.maximum(peak, top)
                if acc is not None:
                    acc = acc * jnp.exp2(peak - new_peak)
                peak = new_peak
                weights = jnp.exp2(scores - peak).astype(jnp.bfloat16)
                part = jnp.dot(weights, allv_ref[used], preferred_element_type=jnp.float32)
                acc = part if acc is None else acc + part
            put(g, 1, acc)
            return carry

        lax.fori_loop(0, members, shifted, 0)


def near(*arrays):
    if sum(x.size * x.dtype.itemsize for x in arrays) > near_bytes:
        return arrays
    return tuple(pltpu.with_memory_space_constraint(x, pltpu.VMEM) for x in arrays)


def exchange(x):
    return lax.all_to_all(x, IN_PLANE, split_axis=0, concat_axis=0, tiled=True)


def upward(x, by):
    size = lax.axis_size("plane")
    return lax.ppermute(x, "plane", [(i, i + by) for i in range(size - by)])


def unpack(x):
    parts, tokens, width = x.shape
    return x.transpose(1, 0, 2).reshape(tokens, parts * width)


def shards(query_local, key_local, value_local, labels, query_global, key_global, value_global):
    planes = lax.axis_size("plane")
    plane = lax.axis_index("plane")
    parts = lax.axis_size("row") * lax.axis_size("head")
    spot = lax.axis_index("row") * lax.axis_size("head") + lax.axis_index("head")
    tokens = query_local.shape[0]
    width = query_local.shape[1] // parts
    members = width // HEAD
    rows = parts * tokens
    dtype = query_local.dtype
    local_back = min(planes - 1, -(-(STRETCH - 1) // rows))

    packed = jax.ShapeDtypeStruct((parts, 4, tokens, HEAD), dtype)
    pack = vmem_call(pack_body, packed, 4, nbytes=16 * key_local.size)
    pack = pack(key_local, value_local, key_global, value_global)
    own = exchange(pack)
    blocks = [own]
    for d in range(1, planes):
        step = 1 if d < 3 else 3
        source = blocks[d - step]
        if d > local_back:
            source = source[:, source.shape[1] - 2 :]
        blocks.append(upward(source, step))

    first = spot * tokens
    where = jnp.stack([plane, first]).astype(jnp.int32)
    bases = rope_tables(planes, rows)
    steps = rope_tables(rows, 1)
    turn = jnp.asarray(np.roll(np.eye(HEAD), HEAD // 2, axis=1), dtype)
    own_pos = plane * rows + first + jnp.arange(tokens, dtype=jnp.int32)
    temper = 1.0 + temper_slope * jnp.log(((own_pos + 1) // temper_floor + 1).astype(jnp.float32))
    temper = jnp.broadcast_to(temper[:, None], (tokens, HEAD))
    label_row = labels[None, :]
    packed = jax.ShapeDtypeStruct((parts, 2, tokens, width), dtype)
    pack = vmem_call(pack_query_body, packed, 8, nbytes=8 * query_local.size, flops=2 * HEAD * query_local.size, smem=1)
    pack = pack(where, query_local, query_global, *bases, *steps, turn, temper)
    queries = exchange(pack)

    n_near = min(2, planes)
    queries, *blocks = near(queries, *blocks)
    shared = (label_row, *bases, *steps, turn)
    sums = jax.ShapeDtypeStruct((members, rows, 2 * HEAD), jnp.float32)
    unit = 2 * 3 * rows * rows * HEAD * members

    def scratch(count, columns):
        return pltpu.VMEM((max(1, count) * rows, columns), dtype)

    early = vmem_call(
        functools.partial(early_body, n_near),
        (sums, sums),
        7 + n_near,
        flops=unit * 2 * n_near,
        nbytes=8 * rows * width,
        exps=rows * rows * members * 2 * n_near,
        scratch=[scratch(n_near, 2 * HEAD)] * 2 + [scratch(n_near, HEAD), scratch(n_near, 2 * HEAD)],
        smem=1,
        limit=vmem_bytes,
    )(where, queries, *shared, *blocks[:n_near])
    early = near(*early)
    out = vmem_call(
        functools.partial(late_body, n_near, local_back, planes),
        jax.ShapeDtypeStruct((parts, 2, tokens, width), dtype),
        7 + planes + 2,
        flops=unit * (planes + local_back + 1 - 2 * n_near),
        nbytes=8 * rows * width,
        exps=rows * rows * members * (planes + local_back + 1 - 2 * n_near),
        scratch=[scratch(local_back + 1 - n_near, 2 * HEAD)] * 2
        + [scratch(planes - n_near, HEAD), scratch(planes - n_near, 2 * HEAD)]
        + [scratch(planes, HEAD), scratch(planes, 2 * HEAD)],
        smem=1,
        limit=vmem_bytes,
    )(where, queries, *shared, *blocks, *early)
    heads = exchange(out)
    return unpack(heads[:, 0]), unpack(heads[:, 1])


def solution(mesh):
    ctx, head = mesh.shape["ctx"], mesh.shape["head"]

    def run(*args):
        key_heads = args[1].shape[1] // HEAD
        row = max(1, key_heads // head)
        grid = Mesh(mesh.devices.reshape(ctx // row, row, head), ("plane", "row", "head"))
        spread = P(("plane", "row", "head"), None)
        return jax.shard_map(
            shards,
            mesh=grid,
            in_specs=(spread, spread, spread, P(), spread, spread, spread),
            out_specs=(spread, spread),
            check_vma=False,
        )(*args)

    return run
```

time: 88.7 us -> 80.9 us (0.912)
  the two profiles are of different devices: /device:TPU:28 before, /device:TPU:0 now
where the time goes in v5:
time: 80.9 us; the launch traced here: 80.5 us
  Pallas kernels  21.3 us (26%)
  starting transfers between devices  20 us (25%)
  blocking collectives  18 us (22%)
  waiting for transfers between devices  17.4 us (22%)
  local copies, waits for them, and re-layouts  2.47 us (3%)
    all_to_all x1, blocking collectives, exchange(): return lax.all_to_all(x, IN_PLANE, split_axis=0, concat_axis=0, tiled=True)  18 us
    ppermute x3, waiting for transfers between devices, upward(): return lax.ppermute(x, 'plane', [(i, i + by) for i in range(size - by)])  13.4 us
    pallas_call x1, Pallas kernels, shards(): vmem_call(functools.partial(late_body, n_near, local_back, planes), jax.S...  12.1 us
    ppermute x3, starting transfers between devices, upward(): return lax.ppermute(x, 'plane', [(i, i + by) for i in range(size - by)])  11.2 us
    all_to_all x2, starting transfers between devices, exchange(): return lax.all_to_all(x, IN_PLANE, split_axis=0, concat_axis=0, tiled=True)  8.75 us
    pallas_call x1, Pallas kernels, shards(): vmem_call(functools.partial(early_body, n_near), (sums, sums), 7 + n_near...  4.35 us
    all_to_all x2, waiting for transfers between devices, exchange(): return lax.all_to_all(x, IN_PLANE, split_axis=0, concat_axis=0, tiled=True)  3.96 us
    pallas_call x1, Pallas kernels, shards(): pack = pack(where, query_local, query_global, *bases, *steps, turn, temper)  3.03 us
  transfers between devices with their start and end apart: 5, of which 3 were waited for; matrix products, arithmetic and copies ran while one was open for 2% of the time, Pallas kernels for 9%

profile of v5, /device:TPU:0, one launch (start us, length us, event | category | flops | bytes accessed | tf_op | source)
XLA Modules:
  0.0 80.5 jit_solution(6245275997462195137)
XLA Ops:
  0.6 1.9 %shard_map.132 = bf16[8,4,48,128]{3,2,1,0:T(8,128)(2,1)} custom-call(bf16[48,1024]{1,0:T(8,128)(2,1)} %kl_ref.1, bf16[48,1024]{1,0:T(8,128)(2,1)} %vl_ref.1, bf16[48,1024]{1,0:T(8,128)(2,1)} %kg_ref.1, bf16[48,1024]{1,0:T(8,128)(2,1)} %vg_ref.1), custom_call_target="tpu_custom_call" | custom-call | bytes 786432 | tf_op jit(solution)/shard_map/pallas_call | solution.py:270
  2.5 5.2 %all-to-all-start.1 = ((bf16[8,4,48,128]{3,2,1,0:T(8,128)(2,1)}), bf16[8,4,48,128]{3,2,1,0:T(8,128)(2,1)S(1)}, u32[]{:S(2)}, u32[]{:S(2)}) async-start(bf16[8,4,48,128]{3,2,1,0:T(8,128)(2,1)} %shard_map.132), calls=%async_computation.1 | async-start | bytes 786432 | tf_op jit(solution)/shard_map/all_to_all | solution.py:243
  7.7 0.6 pad_add_fusion.where_ref
  8.3 0.7 broadcast_in_dim.4.temper_ref
  9.0 0.0 copy-start.6
  9.0 0.0 copy-start
  9.0 0.0 copy-start.1
  9.0 0.0 copy-start.2
  9.0 0.0 copy-start.3
  9.0 0.0 copy-start.4
  9.0 0.0 copy-start.5
  9.0 3.0 %shard_map.131 = bf16[8,2,48,640]{3,2,1,0:T(8,128)(2,1)} custom-call(s32[2]{0:T(128)} %pad_add_fusion.where_ref, bf16[48,5120]{1,0:T(8,128)(2,1)} %ql_ref.1, bf16[48,5120]{1,0:T(8,128)(2,1)} %qg_ref.1, f32[4,128]{1,0:T(4,128)} %constant.49.clone.cosb_ref.refs_2_, f32[4,128]{1,0:T(4,128)} %constant.50.clone.sinb_ref.refs_3_, ...), custom_call_target="tpu_custom_call" | custom-call | flops 62914560 | bytes 1966080 | tf_op jit(solution)/shard_map/pallas_call | solution.py:291
  12.0 4.0 %all-to-all-done.1.refs_7_ = bf16[8,4,48,128]{3,2,1,0:T(8,128)(2,1)S(1)} async-done(((bf16[8,4,48,128]{3,2,1,0:T(8,128)(2,1)}), bf16[8,4,48,128]{3,2,1,0:T(8,128)(2,1)S(1)}, u32[]{:S(2)}, u32[]{:S(2)}) %all-to-all-start.1) | async-done | bytes 393248 | tf_op jit(solution)/shard_map/all_to_all | solution.py:243
  16.0 3.6 %all-to-all-start = ((bf16[8,2,48,640]{3,2,1,0:T(8,128)(2,1)}), bf16[8,2,48,640]{3,2,1,0:T(8,128)(2,1)S(1)}, u32[]{:S(2)}, u32[]{:S(2)}) async-start(bf16[8,2,48,640]{3,2,1,0:T(8,128)(2,1)} %shard_map.131), calls=%async_computation | async-start | bytes 1966080 | tf_op jit(solution)/shard_map/all_to_all | solution.py:243
  19.6 3.5 %collective-permute-start = (bf16[8,4,48,128]{3,2,1,0:T(8,128)(2,1)S(1)}, bf16[8,4,48,128]{3,2,1,0:T(8,128)(2,1)S(1)}, u32[]{:S(2)}, u32[]{:S(2)}) collective-permute-start(bf16[8,4,48,128]{3,2,1,0:T(8,128)(2,1)S(1)} %all-to-all-done.1.refs_7_), channel_id=1, source_target_pairs={{0,8},{8,16},{16,24},{1,9},{9,17},{17,25},{2,10},{10,18},{18,26},{... | collective-permute-start | bytes 1179656 | tf_op jit(solution)/shard_map/ppermute | solution.py:248
  23.1 8.9 %collective-permute-done.refs_8_ = bf16[8,4,48,128]{3,2,1,0:T(8,128)(2,1)S(1)} collective-permute-done((bf16[8,4,48,128]{3,2,1,0:T(8,128)(2,1)S(1)}, bf16[8,4,48,128]{3,2,1,0:T(8,128)(2,1)S(1)}, u32[]{:S(2)}, u32[]{:S(2)}) %collective-permute-start) | collective-permute-done | bytes 393248 | tf_op jit(solution)/shard_map/ppermute | solution.py:248
  32.0 4.4 %collective-permute-start.1 = (bf16[8,4,48,128]{3,2,1,0:T(8,128)(2,1)S(1)}, bf16[8,4,48,128]{3,2,1,0:T(8,128)(2,1)S(1)}, u32[]{:S(2)}, u32[]{:S(2)}) collective-permute-start(bf16[8,4,48,128]{3,2,1,0:T(8,128)(2,1)S(1)} %collective-permute-done.refs_8_), channel_id=1, source_target_pairs={{0,8},{8,16},{16,24},{1,9},{9,17},{17,25},{2,10},{10,18},{18,26},{... | collective-permute-start | bytes 1179656 | tf_op jit(solution)/shard_map/ppermute | solution.py:248
  36.4 0.0 copy-done.6
  36.4 3.3 %collective-permute-start.2 = (bf16[8,2,48,128]{3,2,1,0:T(8,128)(2,1)S(1)}, bf16[8,2,48,128]{3,2,1,0:T(8,128)(2,1)S(1)}, u32[]{:S(2)}, u32[]{:S(2)}) collective-permute-start(bf16[8,2,48,128]{3,2,1,0:T(8,128)(2,1)S(1)} %slice.12), channel_id=1, source_target_pairs={{0,24},{1,25},{2,26},{3,27},{4,28},{5,29},{6,30},{7,31}} | collective-permute-start | bytes 589832 | tf_op jit(solution)/shard_map/ppermute | solution.py:248
  39.7 0.0 all-to-all-done.refs_0_
  39.7 0.0 copy-done
  39.7 0.0 copy-done.1
  39.8 0.0 copy-done.2
  39.8 0.0 copy-done.3
  39.8 0.0 copy-done.4
  39.8 0.0 copy-done.5
  39.8 4.3 %shard_map.133 = (f32[5,384,256]{2,1,0:T(8,128)S(1)}, f32[5,384,256]{2,1,0:T(8,128)S(1)}) custom-call(s32[2]{0:T(128)S(1)} %copy-done.5, bf16[8,2,48,640]{3,2,1,0:T(8,128)(2,1)S(1)} %all-to-all-done.refs_0_, s32[1,1536]{1,0:T(1,128)S(1)} %broadcast_in_dim.10.refs_1_, f32[4,128]{1,0:T(4,128)S(1)} %copy-done.4, f32[4,128]{1,0:T(4,128)S(1)} %copy-done.3, ...), custom_call_target="tpu_custom_call" | custom-call | flops 2264924160 | bytes 1966080 | tf_op jit(solution)/shard_map/pallas_call | solution.py:303
  44.1 4.5 %collective-permute-done.2.refs_10_ = bf16[8,2,48,128]{3,2,1,0:T(8,128)(2,1)S(1)} collective-permute-done((bf16[8,2,48,128]{3,2,1,0:T(8,128)(2,1)S(1)}, bf16[8,2,48,128]{3,2,1,0:T(8,128)(2,1)S(1)}, u32[]{:S(2)}, u32[]{:S(2)}) %collective-permute-start.2) | collective-permute-done | bytes 196640 | tf_op jit(solution)/shard_map/ppermute | solution.py:248
  48.7 0.0 collective-permute-done.1.refs_9_
  48.7 12.1 %shard_map.134 = bf16[8,2,48,640]{3,2,1,0:T(8,128)(2,1)S(1)} custom-call(s32[2]{0:T(128)S(1)} %copy-done.5, bf16[8,2,48,640]{3,2,1,0:T(8,128)(2,1)S(1)} %all-to-all-done.refs_0_, s32[1,1536]{1,0:T(1,128)S(1)} %broadcast_in_dim.10.refs_1_, f32[4,128]{1,0:T(4,128)S(1)} %copy-done.4, f32[4,128]{1,0:T(4,128)S(1)} %copy-done.3, f32[384,128]{1,0:T(8,128)S(1)} %copy-done.1, ...), custom_call_target="tpu_custom_call" | custom-call | flops 1698693120 | bytes 1966080 | tf_op jit(solution)/shard_map/pallas_call | solution.py:315
  60.8 18.0 %all_to_all.15 = bf16[8,2,48,640]{3,2,1,0:T(8,128)(2,1)S(1)} all-to-all(bf16[8,2,48,640]{3,2,1,0:T(8,128)(2,1)S(1)} %shard_map.134), channel_id=1, replica_groups=mesh['plane'=4,'row'=2,'head'=4] {'row','head'}, dimensions={0} | all-to-all | bytes 1966080 | tf_op jit(solution)/shard_map/all_to_all | solution.py:243
  78.8 0.1 slice_bitcast_fusion
  78.8 0.8 %copy.17 = bf16[8,6,8,640]{3,2,0,1:T(8,128)(2,1)} copy(bf16[8,6,8,640]{3,2,1,0:T(8,128)(2,1)S(1)} %get-tuple-element.6) | data formatting | bytes 983040 | tf_op jit(solution)/shard_map/reshape | solution.py:253
  79.7 0.8 %copy.16 = bf16[8,6,8,640]{3,2,0,1:T(8,128)(2,1)} copy(bf16[8,6,8,640]{3,2,1,0:T(8,128)(2,1)S(1)} %get-tuple-element.7) | data formatting | bytes 983040 | tf_op jit(solution)/shard_map/reshape | solution.py:253
  (3 shorter events, 0.0 us)
Async XLA Ops:
  2.5 13.5 %all-to-all-start.1 = ((bf16[8,4,48,128]{3,2,1,0:T(8,128)(2,1)}), bf16[8,4,48,128]{3,2,1,0:T(8,128)(2,1)S(1)}, u32[]{:S(2)}, u32[]{:S(2)}) async-start(bf16[8,4,48,128]{3,2,1,0:T(8,128)(2,1)} %shard_map.132), calls=%async_computation.1 | async-start | bytes 786432 | tf_op jit(solution)/shard_map/all_to_all | solution.py:243
  9.0 27.4 %copy-start.6 = (s32[1536]{0:T(1024)S(1)}, s32[1536]{0:T(1024)}, u32[]{:S(2)}) copy-start(s32[1536]{0:T(1024)} %param.15) | copy-start | bytes 18436
  9.0 30.8 %copy-start = (f32[384,128]{1,0:T(8,128)S(1)}, f32[384,128]{1,0:T(8,128)}, u32[]{:S(2)}) copy-start(f32[384,128]{1,0:T(8,128)} %constant.52.clone.sinr_ref.refs_5_) | copy-start | bytes 589828
  9.0 30.8 %copy-start.1 = (f32[384,128]{1,0:T(8,128)S(1)}, f32[384,128]{1,0:T(8,128)}, u32[]{:S(2)}) copy-start(f32[384,128]{1,0:T(8,128)} %constant.51.clone.cosr_ref.refs_4_) | copy-start | bytes 589828
  9.0 30.8 %copy-start.2 = (bf16[128,128]{1,0:T(8,128)(2,1)S(1)}, bf16[128,128]{1,0:T(8,128)(2,1)}, u32[]{:S(2)}) copy-start(bf16[128,128]{1,0:T(8,128)(2,1)} %constant.53.clone.turn_ref.refs_6_) | copy-start | bytes 98308
  9.0 30.8 %copy-start.3 = (f32[4,128]{1,0:T(4,128)S(1)}, f32[4,128]{1,0:T(4,128)}, u32[]{:S(2)}) copy-start(f32[4,128]{1,0:T(4,128)} %constant.50.clone.sinb_ref.refs_3_) | copy-start | bytes 6148
  9.0 30.8 %copy-start.4 = (f32[4,128]{1,0:T(4,128)S(1)}, f32[4,128]{1,0:T(4,128)}, u32[]{:S(2)}) copy-start(f32[4,128]{1,0:T(4,128)} %constant.49.clone.cosb_ref.refs_2_) | copy-start | bytes 6148
  9.0 30.8 %copy-start.5 = (s32[2]{0:T(128)S(1)}, s32[2]{0:T(128)}, u32[]{:S(2)}) copy-start(s32[2]{0:T(128)} %pad_add_fusion.where_ref) | copy-start | bytes 28
  16.0 23.7 %all-to-all-start = ((bf16[8,2,48,640]{3,2,1,0:T(8,128)(2,1)}), bf16[8,2,48,640]{3,2,1,0:T(8,128)(2,1)S(1)}, u32[]{:S(2)}, u32[]{:S(2)}) async-start(bf16[8,2,48,640]{3,2,1,0:T(8,128)(2,1)} %shard_map.131), calls=%async_computation | async-start | bytes 1966080 | tf_op jit(solution)/shard_map/all_to_all | solution.py:243
  19.6 12.4 %collective-permute-start = (bf16[8,4,48,128]{3,2,1,0:T(8,128)(2,1)S(1)}, bf16[8,4,48,128]{3,2,1,0:T(8,128)(2,1)S(1)}, u32[]{:S(2)}, u32[]{:S(2)}) collective-permute-start(bf16[8,4,48,128]{3,2,1,0:T(8,128)(2,1)S(1)} %all-to-all-done.1.refs_7_), channel_id=1, source_target_pairs={{0,8},{8,16},{16,24},{1,9},{9,17},{17,25},{2,10},{10,18},{18,26},{... | collective-permute-start | bytes 1179656 | tf_op jit(solution)/shard_map/ppermute | solution.py:248
  32.0 16.7 %collective-permute-start.1 = (bf16[8,4,48,128]{3,2,1,0:T(8,128)(2,1)S(1)}, bf16[8,4,48,128]{3,2,1,0:T(8,128)(2,1)S(1)}, u32[]{:S(2)}, u32[]{:S(2)}) collective-permute-start(bf16[8,4,48,128]{3,2,1,0:T(8,128)(2,1)S(1)} %collective-permute-done.refs_8_), channel_id=1, source_target_pairs={{0,8},{8,16},{16,24},{1,9},{9,17},{17,25},{2,10},{10,18},{18,26},{... | collective-permute-start | bytes 1179656 | tf_op jit(solution)/shard_map/ppermute | solution.py:248
  36.4 12.2 %collective-permute-start.2 = (bf16[8,2,48,128]{3,2,1,0:T(8,128)(2,1)S(1)}, bf16[8,2,48,128]{3,2,1,0:T(8,128)(2,1)S(1)}, u32[]{:S(2)}, u32[]{:S(2)}) collective-permute-start(bf16[8,2,48,128]{3,2,1,0:T(8,128)(2,1)S(1)} %slice.12), channel_id=1, source_target_pairs={{0,24},{1,25},{2,26},{3,27},{4,28},{5,29},{6,30},{7,31}} | collective-permute-start | bytes 589832 | tf_op jit(solution)/shard_map/ppermute | solution.py:248

commit v6 on v5

--- a/solution.py
+++ b/solution.py
@@ -20,7 +20,7 @@
 masked_score = -1e30
 log2e = 1.4426950408889634
 far = 30000.0
-near_bytes = 5 << 20
+near_bytes = 6 << 20
 vmem_bytes = 40 << 20
 
 IN_PLANE = ("row", "head")
@@ -42,6 +42,14 @@
     swapped = jnp.dot(x, turn, preferred_element_type=jnp.float32)
     y = x.astype(jnp.float32) * cosine + swapped * sine
     return y * lax.rsqrt(jnp.mean(y * y, axis=-1, keepdims=True) + norm_epsilon)
+
+
+def spot_of():
+    return lax.axis_index("row") * lax.axis_size("head") + lax.axis_index("head")
+
+
+def partner_orders(parts):
+    return sorted(range(1, parts), key=lambda s: (s & 1, -s)) if parts > 1 else []
 
 
 def vmem_call(body, out_shapes, n_in, flops=0, nbytes=0, exps=0, scratch=(), smem=0, limit=None):
@@ -63,21 +71,19 @@
             o_ref[d, a] = ref[:, d * HEAD : (d + 1) * HEAD]
 
 
-def pack_query_body(where_ref, ql_ref, qg_ref, cosb_ref, sinb_ref, cosr_ref, sinr_ref, turn_ref, temper_ref, o_ref):
-    members = o_ref.shape[3] // HEAD
-    tokens = ql_ref.shape[0]
-    plane, first = where_ref[0], pl.multiple_of(where_ref[1], 16)
-    mine = pl.ds(first, tokens)
-    cosine, sine = turned(cosb_ref[pl.ds(plane, 1)], sinb_ref[pl.ds(plane, 1)], cosr_ref[mine], sinr_ref[mine])
+def pack_query_body(ql_ref, qg_ref, cosb_ref, sinb_ref, cosr_ref, sinr_ref, turn_ref, temper_ref, *o_refs):
+    tokens, width = ql_ref.shape[0], o_refs[0].shape[2]
+    spot = spot_of()
+    base, mine = pl.ds(lax.axis_index("plane"), 1), pl.ds(pl.multiple_of(spot * tokens, 16), tokens)
+    cosine, sine = turned(cosb_ref[base], sinb_ref[base], cosr_ref[mine], sinr_ref[mine])
     turn = turn_ref[...]
-    for d in range(o_ref.shape[0]):
-        for g in range(members):
-            at = (d * members + g) * HEAD
-            to = slice(g * HEAD, (g + 1) * HEAD)
-            y = rotated_unit(ql_ref[:, at : at + HEAD], turn, cosine, sine)
-            o_ref[d, 0, :, to] = y.astype(o_ref.dtype)
-            z = qg_ref[:, at : at + HEAD].astype(jnp.float32) * temper_ref[...]
-            o_ref[d, 1, :, to] = z.astype(o_ref.dtype)
+    for s, o_ref in enumerate(o_refs):
+        to = lax.bitwise_xor(spot, s)
+        for g in range(width // HEAD):
+            at = pl.ds(pl.multiple_of(to * width + g * HEAD, HEAD), HEAD)
+            out = slice(g * HEAD, (g + 1) * HEAD)
+            o_ref[0, :, out] = rotated_unit(ql_ref[:, at], turn, cosine, sine).astype(o_ref.dtype)
+            o_ref[1, :, out] = (qg_ref[:, at].astype(jnp.float32) * temper_ref[...]).astype(o_ref.dtype)
 
 
 def causal(rows):
@@ -132,9 +138,7 @@
 
 
 def query_of(q_ref, layer, g):
-    parts, _, tokens, _ = q_ref.shape
-    at = pl.multiple_of(g * HEAD, HEAD)
-    return q_ref[:, layer, :, pl.ds(at, HEAD)].reshape(parts * tokens, HEAD)
+    return q_ref[layer, :, pl.ds(pl.multiple_of(g * HEAD, HEAD), HEAD)]
 
 
 def summed(q, k_ref, v_ref, rows, own):
@@ -150,12 +154,17 @@
     return acc
 
 
-def early_body(n_near, where_ref, *refs):
-    q_ref, *shared = refs[:7]
-    blocks = refs[7 : 7 + n_near]
-    lacc_ref, gacc_ref, lk_ref, lv_ref, gk_ref, gv_ref = refs[7 + n_near :]
+def early_body(n_near, *refs):
+    shared, refs = refs[:6], refs[6:]
+    parts = refs[0].shape[0]
+    queries, blocks, refs = refs[n_near : n_near + parts], refs[:n_near], refs[n_near + parts :]
+    q_ref, lacc_ref, gacc_ref, lk_ref, lv_ref, gk_ref, gv_ref = refs
     members, rows, _ = lacc_ref.shape
-    plane = where_ref[0]
+    tokens = rows // parts
+    plane, spot = lax.axis_index("plane"), spot_of()
+    for s, ref in enumerate(queries):
+        at = pl.ds(pl.multiple_of(lax.bitwise_xor(spot, s) * tokens, 16), tokens)
+        q_ref[:, at] = ref[...]
     take_local(shared, plane, range(n_near), blocks, lk_ref, lv_ref)
     take_global(plane, range(n_near), blocks, gk_ref, gv_ref)
     other = ((same_stretch(shared[0], plane, rows) - 1.0) * far).astype(lk_ref.dtype)
@@ -169,13 +178,16 @@
     lax.fori_loop(0, members, member, 0, unroll=True)
 
 
-def late_body(n_near, local_back, n, where_ref, *refs):
-    q_ref, *shared = refs[:7]
-    blocks = refs[7 : 7 + n]
-    lacc_ref, gacc_ref, o_ref, lk_ref, lv_ref, gk_ref, gv_ref, allk_ref, allv_ref = refs[7 + n :]
-    parts, _, tokens, _ = q_ref.shape
+def late_body(n_near, local_back, n, *refs):
+    shared, refs = refs[:6], refs[6:]
+    blocks, refs = refs[:n], refs[n:]
+    parts = blocks[0].shape[0]
+    q_ref, lacc_ref, gacc_ref = refs[:3]
+    o_refs, refs = refs[3 : 3 + parts], refs[3 + parts :]
+    out_ref, lk_ref, lv_ref, gk_ref, gv_ref, allk_ref, allv_ref = refs
     members, rows, _ = lacc_ref.shape
-    plane = where_ref[0]
+    tokens = rows // parts
+    plane, spot = lax.axis_index("plane"), spot_of()
     local_far = range(n_near, local_back + 1)
     take_local(shared, plane, local_far, [blocks[d] for d in local_far], lk_ref, lv_ref)
     take_global(plane, range(n_near, n), blocks[n_near:], gk_ref, gv_ref)
@@ -183,8 +195,7 @@
 
     def put(g, layer, acc):
         at = pl.multiple_of(g * HEAD, HEAD)
-        out = (acc[:, :HEAD] / acc[:, HEAD:]).astype(o_ref.dtype)
-        o_ref[:, layer, :, pl.ds(at, HEAD)] = out.reshape(parts, tokens, HEAD)
+        out_ref[layer, :, pl.ds(at, HEAD)] = (acc[:, :HEAD] / acc[:, HEAD:]).astype(out_ref.dtype)
 
     def member(g, carry):
         low, high = carry
@@ -232,6 +243,10 @@
 
         lax.fori_loop(0, members, shifted, 0)
 
+    for s, o_ref in enumerate(o_refs):
+        at = pl.ds(pl.multiple_of(lax.bitwise_xor(spot, s) * tokens, 16), tokens)
+        o_ref[...] = out_ref[:, at]
+
 
 def near(*arrays):
     if sum(x.size * x.dtype.itemsize for x in arrays) > near_bytes:
@@ -248,9 +263,41 @@
     return lax.ppermute(x, "plane", [(i, i + by) for i in range(size - by)])
 
 
-def unpack(x):
-    parts, tokens, width = x.shape
-    return x.transpose(1, 0, 2).reshape(tokens, parts * width)
+def unpack_body(parts, *refs):
+    x_refs, o_refs, sems = refs[:parts], refs[parts:-1], refs[-1]
+    width = x_refs[0].shape[2]
+    spot = spot_of()
+    copies = []
+    for s, x_ref in enumerate(x_refs):
+        at = pl.ds(pl.multiple_of(lax.bitwise_xor(spot, s) * width, HEAD), width)
+        for layer, o_ref in enumerate(o_refs):
+            copies.append(pltpu.make_async_copy(x_ref.at[layer], o_ref.at[:, at], sems.at[s, layer]))
+    for copy in copies:
+        copy.start()
+    for copy in copies:
+        copy.wait()
+
+
+def unpack(pieces):
+    parts = len(pieces)
+    layers, tokens, width = pieces[0].shape
+    shape = jax.ShapeDtypeStruct((tokens, parts * width), pieces[0].dtype)
+    return pl.pallas_call(
+        functools.partial(unpack_body, parts),
+        out_shape=(shape,) * layers,
+        in_specs=[pl.BlockSpec(memory_space=pltpu.VMEM)] * parts,
+        out_specs=(pl.BlockSpec(memory_space=pl.ANY),) * layers,
+        scratch_shapes=[pltpu.SemaphoreType.DMA((parts, layers))],
+        cost_estimate=pl.CostEstimate(flops=0, bytes_accessed=4 * parts * pieces[0].size, transcendentals=0),
+    )(*pieces)
+
+
+def swapped(pieces):
+    parts = len(pieces)
+    came = [pieces[0]] * parts
+    for s in partner_orders(parts):
+        came[s] = lax.ppermute(pieces[s], IN_PLANE, [(i, i ^ s) for i in range(parts)])
+    return came
 
 
 def shards(query_local, key_local, value_local, labels, query_global, key_global, value_global):
@@ -277,23 +324,25 @@
             source = source[:, source.shape[1] - 2 :]
         blocks.append(upward(source, step))
 
-    first = spot * tokens
-    where = jnp.stack([plane, first]).astype(jnp.int32)
     bases = rope_tables(planes, rows)
     steps = rope_tables(rows, 1)
     turn = jnp.asarray(np.roll(np.eye(HEAD), HEAD // 2, axis=1), dtype)
-    own_pos = plane * rows + first + jnp.arange(tokens, dtype=jnp.int32)
+    own_pos = plane * rows + spot * tokens + jnp.arange(tokens, dtype=jnp.int32)
     temper = 1.0 + temper_slope * jnp.log(((own_pos + 1) // temper_floor + 1).astype(jnp.float32))
     temper = jnp.broadcast_to(temper[:, None], (tokens, HEAD))
     label_row = labels[None, :]
-    packed = jax.ShapeDtypeStruct((parts, 2, tokens, width), dtype)
-    pack = vmem_call(pack_query_body, packed, 8, nbytes=8 * query_local.size, flops=2 * HEAD * query_local.size, smem=1)
-    pack = pack(where, query_local, query_global, *bases, *steps, turn, temper)
-    queries = exchange(pack)
+    piece = jax.ShapeDtypeStruct((2, tokens, width), dtype)
+    pack = vmem_call(
+        pack_query_body, (piece,) * parts, 8, nbytes=8 * query_local.size, flops=2 * HEAD * query_local.size
+    )
+    queries = pack(query_local, query_global, *bases, *steps, turn, temper)
+    queries = swapped(queries)
 
     n_near = min(2, planes)
-    queries, *blocks = near(queries, *blocks)
+    kept = near(*queries[1:], *blocks)
+    queries, blocks = (queries[0], *kept[: parts - 1]), kept[parts - 1 :]
     shared = (label_row, *bases, *steps, turn)
+    placed = jax.ShapeDtypeStruct((2, rows, width), dtype)
     sums = jax.ShapeDtypeStruct((members, rows, 2 * HEAD), jnp.float32)
     unit = 2 * 3 * rows * rows * HEAD * members
 
@@ -302,31 +351,29 @@
 
     early = vmem_call(
         functools.partial(early_body, n_near),
-        (sums, sums),
-        7 + n_near,
+        (placed, sums, sums),
+        6 + n_near + parts,
         flops=unit * 2 * n_near,
         nbytes=8 * rows * width,
         exps=rows * rows * members * 2 * n_near,
         scratch=[scratch(n_near, 2 * HEAD)] * 2 + [scratch(n_near, HEAD), scratch(n_near, 2 * HEAD)],
-        smem=1,
         limit=vmem_bytes,
-    )(where, queries, *shared, *blocks[:n_near])
+    )(*shared, *blocks[:n_near], *queries)
     early = near(*early)
     out = vmem_call(
         functools.partial(late_body, n_near, local_back, planes),
-        jax.ShapeDtypeStruct((parts, 2, tokens, width), dtype),
-        7 + planes + 2,
+        (piece,) * parts,
+        6 + planes + 3,
         flops=unit * (planes + local_back + 1 - 2 * n_near),
         nbytes=8 * rows * width,
         exps=rows * rows * members * (planes + local_back + 1 - 2 * n_near),
-        scratch=[scratch(local_back + 1 - n_near, 2 * HEAD)] * 2
+        scratch=[pltpu.VMEM((2, rows, width), dtype)]
+        + [scratch(local_back + 1 - n_near, 2 * HEAD)] * 2
         + [scratch(planes - n_near, HEAD), scratch(planes - n_near, 2 * HEAD)]
         + [scratch(planes, HEAD), scratch(planes, 2 * HEAD)],
-        smem=1,
         limit=vmem_bytes,
-    )(where, queries, *shared, *blocks, *early)
-    heads = exchange(out)
-    return unpack(heads[:, 0]), unpack(heads[:, 1])
+    )(*shared, *blocks, *early)
+    return unpack(near(*swapped(out)))
 
 
 def solution(mesh):

time: 80.9 us -> 79.9 us (0.988)
  blocking collectives: 18 us -> 13.5 us
  waiting for transfers between devices: 17.4 us -> 20.6 us
  starting transfers between devices: 20 us -> 21.6 us
  local copies, waits for them, and re-layouts: 2.47 us -> 1.65 us
    ppermute x0 -> x14, waiting for transfers between devices: none -> 17.9 us  [swapped(): lax.ppermute(pieces[s], IN_PLANE, [(i, i ^ s) for i in range(parts)])]
    ppermute x3, waiting for transfers between devices: 13.4 us -> 2.63 us  [upward(): return lax.ppermute(x, 'plane', [(i, i + by) for i in range(size - by)])]
    ppermute x0 -> x14, starting transfers between devices: none -> 10.4 us  [swapped(): lax.ppermute(pieces[s], IN_PLANE, [(i, i ^ s) for i in range(parts)])]
    all_to_all x2 -> x0, starting transfers between devices: 8.75 us -> none  [exchange(): return lax.all_to_all(x, IN_PLANE, split_axis=0, concat_axis=0, tiled=True)]
    all_to_all x1, blocking collectives: 18 us -> 13.5 us  [exchange(): return lax.all_to_all(x, IN_PLANE, split_axis=0, concat_axis=0, tiled=True)]
    all_to_all x2 -> x0, waiting for transfers between devices: 3.96 us -> none  [exchange(): return lax.all_to_all(x, IN_PLANE, split_axis=0, concat_axis=0, tiled=True)]
    reshape x2 -> x0, local copies, waits for them, and re-layouts: 1.65 us -> none  [unpack(): return x.transpose(1, 0, 2).reshape(tokens, parts * width)]
    unnamed x15 -> x14, local copies, waits for them, and re-layouts: 0.12 us -> 0.94 us
  transfers between devices with their start and end apart: 5 -> 17, of which waited for: 3 -> 6; matrix products, arithmetic and copies ran while one was open for 2% -> 1% of each run, Pallas kernels for 9% -> 8%
where the time goes in v6:
time: 79.9 us; the launch traced here: 79.5 us
  starting transfers between devices  21.6 us (27%)
  Pallas kernels  21.4 us (27%)
  waiting for transfers between devices  20.6 us (26%)
  blocking collectives  13.5 us (17%)
  local copies, waits for them, and re-layouts  1.65 us (2%)
  between operations  0.85 us (1%)
    ppermute x14, waiting for transfers between devices, swapped(): lax.ppermute(pieces[s], IN_PLANE, [(i, i ^ s) for i in range(parts)])  17.9 us
    all_to_all x1, blocking collectives, exchange(): return lax.all_to_all(x, IN_PLANE, split_axis=0, concat_axis=0, tiled=True)  13.5 us
    pallas_call x1, Pallas kernels, shards(): vmem_call(functools.partial(late_body, n_near, local_back, planes), (piec...  11.7 us
    ppermute x3, starting transfers between devices, upward(): return lax.ppermute(x, 'plane', [(i, i + by) for i in range(size - by)])  11.2 us
    ppermute x14, starting transfers between devices, swapped(): lax.ppermute(pieces[s], IN_PLANE, [(i, i ^ s) for i in range(parts)])  10.4 us
    pallas_call x1, Pallas kernels, shards(): vmem_call(functools.partial(early_body, n_near), (placed, sums, sums), 6...  3.86 us
    pallas_call x1, Pallas kernels, shards(): queries = pack(query_local, query_global, *bases, *steps, turn, temper)  2.82 us
    ppermute x3, waiting for transfers between devices, upward(): return lax.ppermute(x, 'plane', [(i, i + by) for i in range(size - by)])  2.63 us
  transfers between devices with their start and end apart: 17, of which 6 were waited for; matrix products, arithmetic and copies ran while one was open for 1% of the time, Pallas kernels for 8%

profile of v6, /device:TPU:0, one launch (start us, length us, event | category | flops | bytes accessed | tf_op | source)
XLA Modules:
  0.0 79.5 jit_solution(14730758563822067206)
XLA Ops:
  0.6 0.0 copy-start.2
  0.6 0.0 copy-start
  0.7 0.0 copy-start.1
  0.7 0.0 copy-start.3
  0.7 0.0 copy-start.4
  0.7 0.0 copy-start.6
  0.7 1.9 %shard_map.131 = bf16[8,4,48,128]{3,2,1,0:T(8,128)(2,1)} custom-call(bf16[48,1024]{1,0:T(8,128)(2,1)} %kl_ref.1, bf16[48,1024]{1,0:T(8,128)(2,1)} %vl_ref.1, bf16[48,1024]{1,0:T(8,128)(2,1)} %kg_ref.1, bf16[48,1024]{1,0:T(8,128)(2,1)} %vg_ref.1), custom_call_target="tpu_custom_call" | custom-call | bytes 786432 | tf_op jit(solution)/shard_map/pallas_call | solution.py:317
  2.6 13.5 %all_to_all.5.refs_6_ = bf16[8,4,48,128]{3,2,1,0:T(8,128)(2,1)S(1)} all-to-all(bf16[8,4,48,128]{3,2,1,0:T(8,128)(2,1)} %shard_map.131), channel_id=1, replica_groups=mesh['plane'=4,'row'=2,'head'=4] {'row','head'}, dimensions={0} | all-to-all | bytes 786432 | tf_op jit(solution)/shard_map/all_to_all | solution.py:258
  16.2 3.5 %collective-permute-start = (bf16[8,4,48,128]{3,2,1,0:T(8,128)(2,1)S(1)}, bf16[8,4,48,128]{3,2,1,0:T(8,128)(2,1)S(1)}, u32[]{:S(2)}, u32[]{:S(2)}) collective-permute-start(bf16[8,4,48,128]{3,2,1,0:T(8,128)(2,1)S(1)} %all_to_all.5.refs_6_), channel_id=1, source_target_pairs={{0,8},{8,16},{16,24},{1,9},{9,17},{17,25},{2,10},{10,18},{18,26},{... | collective-permute-start | bytes 1179656 | tf_op jit(solution)/shard_map/ppermute | solution.py:263
  19.7 0.7 broadcast_in_dim.10.temper_ref
  20.4 2.8 %shard_map.132 = (bf16[2,48,640]{2,1,0:T(8,128)(2,1)}, bf16[2,48,640]{2,1,0:T(8,128)(2,1)}, bf16[2,48,640]{2,1,0:T(8,128)(2,1)}, bf16[2,48,640]{2,1,0:T(8,128)(2...) custom-call(bf16[48,5120]{1,0:T(8,128)(2,1)} %ql_ref.1, ...), custom_call_target="tpu_custom_call" | custom-call | flops 62914560 | bytes 1966080 | tf_op jit(solution)/shard_map/pallas_call | solution.py:338
  23.2 0.0 collective-permute-start.3
  23.2 0.6 collective-permute-start.4
  23.8 1.2 %collective-permute-start.5 = (bf16[2,48,640]{2,1,0:T(8,128)(2,1)}, bf16[2,48,640]{2,1,0:T(8,128)(2,1)S(1)}, u32[]{:S(2)}, u32[]{:S(2)}) collective-permute-start(bf16[2,48,640]{2,1,0:T(8,128)(2,1)} %get-tuple-element.24), channel_id=1, source_target_pairs={{0,3},{1,2},{2,1},{3,0},{4,7},{5,6},{6,5},{7,4},{8,11},{9,10},{10,... | collective-permute-start | bytes 368648 | tf_op jit(solution)/shard_map/ppermute | solution.py:299
  25.1 2.6 %collective-permute-done.refs_7_ = bf16[8,4,48,128]{3,2,1,0:T(8,128)(2,1)S(1)} collective-permute-done((bf16[8,4,48,128]{3,2,1,0:T(8,128)(2,1)S(1)}, bf16[8,4,48,128]{3,2,1,0:T(8,128)(2,1)S(1)}, u32[]{:S(2)}, u32[]{:S(2)}) %collective-permute-start) | collective-permute-done | bytes 393248 | tf_op jit(solution)/shard_map/ppermute | solution.py:263
  27.7 4.4 %collective-permute-start.1 = (bf16[8,4,48,128]{3,2,1,0:T(8,128)(2,1)S(1)}, bf16[8,4,48,128]{3,2,1,0:T(8,128)(2,1)S(1)}, u32[]{:S(2)}, u32[]{:S(2)}) collective-permute-start(bf16[8,4,48,128]{3,2,1,0:T(8,128)(2,1)S(1)} %collective-permute-done.refs_7_), channel_id=1, source_target_pairs={{0,8},{8,16},{16,24},{1,9},{9,17},{17,25},{2,10},{10,18},{18,26},{... | collective-permute-start | bytes 1179656 | tf_op jit(solution)/shard_map/ppermute | solution.py:263
  32.1 0.6 collective-permute-start.6
  32.7 0.0 collective-permute-done.3.refs_9_
  32.7 0.0 collective-permute-start.7
  32.7 0.0 collective-permute-done.4.refs_10_
  32.7 1.8 %collective-permute-start.8 = (bf16[2,48,640]{2,1,0:T(8,128)(2,1)}, bf16[2,48,640]{2,1,0:T(8,128)(2,1)S(1)}, u32[]{:S(2)}, u32[]{:S(2)}) collective-permute-start(bf16[2,48,640]{2,1,0:T(8,128)(2,1)} %get-tuple-element.27), channel_id=1, source_target_pairs={{0,6},{1,7},{2,4},{3,5},{4,2},{5,3},{6,0},{7,1},{8,14},{9,15},{10,... | collective-permute-start | bytes 368648 | tf_op jit(solution)/shard_map/ppermute | solution.py:299
  34.5 0.0 collective-permute-done.5.refs_11_
  34.5 2.1 %collective-permute-start.9 = (bf16[2,48,640]{2,1,0:T(8,128)(2,1)}, bf16[2,48,640]{2,1,0:T(8,128)(2,1)S(1)}, u32[]{:S(2)}, u32[]{:S(2)}) collective-permute-start(bf16[2,48,640]{2,1,0:T(8,128)(2,1)} %get-tuple-element.28), channel_id=1, source_target_pairs={{0,7},{1,6},{2,5},{3,4},{4,3},{5,2},{6,1},{7,0},{8,15},{9,14},{10,... | collective-permute-start | bytes 368648 | tf_op jit(solution)/shard_map/ppermute | solution.py:299
  36.6 0.0 copy-done.6
  36.6 7.2 %collective-permute-done.6.refs_12_ = bf16[2,48,640]{2,1,0:T(8,128)(2,1)S(1)} collective-permute-done((bf16[2,48,640]{2,1,0:T(8,128)(2,1)}, bf16[2,48,640]{2,1,0:T(8,128)(2,1)S(1)}, u32[]{:S(2)}, u32[]{:S(2)}) %collective-permute-start.6) | collective-permute-done | bytes 122912 | tf_op jit(solution)/shard_map/ppermute | solution.py:299
  43.8 3.3 %collective-permute-start.2 = (bf16[8,2,48,128]{3,2,1,0:T(8,128)(2,1)S(1)}, bf16[8,2,48,128]{3,2,1,0:T(8,128)(2,1)S(1)}, u32[]{:S(2)}, u32[]{:S(2)}) collective-permute-start(bf16[8,2,48,128]{3,2,1,0:T(8,128)(2,1)S(1)} %slice.4), channel_id=1, source_target_pairs={{0,24},{1,25},{2,26},{3,27},{4,28},{5,29},{6,30},{7,31}} | collective-permute-start | bytes 589832 | tf_op jit(solution)/shard_map/ppermute | solution.py:263
  47.1 0.0 collective-permute-done.7.refs_13_
  47.1 0.0 collective-permute-done.8.refs_14_
  47.1 0.0 collective-permute-done.9.refs_15_
  47.2 0.0 copy-done.2
  47.2 0.0 copy-done
  47.2 0.0 copy-done.1
  47.2 0.0 copy-done.3
  47.2 0.0 copy-done.4
  47.2 0.0 copy-start.5
  47.2 0.9 %copy-done.5 = bf16[2,48,640]{2,1,0:T(8,128)(2,1)S(1)} copy-done((bf16[2,48,640]{2,1,0:T(8,128)(2,1)S(1)}, bf16[2,48,640]{2,1,0:T(8,128)(2,1)}, u32[]{:S(2)}) %copy-start.5) | copy-done | bytes 122904
  48.1 3.9 %shard_map.133 = (bf16[2,384,640]{2,1,0:T(8,128)(2,1)S(1)}, f32[5,384,256]{2,1,0:T(8,128)S(1)}, f32[5,384,256]{2,1,0:T(8,128)S(1)}) custom-call(s32[1,1536]{1,0:T(1,128)S(1)} %broadcast_in_dim.4.refs_0_, f32[4,128]{1,0:T(4,128)S(1)} %copy-done.4, f32[4,128]{1,0:T(4,128)S(1)} %copy-done.3, f32[384,128]{1,0:T(8,128)S(1)} %copy-done.1, f32[384,128]{1,0:T(8,128)S(1)} %copy-done, ...), custom_call_target="tpu_custom_call" | custom-call | flops 2264924160 | bytes 1966080 | tf_op jit(solution)/shard_map/pallas_call | solution.py:352
  52.0 0.0 collective-permute-done.2.refs_9_
  52.0 0.0 collective-permute-done.1.refs_8_
  52.0 11.7 %shard_map.134 = (bf16[2,48,640]{2,1,0:T(8,128)(2,1)S(1)}, bf16[2,48,640]{2,1,0:T(8,128)(2,1)S(1)}, bf16[2,48,640]{2,1,0:T(8,128)(2,1)S(1)}, bf16[2,48,640]{2,1,...) custom-call(s32[1,1536]{1,0:T(1,128)S(1)} %broadcast_in_dim.4.refs_0, ...), custom_call_target="tpu_custom_call" | custom-call | flops 1698693120 | bytes 1966080 | tf_op jit(solution)/shard_map/pallas_call | solution.py:363
  63.7 0.1 collective-permute-start.10
  63.8 0.8 collective-permute-start.11
  64.5 1.1 %collective-permute-start.12 = (bf16[2,48,640]{2,1,0:T(8,128)(2,1)S(1)}, bf16[2,48,640]{2,1,0:T(8,128)(2,1)S(1)}, u32[]{:S(2)}, u32[]{:S(2)}) collective-permute-start(bf16[2,48,640]{2,1,0:T(8,128)(2,1)S(1)} %get-tuple-element.35), channel_id=1, source_target_pairs={{0,3},{1,2},{2,1},{3,0},{4,7},{5,6},{6,5},{7,4},{8,11},{9,10},{10,... | collective-permute-start | bytes 368648 | tf_op jit(solution)/shard_map/ppermute | solution.py:299
  65.6 0.0 collective-permute-start.13
  65.6 1.7 %collective-permute-start.14 = (bf16[2,48,640]{2,1,0:T(8,128)(2,1)S(1)}, bf16[2,48,640]{2,1,0:T(8,128)(2,1)S(1)}, u32[]{:S(2)}, u32[]{:S(2)}) collective-permute-start(bf16[2,48,640]{2,1,0:T(8,128)(2,1)S(1)} %get-tuple-element.37), channel_id=1, source_target_pairs={{0,5},{1,4},{2,7},{3,6},{4,1},{5,0},{6,3},{7,2},{8,13},{9,12},{10,... | collective-permute-start | bytes 368648 | tf_op jit(solution)/shard_map/ppermute | solution.py:299
  67.3 0.0 collective-permute-done.10.refs_1_
  67.3 0.5 collective-permute-start.15
  67.8 2.2 %collective-permute-done.11.refs_2_ = bf16[2,48,640]{2,1,0:T(8,128)(2,1)S(1)} collective-permute-done((bf16[2,48,640]{2,1,0:T(8,128)(2,1)S(1)}, bf16[2,48,640]{2,1,0:T(8,128)(2,1)S(1)}, u32[]{:S(2)}, u32[]{:S(2)}) %collective-permute-start.11) | collective-permute-done | bytes 122912 | tf_op jit(solution)/shard_map/ppermute | solution.py:299
  70.0 0.0 collective-permute-start.16
  70.0 1.5 %collective-permute-done.12.refs_3_ = bf16[2,48,640]{2,1,0:T(8,128)(2,1)S(1)} collective-permute-done((bf16[2,48,640]{2,1,0:T(8,128)(2,1)S(1)}, bf16[2,48,640]{2,1,0:T(8,128)(2,1)S(1)}, u32[]{:S(2)}, u32[]{:S(2)}) %collective-permute-start.12) | collective-permute-done | bytes 122912 | tf_op jit(solution)/shard_map/ppermute | solution.py:299
  71.6 5.5 %collective-permute-done.13.refs_4_ = bf16[2,48,640]{2,1,0:T(8,128)(2,1)S(1)} collective-permute-done((bf16[2,48,640]{2,1,0:T(8,128)(2,1)S(1)}, bf16[2,48,640]{2,1,0:T(8,128)(2,1)S(1)}, u32[]{:S(2)}, u32[]{:S(2)}) %collective-permute-start.13) | collective-permute-done | bytes 122912 | tf_op jit(solution)/shard_map/ppermute | solution.py:299
  77.1 1.4 %collective-permute-done.14.refs_5_ = bf16[2,48,640]{2,1,0:T(8,128)(2,1)S(1)} collective-permute-done((bf16[2,48,640]{2,1,0:T(8,128)(2,1)S(1)}, bf16[2,48,640]{2,1,0:T(8,128)(2,1)S(1)}, u32[]{:S(2)}, u32[]{:S(2)}) %collective-permute-start.14) | collective-permute-done | bytes 122912 | tf_op jit(solution)/shard_map/ppermute | solution.py:299
  78.5 0.0 collective-permute-done.15.refs_6_
  78.5 0.0 collective-permute-done.16.refs_7_
  78.5 1.1 %shard_map.135 = (bf16[48,5120]{1,0:T(8,128)(2,1)}, bf16[48,5120]{1,0:T(8,128)(2,1)}) custom-call(bf16[2,48,640]{2,1,0:T(8,128)(2,1)S(1)} %get-tuple-element.32.refs_0_, bf16[2,48,640]{2,1,0:T(8,128)(2,1)S(1)} %collective-permute-done.10.refs_1_, bf16[2,48,640]{2,1,0:T(8,128)(2,1)S(1)} %collective-permute-done.11.refs_2_, ...), custom_call_target="tpu_custom_call" | custom-call | bytes 1966080 | tf_op jit(solution)/shard_map/pallas_call | solution.py:285
  (3 shorter events, 0.0 us)
Async XLA Ops:
  0.6 46.5 %copy-start.2 = (bf16[128,128]{1,0:T(8,128)(2,1)S(1)}, bf16[128,128]{1,0:T(8,128)(2,1)}, u32[]{:S(2)}) copy-start(bf16[128,128]{1,0:T(8,128)(2,1)} %constant.53.clone.turn_ref.refs_5_) | copy-start | bytes 98308
  0.6 46.5 %copy-start = (f32[384,128]{1,0:T(8,128)S(1)}, f32[384,128]{1,0:T(8,128)}, u32[]{:S(2)}) copy-start(f32[384,128]{1,0:T(8,128)} %constant.52.clone.sinr_ref.refs_4_) | copy-start | bytes 589828
  0.7 46.5 %copy-start.1 = (f32[384,128]{1,0:T(8,128)S(1)}, f32[384,128]{1,0:T(8,128)}, u32[]{:S(2)}) copy-start(f32[384,128]{1,0:T(8,128)} %constant.51.clone.cosr_ref.refs_3_) | copy-start | bytes 589828
  0.7 46.5 %copy-start.3 = (f32[4,128]{1,0:T(4,128)S(1)}, f32[4,128]{1,0:T(4,128)}, u32[]{:S(2)}) copy-start(f32[4,128]{1,0:T(4,128)} %constant.50.clone.sinb_ref.refs_2_) | copy-start | bytes 6148
  0.7 46.5 %copy-start.4 = (f32[4,128]{1,0:T(4,128)S(1)}, f32[4,128]{1,0:T(4,128)}, u32[]{:S(2)}) copy-start(f32[4,128]{1,0:T(4,128)} %constant.49.clone.cosb_ref.refs_1_) | copy-start | bytes 6148
  0.7 35.9 %copy-start.6 = (s32[1536]{0:T(1024)S(1)}, s32[1536]{0:T(1024)}, u32[]{:S(2)}) copy-start(s32[1536]{0:T(1024)} %param.15) | copy-start | bytes 18436
  16.2 11.5 %collective-permute-start = (bf16[8,4,48,128]{3,2,1,0:T(8,128)(2,1)S(1)}, bf16[8,4,48,128]{3,2,1,0:T(8,128)(2,1)S(1)}, u32[]{:S(2)}, u32[]{:S(2)}) collective-permute-start(bf16[8,4,48,128]{3,2,1,0:T(8,128)(2,1)S(1)} %all_to_all.5.refs_6_), channel_id=1, source_target_pairs={{0,8},{8,16},{16,24},{1,9},{9,17},{17,25},{2,10},{10,18},{18,26},{... | collective-permute-start | bytes 1179656 | tf_op jit(solution)/shard_map/ppermute | solution.py:263
  23.2 9.5 %collective-permute-start.3 = (bf16[2,48,640]{2,1,0:T(8,128)(2,1)}, bf16[2,48,640]{2,1,0:T(8,128)(2,1)S(1)}, u32[]{:S(2)}, u32[]{:S(2)}) collective-permute-start(bf16[2,48,640]{2,1,0:T(8,128)(2,1)} %get-tuple-element.22), channel_id=1, source_target_pairs={{0,1},{1,0},{2,3},{3,2},{4,5},{5,4},{6,7},{7,6},{8,9},{9,8},{10,11... | collective-permute-start | bytes 368648 | tf_op jit(solution)/shard_map/ppermute | solution.py:299
  23.2 9.5 %collective-permute-start.4 = (bf16[2,48,640]{2,1,0:T(8,128)(2,1)}, bf16[2,48,640]{2,1,0:T(8,128)(2,1)S(1)}, u32[]{:S(2)}, u32[]{:S(2)}) collective-permute-start(bf16[2,48,640]{2,1,0:T(8,128)(2,1)} %get-tuple-element.23), channel_id=1, source_target_pairs={{0,2},{1,3},{2,0},{3,1},{4,6},{5,7},{6,4},{7,5},{8,10},{9,11},{10,... | collective-permute-start | bytes 368648 | tf_op jit(solution)/shard_map/ppermute | solution.py:299
  23.8 10.7 %collective-permute-start.5 = (bf16[2,48,640]{2,1,0:T(8,128)(2,1)}, bf16[2,48,640]{2,1,0:T(8,128)(2,1)S(1)}, u32[]{:S(2)}, u32[]{:S(2)}) collective-permute-start(bf16[2,48,640]{2,1,0:T(8,128)(2,1)} %get-tuple-element.24), channel_id=1, source_target_pairs={{0,3},{1,2},{2,1},{3,0},{4,7},{5,6},{6,5},{7,4},{8,11},{9,10},{10,... | collective-permute-start | bytes 368648 | tf_op jit(solution)/shard_map/ppermute | solution.py:299
  27.7 24.3 %collective-permute-start.1 = (bf16[8,4,48,128]{3,2,1,0:T(8,128)(2,1)S(1)}, bf16[8,4,48,128]{3,2,1,0:T(8,128)(2,1)S(1)}, u32[]{:S(2)}, u32[]{:S(2)}) collective-permute-start(bf16[8,4,48,128]{3,2,1,0:T(8,128)(2,1)S(1)} %collective-permute-done.refs_7_), channel_id=1, source_target_pairs={{0,8},{8,16},{16,24},{1,9},{9,17},{17,25},{2,10},{10,18},{18,26},{... | collective-permute-start | bytes 1179656 | tf_op jit(solution)/shard_map/ppermute | solution.py:263
  32.1 11.7 %collective-permute-start.6 = (bf16[2,48,640]{2,1,0:T(8,128)(2,1)}, bf16[2,48,640]{2,1,0:T(8,128)(2,1)S(1)}, u32[]{:S(2)}, u32[]{:S(2)}) collective-permute-start(bf16[2,48,640]{2,1,0:T(8,128)(2,1)} %get-tuple-element.25), channel_id=1, source_target_pairs={{0,4},{1,5},{2,6},{3,7},{4,0},{5,1},{6,2},{7,3},{8,12},{9,13},{10,... | collective-permute-start | bytes 368648 | tf_op jit(solution)/shard_map/ppermute | solution.py:299
  32.7 14.4 %collective-permute-start.7 = (bf16[2,48,640]{2,1,0:T(8,128)(2,1)}, bf16[2,48,640]{2,1,0:T(8,128)(2,1)S(1)}, u32[]{:S(2)}, u32[]{:S(2)}) collective-permute-start(bf16[2,48,640]{2,1,0:T(8,128)(2,1)} %get-tuple-element.26), channel_id=1, source_target_pairs={{0,5},{1,4},{2,7},{3,6},{4,1},{5,0},{6,3},{7,2},{8,13},{9,12},{10,... | collective-permute-start | bytes 368648 | tf_op jit(solution)/shard_map/ppermute | solution.py:299
  32.7 14.4 %collective-permute-start.8 = (bf16[2,48,640]{2,1,0:T(8,128)(2,1)}, bf16[2,48,640]{2,1,0:T(8,128)(2,1)S(1)}, u32[]{:S(2)}, u32[]{:S(2)}) collective-permute-start(bf16[2,48,640]{2,1,0:T(8,128)(2,1)} %get-tuple-element.27), channel_id=1, source_target_pairs={{0,6},{1,7},{2,4},{3,5},{4,2},{5,3},{6,0},{7,1},{8,14},{9,15},{10,... | collective-permute-start | bytes 368648 | tf_op jit(solution)/shard_map/ppermute | solution.py:299
  34.5 12.7 %collective-permute-start.9 = (bf16[2,48,640]{2,1,0:T(8,128)(2,1)}, bf16[2,48,640]{2,1,0:T(8,128)(2,1)S(1)}, u32[]{:S(2)}, u32[]{:S(2)}) collective-permute-start(bf16[2,48,640]{2,1,0:T(8,128)(2,1)} %get-tuple-element.28), channel_id=1, source_target_pairs={{0,7},{1,6},{2,5},{3,4},{4,3},{5,2},{6,1},{7,0},{8,15},{9,14},{10,... | collective-permute-start | bytes 368648 | tf_op jit(solution)/shard_map/ppermute | solution.py:299
  43.8 8.2 %collective-permute-start.2 = (bf16[8,2,48,128]{3,2,1,0:T(8,128)(2,1)S(1)}, bf16[8,2,48,128]{3,2,1,0:T(8,128)(2,1)S(1)}, u32[]{:S(2)}, u32[]{:S(2)}) collective-permute-start(bf16[8,2,48,128]{3,2,1,0:T(8,128)(2,1)S(1)} %slice.4), channel_id=1, source_target_pairs={{0,24},{1,25},{2,26},{3,27},{4,28},{5,29},{6,30},{7,31}} | collective-permute-start | bytes 589832 | tf_op jit(solution)/shard_map/ppermute | solution.py:263
  47.2 0.9 %copy-start.5 = (bf16[2,48,640]{2,1,0:T(8,128)(2,1)S(1)}, bf16[2,48,640]{2,1,0:T(8,128)(2,1)}, u32[]{:S(2)}) copy-start(bf16[2,48,640]{2,1,0:T(8,128)(2,1)} %get-tuple-element.21.refs_8_) | copy-start | bytes 368644
  63.7 3.6 %collective-permute-start.10 = (bf16[2,48,640]{2,1,0:T(8,128)(2,1)S(1)}, bf16[2,48,640]{2,1,0:T(8,128)(2,1)S(1)}, u32[]{:S(2)}, u32[]{:S(2)}) collective-permute-start(bf16[2,48,640]{2,1,0:T(8,128)(2,1)S(1)} %get-tuple-element.33), channel_id=1, source_target_pairs={{0,1},{1,0},{2,3},{3,2},{4,5},{5,4},{6,7},{7,6},{8,9},{9,8},{10,11... | collective-permute-start | bytes 368648 | tf_op jit(solution)/shard_map/ppermute | solution.py:299
  63.8 6.3 %collective-permute-start.11 = (bf16[2,48,640]{2,1,0:T(8,128)(2,1)S(1)}, bf16[2,48,640]{2,1,0:T(8,128)(2,1)S(1)}, u32[]{:S(2)}, u32[]{:S(2)}) collective-permute-start(bf16[2,48,640]{2,1,0:T(8,128)(2,1)S(1)} %get-tuple-element.34), channel_id=1, source_target_pairs={{0,2},{1,3},{2,0},{3,1},{4,6},{5,7},{6,4},{7,5},{8,10},{9,11},{10,... | collective-permute-start | bytes 368648 | tf_op jit(solution)/shard_map/ppermute | solution.py:299
  64.5 7.0 %collective-permute-start.12 = (bf16[2,48,640]{2,1,0:T(8,128)(2,1)S(1)}, bf16[2,48,640]{2,1,0:T(8,128)(2,1)S(1)}, u32[]{:S(2)}, u32[]{:S(2)}) collective-permute-start(bf16[2,48,640]{2,1,0:T(8,128)(2,1)S(1)} %get-tuple-element.35), channel_id=1, source_target_pairs={{0,3},{1,2},{2,1},{3,0},{4,7},{5,6},{6,5},{7,4},{8,11},{9,10},{10,... | collective-permute-start | bytes 368648 | tf_op jit(solution)/shard_map/ppermute | solution.py:299
  65.6 11.5 %collective-permute-start.13 = (bf16[2,48,640]{2,1,0:T(8,128)(2,1)S(1)}, bf16[2,48,640]{2,1,0:T(8,128)(2,1)S(1)}, u32[]{:S(2)}, u32[]{:S(2)}) collective-permute-start(bf16[2,48,640]{2,1,0:T(8,128)(2,1)S(1)} %get-tuple-element.36), channel_id=1, source_target_pairs={{0,4},{1,5},{2,6},{3,7},{4,0},{5,1},{6,2},{7,3},{8,12},{9,13},{10,... | collective-permute-start | bytes 368648 | tf_op jit(solution)/shard_map/ppermute | solution.py:299
  65.6 12.9 %collective-permute-start.14 = (bf16[2,48,640]{2,1,0:T(8,128)(2,1)S(1)}, bf16[2,48,640]{2,1,0:T(8,128)(2,1)S(1)}, u32[]{:S(2)}, u32[]{:S(2)}) collective-permute-start(bf16[2,48,640]{2,1,0:T(8,128)(2,1)S(1)} %get-tuple-element.37), channel_id=1, source_target_pairs={{0,5},{1,4},{2,7},{3,6},{4,1},{5,0},{6,3},{7,2},{8,13},{9,12},{10,... | collective-permute-start | bytes 368648 | tf_op jit(solution)/shard_map/ppermute | solution.py:299
  67.3 11.2 %collective-permute-start.15 = (bf16[2,48,640]{2,1,0:T(8,128)(2,1)S(1)}, bf16[2,48,640]{2,1,0:T(8,128)(2,1)S(1)}, u32[]{:S(2)}, u32[]{:S(2)}) collective-permute-start(bf16[2,48,640]{2,1,0:T(8,128)(2,1)S(1)} %get-tuple-element.38), channel_id=1, source_target_pairs={{0,6},{1,7},{2,4},{3,5},{4,2},{5,3},{6,0},{7,1},{8,14},{9,15},{10,... | collective-permute-start | bytes 368648 | tf_op jit(solution)/shard_map/ppermute | solution.py:299
  70.0 8.5 %collective-permute-start.16 = (bf16[2,48,640]{2,1,0:T(8,128)(2,1)S(1)}, bf16[2,48,640]{2,1,0:T(8,128)(2,1)S(1)}, u32[]{:S(2)}, u32[]{:S(2)}) collective-permute-start(bf16[2,48,640]{2,1,0:T(8,128)(2,1)S(1)} %get-tuple-element.39), channel_id=1, source_target_pairs={{0,7},{1,6},{2,5},{3,4},{4,3},{5,2},{6,1},{7,0},{8,15},{9,14},{10,... | collective-permute-start | bytes 368648 | tf_op jit(solution)/shard_map/ppermute | solution.py:299

commit v7 on v6

--- a/solution.py
+++ b/solution.py
@@ -114,27 +114,26 @@
     return jnp.where(lax.broadcasted_iota(jnp.int32, (HEAD, rows), 0) == ids, 1.0, 0.0).T
 
 
-def take_local(shared, plane, distances, blocks, k_ref, v_ref):
-    labels_ref, cosb_ref, sinb_ref, cosr_ref, sinr_ref, turn_ref = shared
+def take_local(shared, plane, distances, blocks, same, k_ref, v_ref):
+    cosb_ref, sinb_ref, cosr_ref, sinr_ref, turn_ref = shared
     turn = turn_ref[...]
     for i, d in enumerate(distances):
         rows = k_ref.shape[0] // len(distances)
-        behind = jnp.maximum(plane - d, 0)
-        base = pl.ds(behind, 1)
+        base = pl.ds(jnp.maximum(plane - d, 0), 1)
         cosine, sine = turned(cosb_ref[base], sinb_ref[base], cosr_ref[...], sinr_ref[...])
         at = slice(i * rows, (i + 1) * rows)
-        keys = blocks[i][:, 0].reshape(rows, HEAD)
+        keys = blocks[d][:, 0].reshape(rows, HEAD)
         k_ref[at, :HEAD] = rotated_unit(keys, turn, cosine, sine).astype(k_ref.dtype)
-        k_ref[at, HEAD:] = same_stretch(labels_ref, behind, rows).astype(k_ref.dtype)
-        take_values(v_ref, i, blocks[i][:, 1].reshape(rows, HEAD), plane >= d)
+        k_ref[at, HEAD:] = same[i].astype(k_ref.dtype)
+        take_values(v_ref, i, blocks[d][:, 1].reshape(rows, HEAD), plane >= d)
 
 
 def take_global(plane, distances, blocks, k_ref, v_ref):
     for i, d in enumerate(distances):
         rows = k_ref.shape[0] // len(distances)
-        last = blocks[i].shape[1] - 1
-        k_ref[i * rows : (i + 1) * rows] = blocks[i][:, last - 1].reshape(rows, HEAD)
-        take_values(v_ref, i, blocks[i][:, last].reshape(rows, HEAD), plane >= d)
+        last = blocks[d].shape[1] - 1
+        k_ref[i * rows : (i + 1) * rows] = blocks[d][:, last - 1].reshape(rows, HEAD)
+        take_values(v_ref, i, blocks[d][:, last].reshape(rows, HEAD), plane >= d)
 
 
 def query_of(q_ref, layer, g):
@@ -154,20 +153,25 @@
     return acc
 
 
-def early_body(n_near, *refs):
-    shared, refs = refs[:6], refs[6:]
-    parts = refs[0].shape[0]
-    queries, blocks, refs = refs[n_near : n_near + parts], refs[:n_near], refs[n_near + parts :]
-    q_ref, lacc_ref, gacc_ref, lk_ref, lv_ref, gk_ref, gv_ref = refs
+def early_body(plan, labels_ref, *refs):
+    _, n_queries, local_near, local_far, global_near, _ = plan
+    shared, refs = refs[:5], refs[5:]
+    blocks = dict(zip(global_near, refs))
+    queries, refs = refs[len(blocks) : len(blocks) + n_queries], refs[len(blocks) + n_queries :]
+    q_ref, lacc_ref, gacc_ref, other_ref, same_ref, lk_ref, lv_ref, gk_ref, gv_ref = refs
     members, rows, _ = lacc_ref.shape
-    tokens = rows // parts
+    tokens = rows // n_queries
     plane, spot = lax.axis_index("plane"), spot_of()
     for s, ref in enumerate(queries):
         at = pl.ds(pl.multiple_of(lax.bitwise_xor(spot, s) * tokens, 16), tokens)
         q_ref[:, at] = ref[...]
-    take_local(shared, plane, range(n_near), blocks, lk_ref, lv_ref)
-    take_global(plane, range(n_near), blocks, gk_ref, gv_ref)
-    other = ((same_stretch(shared[0], plane, rows) - 1.0) * far).astype(lk_ref.dtype)
+    same = [same_stretch(labels_ref, jnp.maximum(plane - d, 0), rows) for d in local_near]
+    other = ((same[0] - 1.0) * far).astype(other_ref.dtype)
+    other_ref[...] = other
+    for i, d in enumerate(local_far):
+        same_ref[i] = same_stretch(labels_ref, jnp.maximum(plane - d, 0), rows).astype(same_ref.dtype)
+    take_local(shared, plane, local_near, blocks, same, lk_ref, lv_ref)
+    take_global(plane, global_near, blocks, gk_ref, gv_ref)
 
     def member(g, carry):
         q = jnp.concatenate([query_of(q_ref, 0, g), other], axis=1)
@@ -178,20 +182,19 @@
     lax.fori_loop(0, members, member, 0, unroll=True)
 
 
-def late_body(n_near, local_back, n, *refs):
-    shared, refs = refs[:6], refs[6:]
+def late_body(plan, *refs):
+    n, n_queries, _, local_far, _, global_far = plan
+    shared, refs = refs[:5], refs[5:]
     blocks, refs = refs[:n], refs[n:]
-    parts = blocks[0].shape[0]
-    q_ref, lacc_ref, gacc_ref = refs[:3]
-    o_refs, refs = refs[3 : 3 + parts], refs[3 + parts :]
+    q_ref, lacc_ref, gacc_ref, other_ref, same_ref = refs[:5]
+    o_refs, refs = refs[5 : 5 + n_queries], refs[5 + n_queries :]
     out_ref, lk_ref, lv_ref, gk_ref, gv_ref, allk_ref, allv_ref = refs
     members, rows, _ = lacc_ref.shape
-    tokens = rows // parts
+    tokens = rows // n_queries
     plane, spot = lax.axis_index("plane"), spot_of()
-    local_far = range(n_near, local_back + 1)
-    take_local(shared, plane, local_far, [blocks[d] for d in local_far], lk_ref, lv_ref)
-    take_global(plane, range(n_near, n), blocks[n_near:], gk_ref, gv_ref)
-    other = ((same_stretch(shared[0], plane, rows) - 1.0) * far).astype(lk_ref.dtype)
+    take_local(shared, plane, local_far, blocks, same_ref, lk_ref, lv_ref)
+    take_global(plane, global_far, blocks, gk_ref, gv_ref)
+    other = other_ref[...]
 
     def put(g, layer, acc):
         at = pl.multiple_of(g * HEAD, HEAD)
@@ -214,7 +217,7 @@
 
     @pl.when(jnp.logical_not(safe))
     def _():
-        take_global(plane, range(n), blocks, allk_ref, allv_ref)
+        take_global(plane, tuple(range(n)), blocks, allk_ref, allv_ref)
 
         def shifted(g, carry):
             q = query_of(q_ref, 1, g)
@@ -338,40 +341,49 @@
     queries = pack(query_local, query_global, *bases, *steps, turn, temper)
     queries = swapped(queries)
 
-    n_near = min(2, planes)
+    global_near = tuple(d for d in range(planes) if d != 2) if planes <= 4 else (0, 1)
+    global_far = tuple(d for d in range(planes) if d not in global_near)
+    local_near = tuple(d for d in global_near if d <= local_back)
+    local_far = tuple(d for d in global_far if d <= local_back)
+    plan = (planes, parts, local_near, local_far, global_near, global_far)
     kept = near(*queries[1:], *blocks)
     queries, blocks = (queries[0], *kept[: parts - 1]), kept[parts - 1 :]
-    shared = (label_row, *bases, *steps, turn)
+    shared = (*bases, *steps, turn)
     placed = jax.ShapeDtypeStruct((2, rows, width), dtype)
     sums = jax.ShapeDtypeStruct((members, rows, 2 * HEAD), jnp.float32)
-    unit = 2 * 3 * rows * rows * HEAD * members
+    other = jax.ShapeDtypeStruct((rows, HEAD), dtype)
+    same = jax.ShapeDtypeStruct((len(local_far), rows, HEAD), dtype)
+
+    def cost(count):
+        return dict(flops=6 * rows * rows * HEAD * members * count, exps=rows * rows * members * count)
 
     def scratch(count, columns):
-        return pltpu.VMEM((max(1, count) * rows, columns), dtype)
+        return pltpu.VMEM((count * rows, columns), dtype)
+
+    def keys_and_values(local, others):
+        both = scratch(len(local), 2 * HEAD)
+        return [both, both, scratch(len(others), HEAD), scratch(len(others), 2 * HEAD)]
 
     early = vmem_call(
-        functools.partial(early_body, n_near),
-        (placed, sums, sums),
-        6 + n_near + parts,
-        flops=unit * 2 * n_near,
+        functools.partial(early_body, plan),
+        (placed, sums, sums, other, same),
+        6 + len(global_near) + parts,
         nbytes=8 * rows * width,
-        exps=rows * rows * members * 2 * n_near,
-        scratch=[scratch(n_near, 2 * HEAD)] * 2 + [scratch(n_near, HEAD), scratch(n_near, 2 * HEAD)],
+        scratch=keys_and_values(local_near, global_near),
         limit=vmem_bytes,
-    )(*shared, *blocks[:n_near], *queries)
+        **cost(len(local_near) + len(global_near)),
+    )(label_row, *shared, *(blocks[d] for d in global_near), *queries)
     early = near(*early)
     out = vmem_call(
-        functools.partial(late_body, n_near, local_back, planes),
+        functools.partial(late_body, plan),
         (piece,) * parts,
-        6 + planes + 3,
-        flops=unit * (planes + local_back + 1 - 2 * n_near),
+        5 + planes + 5,
         nbytes=8 * rows * width,
-        exps=rows * rows * members * (planes + local_back + 1 - 2 * n_near),
         scratch=[pltpu.VMEM((2, rows, width), dtype)]
-        + [scratch(local_back + 1 - n_near, 2 * HEAD)] * 2
-        + [scratch(planes - n_near, HEAD), scratch(planes - n_near, 2 * HEAD)]
+        + keys_and_values(local_far, global_far)
         + [scratch(planes, HEAD), scratch(planes, 2 * HEAD)],
         limit=vmem_bytes,
+        **cost(len(local_far) + len(global_far)),
     )(*shared, *blocks, *early)
     return unpack(near(*swapped(out)))
 

time: 79.9 us -> 75.3 us (0.942)
  waiting for transfers between devices: 20.6 us -> 16.4 us
    ppermute x3, waiting for transfers between devices: 2.63 us -> 0.01 us  [upward(): return lax.ppermute(x, 'plane', [(i, i + by) for i in range(size - by)])]
    ppermute x14, waiting for transfers between devices: 17.9 us -> 16.4 us  [swapped(): lax.ppermute(pieces[s], IN_PLANE, [(i, i ^ s) for i in range(parts)])]
    ppermute x3, starting transfers between devices: 11.2 us -> 9.91 us  [upward(): return lax.ppermute(x, 'plane', [(i, i + by) for i in range(size - by)])]
  transfers between devices with their start and end apart: 17 -> 17, of which waited for: 6 -> 5; matrix products, arithmetic and copies ran while one was open for 1% -> 1% of each run, Pallas kernels for 8% -> 10%
where the time goes in v7:
time: 75.3 us; the launch traced here: 75 us
  Pallas kernels  21.6 us (29%)
  starting transfers between devices  20.9 us (28%)
  waiting for transfers between devices  16.4 us (22%)
  blocking collectives  13.5 us (18%)
  local copies, waits for them, and re-layouts  1.65 us (2%)
  between operations  0.85 us (1%)
    ppermute x14, waiting for transfers between devices, swapped(): lax.ppermute(pieces[s], IN_PLANE, [(i, i ^ s) for i in range(parts)])  16.4 us
    all_to_all x1, blocking collectives, exchange(): return lax.all_to_all(x, IN_PLANE, split_axis=0, concat_axis=0, tiled=True)  13.5 us
    ppermute x14, starting transfers between devices, swapped(): lax.ppermute(pieces[s], IN_PLANE, [(i, i ^ s) for i in range(parts)])  11 us
    pallas_call x1, Pallas kernels, shards(): vmem_call(functools.partial(late_body, plan), (piece,) * parts, 5 + plane...  10.8 us
    ppermute x3, starting transfers between devices, upward(): return lax.ppermute(x, 'plane', [(i, i + by) for i in range(size - by)])  9.91 us
    pallas_call x1, Pallas kernels, shards(): vmem_call(functools.partial(early_body, plan), (placed, sums, sums, other...  4.96 us
    pallas_call x1, Pallas kernels, shards(): queries = pack(query_local, query_global, *bases, *steps, turn, temper)  2.82 us
    pallas_call x1, Pallas kernels, shards(): pack = pack(key_local, value_local, key_global, value_global)  1.93 us
  transfers between devices with their start and end apart: 17, of which 5 were waited for; matrix products, arithmetic and copies ran while one was open for 1% of the time, Pallas kernels for 10%

profile of v7, /device:TPU:0, one launch (start us, length us, event | category | flops | bytes accessed | tf_op | source)
XLA Modules:
  0.0 75.0 jit_solution(871595764061844349)
XLA Ops:
  0.6 0.0 copy-start.3
  0.6 0.0 copy-start.4
  0.7 0.0 copy-start
  0.7 0.0 copy-start.1
  0.7 0.0 copy-start.2
  0.7 0.0 copy-start.6
  0.7 1.9 %shard_map.131 = bf16[8,4,48,128]{3,2,1,0:T(8,128)(2,1)} custom-call(bf16[48,1024]{1,0:T(8,128)(2,1)} %kl_ref.1, bf16[48,1024]{1,0:T(8,128)(2,1)} %vl_ref.1, bf16[48,1024]{1,0:T(8,128)(2,1)} %kg_ref.1, bf16[48,1024]{1,0:T(8,128)(2,1)} %vg_ref.1), custom_call_target="tpu_custom_call" | custom-call | bytes 786432 | tf_op jit(solution)/shard_map/pallas_call | solution.py:320
  2.6 13.5 %all_to_all.5.refs_5_ = bf16[8,4,48,128]{3,2,1,0:T(8,128)(2,1)S(1)} all-to-all(bf16[8,4,48,128]{3,2,1,0:T(8,128)(2,1)} %shard_map.131), channel_id=1, replica_groups=mesh['plane'=4,'row'=2,'head'=4] {'row','head'}, dimensions={0} | all-to-all | bytes 786432 | tf_op jit(solution)/shard_map/all_to_all | solution.py:261
  16.1 3.5 %collective-permute-start = (bf16[8,4,48,128]{3,2,1,0:T(8,128)(2,1)S(1)}, bf16[8,4,48,128]{3,2,1,0:T(8,128)(2,1)S(1)}, u32[]{:S(2)}, u32[]{:S(2)}) collective-permute-start(bf16[8,4,48,128]{3,2,1,0:T(8,128)(2,1)S(1)} %all_to_all.5.refs_5_), channel_id=1, source_target_pairs={{0,8},{8,16},{16,24},{1,9},{9,17},{17,25},{2,10},{10,18},{18,26},{... | collective-permute-start | bytes 1179656 | tf_op jit(solution)/shard_map/ppermute | solution.py:266
  19.7 0.7 broadcast_in_dim.10.temper_ref
  20.4 2.8 %shard_map.132 = (bf16[2,48,640]{2,1,0:T(8,128)(2,1)}, bf16[2,48,640]{2,1,0:T(8,128)(2,1)}, bf16[2,48,640]{2,1,0:T(8,128)(2,1)}, bf16[2,48,640]{2,1,0:T(8,128)(2...) custom-call(bf16[48,5120]{1,0:T(8,128)(2,1)} %ql_ref.1, ...), custom_call_target="tpu_custom_call" | custom-call | flops 62914560 | bytes 1966080 | tf_op jit(solution)/shard_map/pallas_call | solution.py:341
  23.2 0.0 collective-permute-start.3
  23.2 0.6 collective-permute-start.4
  23.8 1.2 %collective-permute-start.5 = (bf16[2,48,640]{2,1,0:T(8,128)(2,1)}, bf16[2,48,640]{2,1,0:T(8,128)(2,1)S(1)}, u32[]{:S(2)}, u32[]{:S(2)}) collective-permute-start(bf16[2,48,640]{2,1,0:T(8,128)(2,1)} %get-tuple-element.26), channel_id=1, source_target_pairs={{0,3},{1,2},{2,1},{3,0},{4,7},{5,6},{6,5},{7,4},{8,11},{9,10},{10,... | collective-permute-start | bytes 368648 | tf_op jit(solution)/shard_map/ppermute | solution.py:302
  25.1 0.6 collective-permute-start.6
  25.6 0.0 collective-permute-done.3.refs_9_
  25.6 3.3 %collective-permute-start.2 = (bf16[8,2,48,128]{3,2,1,0:T(8,128)(2,1)S(1)}, bf16[8,2,48,128]{3,2,1,0:T(8,128)(2,1)S(1)}, u32[]{:S(2)}, u32[]{:S(2)}) collective-permute-start(bf16[8,2,48,128]{3,2,1,0:T(8,128)(2,1)S(1)} %slice.4), channel_id=1, source_target_pairs={{0,24},{1,25},{2,26},{3,27},{4,28},{5,29},{6,30},{7,31}} | collective-permute-start | bytes 589832 | tf_op jit(solution)/shard_map/ppermute | solution.py:266
  29.0 0.0 collective-permute-done.refs_6_
  29.0 3.1 %collective-permute-start.1 = (bf16[8,4,48,128]{3,2,1,0:T(8,128)(2,1)S(1)}, bf16[8,4,48,128]{3,2,1,0:T(8,128)(2,1)S(1)}, u32[]{:S(2)}, u32[]{:S(2)}) collective-permute-start(bf16[8,4,48,128]{3,2,1,0:T(8,128)(2,1)S(1)} %collective-permute-done.refs_6_), channel_id=1, source_target_pairs={{0,8},{8,16},{16,24},{1,9},{9,17},{17,25},{2,10},{10,18},{18,26},{... | collective-permute-start | bytes 1179656 | tf_op jit(solution)/shard_map/ppermute | solution.py:266
  32.1 0.0 collective-permute-done.4.refs_10_
  32.1 0.1 collective-permute-start.7
  32.2 0.0 collective-permute-done.5.refs_11_
  32.2 0.9 %collective-permute-start.8 = (bf16[2,48,640]{2,1,0:T(8,128)(2,1)}, bf16[2,48,640]{2,1,0:T(8,128)(2,1)S(1)}, u32[]{:S(2)}, u32[]{:S(2)}) collective-permute-start(bf16[2,48,640]{2,1,0:T(8,128)(2,1)} %get-tuple-element.29), channel_id=1, source_target_pairs={{0,6},{1,7},{2,4},{3,5},{4,2},{5,3},{6,0},{7,1},{8,14},{9,15},{10,... | collective-permute-start | bytes 368648 | tf_op jit(solution)/shard_map/ppermute | solution.py:302
  33.1 0.0 collective-permute-done.6.refs_12_
  33.1 2.0 %collective-permute-start.9 = (bf16[2,48,640]{2,1,0:T(8,128)(2,1)}, bf16[2,48,640]{2,1,0:T(8,128)(2,1)S(1)}, u32[]{:S(2)}, u32[]{:S(2)}) collective-permute-start(bf16[2,48,640]{2,1,0:T(8,128)(2,1)} %get-tuple-element.30), channel_id=1, source_target_pairs={{0,7},{1,6},{2,5},{3,4},{4,3},{5,2},{6,1},{7,0},{8,15},{9,14},{10,... | collective-permute-start | bytes 368648 | tf_op jit(solution)/shard_map/ppermute | solution.py:302
  35.1 0.0 copy-done.6
  35.1 7.3 %collective-permute-done.7.refs_13_ = bf16[2,48,640]{2,1,0:T(8,128)(2,1)S(1)} collective-permute-done((bf16[2,48,640]{2,1,0:T(8,128)(2,1)}, bf16[2,48,640]{2,1,0:T(8,128)(2,1)S(1)}, u32[]{:S(2)}, u32[]{:S(2)}) %collective-permute-start.7) | collective-permute-done | bytes 122912 | tf_op jit(solution)/shard_map/ppermute | solution.py:302
  42.4 0.0 collective-permute-done.8.refs_14_
  42.4 0.0 collective-permute-done.9.refs_15_
  42.4 0.0 collective-permute-done.2.refs_7_.refs_8_
  42.4 0.0 copy-done.3
  42.4 0.0 copy-done.4
  42.4 0.0 copy-done
  42.4 0.0 copy-done.1
  42.4 0.0 copy-done.2
  42.4 0.0 copy-start.5
  42.4 0.9 %copy-done.5 = bf16[2,48,640]{2,1,0:T(8,128)(2,1)S(1)} copy-done((bf16[2,48,640]{2,1,0:T(8,128)(2,1)S(1)}, bf16[2,48,640]{2,1,0:T(8,128)(2,1)}, u32[]{:S(2)}) %copy-start.5) | copy-done | bytes 122904
  43.3 5.0 %shard_map.133 = (bf16[2,384,640]{2,1,0:T(8,128)(2,1)S(1)}, f32[5,384,256]{2,1,0:T(8,128)S(1)}, f32[5,384,256]{2,1,0:T(8,128)S(1)}, bf16[384,128]{1,0:T(8,128)(2,1)S(1)}, bf16[1,384,128]{2,1,0:T(8,128)(2,1)S(1)}) custom-call(s32[1,1536]{1,0:T(1,128)S(1)} %broadcast_in_dim.4.labels_ref, f32[4,128]{1,0:T(4,128)S(1)} %copy-done.3, f32[4,128]{1,0:T(4,128)S(1)} %copy-done.4, ...), custom_call_target="tpu_custom_call" | custom-call | flops 2831155200 | bytes 1966080 | tf_op jit(solution)/shard_map/pallas_call | solution.py:367
  48.3 0.0 collective-permute-done.1.refs_7_
  48.3 10.8 %shard_map.134 = (bf16[2,48,640]{2,1,0:T(8,128)(2,1)S(1)}, bf16[2,48,640]{2,1,0:T(8,128)(2,1)S(1)}, bf16[2,48,640]{2,1,0:T(8,128)(2,1)S(1)}, bf16[2,48,640]{2,1,...) custom-call(f32[4,128]{1,0:T(4,128)S(1)} %copy-done.3, ...), custom_call_target="tpu_custom_call" | custom-call | flops 1132462080 | bytes 1966080 | tf_op jit(solution)/shard_map/pallas_call | solution.py:377
  59.1 0.1 collective-permute-start.10
  59.2 0.9 %collective-permute-start.11 = (bf16[2,48,640]{2,1,0:T(8,128)(2,1)S(1)}, bf16[2,48,640]{2,1,0:T(8,128)(2,1)S(1)}, u32[]{:S(2)}, u32[]{:S(2)}) collective-permute-start(bf16[2,48,640]{2,1,0:T(8,128)(2,1)S(1)} %get-tuple-element.38), channel_id=1, source_target_pairs={{0,2},{1,3},{2,0},{3,1},{4,6},{5,7},{6,4},{7,5},{8,10},{9,11},{10,... | collective-permute-start | bytes 368648 | tf_op jit(solution)/shard_map/ppermute | solution.py:302
  60.1 0.9 %collective-permute-start.12 = (bf16[2,48,640]{2,1,0:T(8,128)(2,1)S(1)}, bf16[2,48,640]{2,1,0:T(8,128)(2,1)S(1)}, u32[]{:S(2)}, u32[]{:S(2)}) collective-permute-start(bf16[2,48,640]{2,1,0:T(8,128)(2,1)S(1)} %get-tuple-element.39), channel_id=1, source_target_pairs={{0,3},{1,2},{2,1},{3,0},{4,7},{5,6},{6,5},{7,4},{8,11},{9,10},{10,... | collective-permute-start | bytes 368648 | tf_op jit(solution)/shard_map/ppermute | solution.py:302
  61.0 1.4 %collective-permute-start.13 = (bf16[2,48,640]{2,1,0:T(8,128)(2,1)S(1)}, bf16[2,48,640]{2,1,0:T(8,128)(2,1)S(1)}, u32[]{:S(2)}, u32[]{:S(2)}) collective-permute-start(bf16[2,48,640]{2,1,0:T(8,128)(2,1)S(1)} %get-tuple-element.40), channel_id=1, source_target_pairs={{0,4},{1,5},{2,6},{3,7},{4,0},{5,1},{6,2},{7,3},{8,12},{9,13},{10,... | collective-permute-start | bytes 368648 | tf_op jit(solution)/shard_map/ppermute | solution.py:302
  62.5 0.3 collective-permute-start.14
  62.7 0.0 collective-permute-done.10.refs_1_
  62.8 1.7 %collective-permute-start.15 = (bf16[2,48,640]{2,1,0:T(8,128)(2,1)S(1)}, bf16[2,48,640]{2,1,0:T(8,128)(2,1)S(1)}, u32[]{:S(2)}, u32[]{:S(2)}) collective-permute-start(bf16[2,48,640]{2,1,0:T(8,128)(2,1)S(1)} %get-tuple-element.42), channel_id=1, source_target_pairs={{0,6},{1,7},{2,4},{3,5},{4,2},{5,3},{6,0},{7,1},{8,14},{9,15},{10,... | collective-permute-start | bytes 368648 | tf_op jit(solution)/shard_map/ppermute | solution.py:302
  64.4 1.0 %collective-permute-done.11.refs_2_ = bf16[2,48,640]{2,1,0:T(8,128)(2,1)S(1)} collective-permute-done((bf16[2,48,640]{2,1,0:T(8,128)(2,1)S(1)}, bf16[2,48,640]{2,1,0:T(8,128)(2,1)S(1)}, u32[]{:S(2)}, u32[]{:S(2)}) %collective-permute-start.11) | collective-permute-done | bytes 122912 | tf_op jit(solution)/shard_map/ppermute | solution.py:302
  65.5 0.3 collective-permute-start.16
  65.8 1.2 %collective-permute-done.12.refs_3_ = bf16[2,48,640]{2,1,0:T(8,128)(2,1)S(1)} collective-permute-done((bf16[2,48,640]{2,1,0:T(8,128)(2,1)S(1)}, bf16[2,48,640]{2,1,0:T(8,128)(2,1)S(1)}, u32[]{:S(2)}, u32[]{:S(2)}) %collective-permute-start.12) | collective-permute-done | bytes 122912 | tf_op jit(solution)/shard_map/ppermute | solution.py:302
  67.0 0.2 collective-permute-done.13.refs_4_
  67.2 6.7 %collective-permute-done.14.refs_5_ = bf16[2,48,640]{2,1,0:T(8,128)(2,1)S(1)} collective-permute-done((bf16[2,48,640]{2,1,0:T(8,128)(2,1)S(1)}, bf16[2,48,640]{2,1,0:T(8,128)(2,1)S(1)}, u32[]{:S(2)}, u32[]{:S(2)}) %collective-permute-start.14) | collective-permute-done | bytes 122912 | tf_op jit(solution)/shard_map/ppermute | solution.py:302
  73.9 0.0 collective-permute-done.15.refs_6_
  73.9 0.0 collective-permute-done.16.refs_7_
  73.9 1.1 %shard_map.135 = (bf16[48,5120]{1,0:T(8,128)(2,1)}, bf16[48,5120]{1,0:T(8,128)(2,1)}) custom-call(bf16[2,48,640]{2,1,0:T(8,128)(2,1)S(1)} %get-tuple-element.36.refs_0_, bf16[2,48,640]{2,1,0:T(8,128)(2,1)S(1)} %collective-permute-done.10.refs_1_, bf16[2,48,640]{2,1,0:T(8,128)(2,1)S(1)} %collective-permute-done.11.refs_2_, ...), custom_call_target="tpu_custom_call" | custom-call | bytes 1966080 | tf_op jit(solution)/shard_map/pallas_call | solution.py:288
  (3 shorter events, 0.0 us)
Async XLA Ops:
  0.6 41.8 %copy-start.3 = (f32[4,128]{1,0:T(4,128)S(1)}, f32[4,128]{1,0:T(4,128)}, u32[]{:S(2)}) copy-start(f32[4,128]{1,0:T(4,128)} %constant.49.clone.cosb_ref.refs_0_) | copy-start | bytes 6148
  0.6 41.8 %copy-start.4 = (f32[4,128]{1,0:T(4,128)S(1)}, f32[4,128]{1,0:T(4,128)}, u32[]{:S(2)}) copy-start(f32[4,128]{1,0:T(4,128)} %constant.50.clone.sinb_ref.refs_1_) | copy-start | bytes 6148
  0.7 41.8 %copy-start = (f32[384,128]{1,0:T(8,128)S(1)}, f32[384,128]{1,0:T(8,128)}, u32[]{:S(2)}) copy-start(f32[384,128]{1,0:T(8,128)} %constant.51.clone.cosr_ref.refs_2_) | copy-start | bytes 589828
  0.7 41.7 %copy-start.1 = (f32[384,128]{1,0:T(8,128)S(1)}, f32[384,128]{1,0:T(8,128)}, u32[]{:S(2)}) copy-start(f32[384,128]{1,0:T(8,128)} %constant.52.clone.sinr_ref.refs_3_) | copy-start | bytes 589828
  0.7 41.7 %copy-start.2 = (bf16[128,128]{1,0:T(8,128)(2,1)S(1)}, bf16[128,128]{1,0:T(8,128)(2,1)}, u32[]{:S(2)}) copy-start(bf16[128,128]{1,0:T(8,128)(2,1)} %constant.53.clone.turn_ref.refs_4_) | copy-start | bytes 98308
  0.7 34.4 %copy-start.6 = (s32[1536]{0:T(1024)S(1)}, s32[1536]{0:T(1024)}, u32[]{:S(2)}) copy-start(s32[1536]{0:T(1024)} %param.15) | copy-start | bytes 18436
  16.1 12.8 %collective-permute-start = (bf16[8,4,48,128]{3,2,1,0:T(8,128)(2,1)S(1)}, bf16[8,4,48,128]{3,2,1,0:T(8,128)(2,1)S(1)}, u32[]{:S(2)}, u32[]{:S(2)}) collective-permute-start(bf16[8,4,48,128]{3,2,1,0:T(8,128)(2,1)S(1)} %all_to_all.5.refs_5_), channel_id=1, source_target_pairs={{0,8},{8,16},{16,24},{1,9},{9,17},{17,25},{2,10},{10,18},{18,26},{... | collective-permute-start | bytes 1179656 | tf_op jit(solution)/shard_map/ppermute | solution.py:266
  23.2 2.4 %collective-permute-start.3 = (bf16[2,48,640]{2,1,0:T(8,128)(2,1)}, bf16[2,48,640]{2,1,0:T(8,128)(2,1)S(1)}, u32[]{:S(2)}, u32[]{:S(2)}) collective-permute-start(bf16[2,48,640]{2,1,0:T(8,128)(2,1)} %get-tuple-element.24), channel_id=1, source_target_pairs={{0,1},{1,0},{2,3},{3,2},{4,5},{5,4},{6,7},{7,6},{8,9},{9,8},{10,11... | collective-permute-start | bytes 368648 | tf_op jit(solution)/shard_map/ppermute | solution.py:302
  23.2 8.9 %collective-permute-start.4 = (bf16[2,48,640]{2,1,0:T(8,128)(2,1)}, bf16[2,48,640]{2,1,0:T(8,128)(2,1)S(1)}, u32[]{:S(2)}, u32[]{:S(2)}) collective-permute-start(bf16[2,48,640]{2,1,0:T(8,128)(2,1)} %get-tuple-element.25), channel_id=1, source_target_pairs={{0,2},{1,3},{2,0},{3,1},{4,6},{5,7},{6,4},{7,5},{8,10},{9,11},{10,... | collective-permute-start | bytes 368648 | tf_op jit(solution)/shard_map/ppermute | solution.py:302
  23.8 8.4 %collective-permute-start.5 = (bf16[2,48,640]{2,1,0:T(8,128)(2,1)}, bf16[2,48,640]{2,1,0:T(8,128)(2,1)S(1)}, u32[]{:S(2)}, u32[]{:S(2)}) collective-permute-start(bf16[2,48,640]{2,1,0:T(8,128)(2,1)} %get-tuple-element.26), channel_id=1, source_target_pairs={{0,3},{1,2},{2,1},{3,0},{4,7},{5,6},{6,5},{7,4},{8,11},{9,10},{10,... | collective-permute-start | bytes 368648 | tf_op jit(solution)/shard_map/ppermute | solution.py:302
  25.1 8.1 %collective-permute-start.6 = (bf16[2,48,640]{2,1,0:T(8,128)(2,1)}, bf16[2,48,640]{2,1,0:T(8,128)(2,1)S(1)}, u32[]{:S(2)}, u32[]{:S(2)}) collective-permute-start(bf16[2,48,640]{2,1,0:T(8,128)(2,1)} %get-tuple-element.27), channel_id=1, source_target_pairs={{0,4},{1,5},{2,6},{3,7},{4,0},{5,1},{6,2},{7,3},{8,12},{9,13},{10,... | collective-permute-start | bytes 368648 | tf_op jit(solution)/shard_map/ppermute | solution.py:302
  25.6 16.7 %collective-permute-start.2 = (bf16[8,2,48,128]{3,2,1,0:T(8,128)(2,1)S(1)}, bf16[8,2,48,128]{3,2,1,0:T(8,128)(2,1)S(1)}, u32[]{:S(2)}, u32[]{:S(2)}) collective-permute-start(bf16[8,2,48,128]{3,2,1,0:T(8,128)(2,1)S(1)} %slice.4), channel_id=1, source_target_pairs={{0,24},{1,25},{2,26},{3,27},{4,28},{5,29},{6,30},{7,31}} | collective-permute-start | bytes 589832 | tf_op jit(solution)/shard_map/ppermute | solution.py:266
  29.0 19.3 %collective-permute-start.1 = (bf16[8,4,48,128]{3,2,1,0:T(8,128)(2,1)S(1)}, bf16[8,4,48,128]{3,2,1,0:T(8,128)(2,1)S(1)}, u32[]{:S(2)}, u32[]{:S(2)}) collective-permute-start(bf16[8,4,48,128]{3,2,1,0:T(8,128)(2,1)S(1)} %collective-permute-done.refs_6_), channel_id=1, source_target_pairs={{0,8},{8,16},{16,24},{1,9},{9,17},{17,25},{2,10},{10,18},{18,26},{... | collective-permute-start | bytes 1179656 | tf_op jit(solution)/shard_map/ppermute | solution.py:266
  32.1 10.3 %collective-permute-start.7 = (bf16[2,48,640]{2,1,0:T(8,128)(2,1)}, bf16[2,48,640]{2,1,0:T(8,128)(2,1)S(1)}, u32[]{:S(2)}, u32[]{:S(2)}) collective-permute-start(bf16[2,48,640]{2,1,0:T(8,128)(2,1)} %get-tuple-element.28), channel_id=1, source_target_pairs={{0,5},{1,4},{2,7},{3,6},{4,1},{5,0},{6,3},{7,2},{8,13},{9,12},{10,... | collective-permute-start | bytes 368648 | tf_op jit(solution)/shard_map/ppermute | solution.py:302
  32.2 10.2 %collective-permute-start.8 = (bf16[2,48,640]{2,1,0:T(8,128)(2,1)}, bf16[2,48,640]{2,1,0:T(8,128)(2,1)S(1)}, u32[]{:S(2)}, u32[]{:S(2)}) collective-permute-start(bf16[2,48,640]{2,1,0:T(8,128)(2,1)} %get-tuple-element.29), channel_id=1, source_target_pairs={{0,6},{1,7},{2,4},{3,5},{4,2},{5,3},{6,0},{7,1},{8,14},{9,15},{10,... | collective-permute-start | bytes 368648 | tf_op jit(solution)/shard_map/ppermute | solution.py:302
  33.1 9.3 %collective-permute-start.9 = (bf16[2,48,640]{2,1,0:T(8,128)(2,1)}, bf16[2,48,640]{2,1,0:T(8,128)(2,1)S(1)}, u32[]{:S(2)}, u32[]{:S(2)}) collective-permute-start(bf16[2,48,640]{2,1,0:T(8,128)(2,1)} %get-tuple-element.30), channel_id=1, source_target_pairs={{0,7},{1,6},{2,5},{3,4},{4,3},{5,2},{6,1},{7,0},{8,15},{9,14},{10,... | collective-permute-start | bytes 368648 | tf_op jit(solution)/shard_map/ppermute | solution.py:302
  42.4 0.9 %copy-start.5 = (bf16[2,48,640]{2,1,0:T(8,128)(2,1)S(1)}, bf16[2,48,640]{2,1,0:T(8,128)(2,1)}, u32[]{:S(2)}) copy-start(bf16[2,48,640]{2,1,0:T(8,128)(2,1)} %get-tuple-element.23.refs_8_) | copy-start | bytes 368644
  59.1 3.6 %collective-permute-start.10 = (bf16[2,48,640]{2,1,0:T(8,128)(2,1)S(1)}, bf16[2,48,640]{2,1,0:T(8,128)(2,1)S(1)}, u32[]{:S(2)}, u32[]{:S(2)}) collective-permute-start(bf16[2,48,640]{2,1,0:T(8,128)(2,1)S(1)} %get-tuple-element.37), channel_id=1, source_target_pairs={{0,1},{1,0},{2,3},{3,2},{4,5},{5,4},{6,7},{7,6},{8,9},{9,8},{10,11... | collective-permute-start | bytes 368648 | tf_op jit(solution)/shard_map/ppermute | solution.py:302
  59.2 6.3 %collective-permute-start.11 = (bf16[2,48,640]{2,1,0:T(8,128)(2,1)S(1)}, bf16[2,48,640]{2,1,0:T(8,128)(2,1)S(1)}, u32[]{:S(2)}, u32[]{:S(2)}) collective-permute-start(bf16[2,48,640]{2,1,0:T(8,128)(2,1)S(1)} %get-tuple-element.38), channel_id=1, source_target_pairs={{0,2},{1,3},{2,0},{3,1},{4,6},{5,7},{6,4},{7,5},{8,10},{9,11},{10,... | collective-permute-start | bytes 368648 | tf_op jit(solution)/shard_map/ppermute | solution.py:302
  60.1 6.9 %collective-permute-start.12 = (bf16[2,48,640]{2,1,0:T(8,128)(2,1)S(1)}, bf16[2,48,640]{2,1,0:T(8,128)(2,1)S(1)}, u32[]{:S(2)}, u32[]{:S(2)}) collective-permute-start(bf16[2,48,640]{2,1,0:T(8,128)(2,1)S(1)} %get-tuple-element.39), channel_id=1, source_target_pairs={{0,3},{1,2},{2,1},{3,0},{4,7},{5,6},{6,5},{7,4},{8,11},{9,10},{10,... | collective-permute-start | bytes 368648 | tf_op jit(solution)/shard_map/ppermute | solution.py:302
  61.0 6.2 %collective-permute-start.13 = (bf16[2,48,640]{2,1,0:T(8,128)(2,1)S(1)}, bf16[2,48,640]{2,1,0:T(8,128)(2,1)S(1)}, u32[]{:S(2)}, u32[]{:S(2)}) collective-permute-start(bf16[2,48,640]{2,1,0:T(8,128)(2,1)S(1)} %get-tuple-element.40), channel_id=1, source_target_pairs={{0,4},{1,5},{2,6},{3,7},{4,0},{5,1},{6,2},{7,3},{8,12},{9,13},{10,... | collective-permute-start | bytes 368648 | tf_op jit(solution)/shard_map/ppermute | solution.py:302
  62.5 11.4 %collective-permute-start.14 = (bf16[2,48,640]{2,1,0:T(8,128)(2,1)S(1)}, bf16[2,48,640]{2,1,0:T(8,128)(2,1)S(1)}, u32[]{:S(2)}, u32[]{:S(2)}) collective-permute-start(bf16[2,48,640]{2,1,0:T(8,128)(2,1)S(1)} %get-tuple-element.41), channel_id=1, source_target_pairs={{0,5},{1,4},{2,7},{3,6},{4,1},{5,0},{6,3},{7,2},{8,13},{9,12},{10,... | collective-permute-start | bytes 368648 | tf_op jit(solution)/shard_map/ppermute | solution.py:302
  62.8 11.2 %collective-permute-start.15 = (bf16[2,48,640]{2,1,0:T(8,128)(2,1)S(1)}, bf16[2,48,640]{2,1,0:T(8,128)(2,1)S(1)}, u32[]{:S(2)}, u32[]{:S(2)}) collective-permute-start(bf16[2,48,640]{2,1,0:T(8,128)(2,1)S(1)} %get-tuple-element.42), channel_id=1, source_target_pairs={{0,6},{1,7},{2,4},{3,5},{4,2},{5,3},{6,0},{7,1},{8,14},{9,15},{10,... | collective-permute-start | bytes 368648 | tf_op jit(solution)/shard_map/ppermute | solution.py:302
  65.5 8.5 %collective-permute-start.16 = (bf16[2,48,640]{2,1,0:T(8,128)(2,1)S(1)}, bf16[2,48,640]{2,1,0:T(8,128)(2,1)S(1)}, u32[]{:S(2)}, u32[]{:S(2)}) collective-permute-start(bf16[2,48,640]{2,1,0:T(8,128)(2,1)S(1)} %get-tuple-element.43), channel_id=1, source_target_pairs={{0,7},{1,6},{2,5},{3,4},{4,3},{5,2},{6,1},{7,0},{8,15},{9,14},{10,... | collective-permute-start | bytes 368648 | tf_op jit(solution)/shard_map/ppermute | solution.py:302
